TPU v7x, 32 devices: a whole 2x2x4 slice. The times are simulated.
32 devices in a mesh: dp: 8 (over z, y), tensor: 4 (over x, core).
Axes of the slice: x: 2, y: 2, z: 4, core: 2. Of those that a mesh axis runs over, the one named last changes fastest.
Arguments:
- layer_input: bfloat16 [3072, 2304], P('dp'), may hold values from -6 to 6
- cotangent: bfloat16 [3072, 2304], P('dp'), may hold values from -6 to 6
- seq_lengths: int32 [8, 8], P('dp'), may hold values from 0 to 256, as said below
- norm_attn_in: float32 [2304], replicated, may hold values from 0.1 to 1.9
- w_query: bfloat16 [2304, 2048], P('dp', 'tensor'), may hold values from -1 to 1
- w_key: bfloat16 [2304, 1024], P('dp', 'tensor'), may hold values from -1 to 1
- w_value: bfloat16 [2304, 1024], P('dp', 'tensor'), may hold values from -0.125 to 0.125
- w_out: bfloat16 [2048, 2304], P('tensor', 'dp'), may hold values from -0.125 to 0.125
- norm_attn_out: float32 [2304], replicated, may hold values from 0.1 to 1.9
- norm_ffn_in: float32 [2304], replicated, may hold values from 0.1 to 1.9
- w_gate: bfloat16 [2304, 9216], P('dp', 'tensor'), may hold values from -0.125 to 0.125
- w_up: bfloat16 [2304, 9216], P('dp', 'tensor'), may hold values from -0.125 to 0.125
- w_down: bfloat16 [9216, 2304], P('tensor', 'dp'), may hold values from -0.0625 to 0.0625
- norm_ffn_out: float32 [2304], replicated, may hold values from 0.1 to 1.9
Outputs:
- layer_output: bfloat16 [3072, 2304], P('dp')
- input_grad: float32 [3072, 2304], P('dp')
- grad_norm_attn_in: float32 [2304], P('dp')
- grad_w_query: float32 [2304, 2048], P('dp', 'tensor')
- grad_w_key: float32 [2304, 1024], P('dp', 'tensor')
- grad_w_value: float32 [2304, 1024], P('dp', 'tensor')
- grad_w_out: float32 [2048, 2304], P('tensor', 'dp')
- grad_norm_attn_out: float32 [2304], P('dp')
- grad_norm_ffn_in: float32 [2304], P('dp')
- grad_w_gate: float32 [2304, 9216], P('dp', 'tensor')
- grad_w_up: float32 [2304, 9216], P('dp', 'tensor')
- grad_w_down: float32 [9216, 2304], P('tensor', 'dp')
- grad_norm_ffn_out: float32 [2304], P('dp')
Inputs may be any that keep to these rules, and one draw needn't show every extreme that they name: `seq_lengths`: row r lists the lengths of the sequences on data index r in packing order; slots after the last sequence hold 0. Each row sums to at most 384 and some row sums to exactly 384; some sequence has exactly 256 tokens.
All inputs are finite; a program needn't handle non-finite values.
Results may differ from a plain program's by a relative error of at most 0.02.
The roundings to bfloat16 on the way count: a program that leaves them out, or rounds other values in their place, can miss the bound.
Values may be sent and summed in bfloat16 or wider, within the bound.
A program may use at most 256 MiB of HBM per device.

v0:
```python
import math

import jax
import jax.numpy as jnp
from jax import lax
from jax.sharding import PartitionSpec as P

H = 8
KV = 4
HD = 256


EPSILON = 1e-06
SOFT_CAP = 50.0
QUERY_SCALE = 0.0625
GELU_COEFF = 0.7978845608028654


def rms_scale(values, scales):
    return values * lax.rsqrt(jnp.mean(values * values, axis=-1, keepdims=True) + EPSILON) * scales


def gelu_tanh(inputs):
    return (
        0.5 * inputs * (1.0 + jnp.tanh(GELU_COEFF * (inputs + 0.044715 * inputs * inputs * inputs)))
    )


def rotate_half(heads):
    middle = heads.shape[-1] // 2
    return jnp.concatenate([-heads[..., middle:], heads[..., :middle]], axis=-1)


def layout(lengths, row_count):
    seq_ends = jnp.cumsum(lengths)
    row_index = jnp.arange(row_count, dtype=jnp.int32)
    passed = (row_index[:, None] >= seq_ends[None, :]).astype(jnp.int32)
    segment = jnp.sum(passed, axis=1)
    is_live = row_index < seq_ends[-1]
    seq_ident = jnp.where(is_live, segment, lengths.shape[0] + row_index)
    offset = row_index - jnp.sum(passed * lengths[None, :], axis=1)
    allowed = (seq_ident[:, None] == seq_ident[None, :]) & (
        row_index[None, :] <= row_index[:, None]
    )
    middle = HD // 2
    inverse = jnp.exp(jnp.arange(middle, dtype=jnp.float32) * (-2.0 * math.log(10000.0) / HD))
    angles = offset.astype(jnp.float32)[:, None] * inverse[None, :]
    cosine = jnp.concatenate([jnp.cos(angles), jnp.cos(angles)], axis=1)
    sine_wave = jnp.concatenate([jnp.sin(angles), jnp.sin(angles)], axis=1)
    return (is_live, allowed, cosine, sine_wave)


def matmul(left, right):
    return jnp.dot(left, right, preferred_element_type=jnp.float32)


def left_product(left, right):
    return jnp.einsum("td,tc->dc", left, right, preferred_element_type=jnp.float32)


def right_product(left, right):
    return jnp.einsum("tc,dc->td", left, right, preferred_element_type=jnp.float32)


def capped_scores(query, keys):
    raw_scores = jnp.einsum("kgqd,ksd->kgqs", query, keys, preferred_element_type=jnp.float32)
    return SOFT_CAP * jnp.tanh(raw_scores / SOFT_CAP)


def shards(
    layer_input,
    cotangent,
    seq_lengths,
    norm_attn_in,
    w_query,
    w_key,
    w_value,
    w_out,
    norm_attn_out,
    norm_ffn_in,
    w_gate,
    w_up,
    w_down,
    norm_ffn_out,
):
    gathered = (
        lax.all_gather(w_query, "dp", axis=0, tiled=True),
        lax.all_gather(w_key, "dp", axis=0, tiled=True),
        lax.all_gather(w_value, "dp", axis=0, tiled=True),
        lax.all_gather(w_out, "dp", axis=1, tiled=True),
        lax.all_gather(w_gate, "dp", axis=0, tiled=True),
        lax.all_gather(w_up, "dp", axis=0, tiled=True),
        lax.all_gather(w_down, "dp", axis=1, tiled=True),
    )
    query_full, key_full, value_full, out_full, gate_full, up_full, down_full = gathered
    row_count = layer_input.shape[0]
    is_live, allowed, cosine, sine_wave = layout(seq_lengths[0], row_count)
    kv_heads = key_full.shape[1] // HD
    groups = H // KV
    layer_float = layer_input.astype(jnp.float32)
    h_attn = rms_scale(layer_float, norm_attn_in).astype(jnp.bfloat16)
    query_pre = (
        matmul(h_attn, query_full).reshape(row_count, kv_heads, groups, HD).transpose(1, 2, 0, 3)
    )
    query = ((query_pre * cosine + rotate_half(query_pre) * sine_wave) * QUERY_SCALE).astype(
        jnp.bfloat16
    )
    key_pre = matmul(h_attn, key_full).reshape(row_count, kv_heads, HD).transpose(1, 0, 2)
    keys = (key_pre * cosine + rotate_half(key_pre) * sine_wave).astype(jnp.bfloat16)
    values = (
        matmul(h_attn, value_full)
        .astype(jnp.bfloat16)
        .reshape(row_count, kv_heads, HD)
        .transpose(1, 0, 2)
    )
    capped = capped_scores(query, keys)
    expo = jnp.where(allowed, jnp.exp(capped), 0.0)
    log_total = jnp.log(jnp.sum(expo, axis=-1, keepdims=True))
    probs = jnp.where(allowed, jnp.exp(capped - log_total), 0.0).astype(jnp.bfloat16)
    mixed = jnp.einsum("kgqs,ksd->kgqd", probs, values, preferred_element_type=jnp.float32).astype(
        jnp.bfloat16
    )
    mixed_flat = mixed.transpose(2, 0, 1, 3).reshape(row_count, -1)
    attn_branch = lax.psum(matmul(mixed_flat, out_full), "tensor")
    resid = layer_float + rms_scale(attn_branch, norm_attn_out)
    h_ffn = rms_scale(resid, norm_ffn_in).astype(jnp.bfloat16)
    gate_pre = matmul(h_ffn, gate_full)
    up_pre = matmul(h_ffn, up_full)
    gelu_gate = gelu_tanh(gate_pre)
    hidden = (gelu_gate * up_pre).astype(jnp.bfloat16)
    ffn_branch = lax.psum(matmul(hidden, down_full), "tensor")
    layer_output = (resid + rms_scale(ffn_branch, norm_ffn_out)).astype(jnp.bfloat16)
    query_back, key_back, value_back, out_back, gate_back, up_back, down_back = gathered
    grad_out = cotangent.astype(jnp.float32) * is_live[:, None].astype(jnp.float32)
    _, pull_four = jax.vjp(rms_scale, ffn_branch, norm_ffn_out)
    grad_ffn_float, grad_norm_ffn_out = pull_four(grad_out)
    grad_ffn_branch = grad_ffn_float.astype(jnp.bfloat16)
    grad_w_down = left_product(hidden, grad_ffn_branch)
    grad_hidden = right_product(grad_ffn_branch, down_back)
    grad_up = (grad_hidden * gelu_gate).astype(jnp.bfloat16)
    _, pull_gelu = jax.vjp(gelu_tanh, gate_pre)
    grad_gate = pull_gelu(grad_hidden * up_pre)[0].astype(jnp.bfloat16)
    grad_w_gate = left_product(h_ffn, grad_gate)
    grad_w_up = left_product(h_ffn, grad_up)
    grad_h_ffn = lax.psum(
        right_product(grad_gate, gate_back) + right_product(grad_up, up_back), "tensor"
    )
    _, pull_three = jax.vjp(rms_scale, resid, norm_ffn_in)
    grad_resid_part, grad_norm_ffn_in = pull_three(grad_h_ffn)
    grad_resid = grad_out + grad_resid_part
    _, pull_two = jax.vjp(rms_scale, attn_branch, norm_attn_out)
    grad_attn_float, grad_norm_attn_out = pull_two(grad_resid)
    grad_attn_branch = grad_attn_float.astype(jnp.bfloat16)
    grad_w_out = left_product(mixed_flat, grad_attn_branch)
    grad_mixed = right_product(grad_attn_branch, out_back).astype(jnp.bfloat16)
    grad_mixed = grad_mixed.reshape(row_count, kv_heads, groups, HD).transpose(1, 2, 0, 3)
    capped_back = capped_scores(query, keys)
    weights_back = jnp.where(allowed, jnp.exp(capped_back - log_total), 0.0)
    grad_values = jnp.einsum(
        "kgqs,kgqd->ksd",
        weights_back.astype(jnp.bfloat16),
        grad_mixed,
        preferred_element_type=jnp.float32,
    ).astype(jnp.bfloat16)
    grad_probs = jnp.einsum(
        "kgqd,ksd->kgqs", grad_mixed, values, preferred_element_type=jnp.float32
    )
    row_delta = jnp.sum(weights_back * grad_probs, axis=-1, keepdims=True)
    tanh_part = capped_back / SOFT_CAP
    grad_scores = (weights_back * (grad_probs - row_delta) * (1.0 - tanh_part * tanh_part)).astype(
        jnp.bfloat16
    )
    grad_query_raw = jnp.einsum(
        "kgqs,ksd->kgqd", grad_scores, keys, preferred_element_type=jnp.float32
    )
    grad_query = (
        (grad_query_raw * cosine - rotate_half(grad_query_raw) * sine_wave) * QUERY_SCALE
    ).astype(jnp.bfloat16)
    grad_keys_raw = jnp.einsum(
        "kgqs,kgqd->ksd", grad_scores, query, preferred_element_type=jnp.float32
    )
    grad_keys = (grad_keys_raw * cosine - rotate_half(grad_keys_raw) * sine_wave).astype(
        jnp.bfloat16
    )
    grad_query_flat = grad_query.transpose(2, 0, 1, 3).reshape(row_count, -1)
    grad_keys_flat = grad_keys.transpose(1, 0, 2).reshape(row_count, -1)
    grad_values_flat = grad_values.transpose(1, 0, 2).reshape(row_count, -1)
    grad_w_query = left_product(h_attn, grad_query_flat)
    grad_w_key = left_product(h_attn, grad_keys_flat)
    grad_w_value = left_product(h_attn, grad_values_flat)
    local_h_attn = (
        right_product(grad_query_flat, query_back)
        + right_product(grad_keys_flat, key_back)
        + right_product(grad_values_flat, value_back)
    )
    grad_h_attn = lax.psum(local_h_attn.astype(jnp.bfloat16), "tensor").astype(jnp.float32)
    _, pull_one = jax.vjp(rms_scale, layer_float, norm_attn_in)
    grad_input_part, grad_norm_attn_in = pull_one(grad_h_attn)
    input_grad = grad_resid + grad_input_part
    summed = (
        lax.psum_scatter(
            grad_norm_attn_in.astype(jnp.bfloat16), "dp", scatter_dimension=0, tiled=True
        ).astype(jnp.float32),
        lax.psum_scatter(
            grad_w_query.astype(jnp.bfloat16), "dp", scatter_dimension=0, tiled=True
        ).astype(jnp.float32),
        lax.psum_scatter(
            grad_w_key.astype(jnp.bfloat16), "dp", scatter_dimension=0, tiled=True
        ).astype(jnp.float32),
        lax.psum_scatter(
            grad_w_value.astype(jnp.bfloat16), "dp", scatter_dimension=0, tiled=True
        ).astype(jnp.float32),
        lax.psum_scatter(
            grad_w_out.astype(jnp.bfloat16), "dp", scatter_dimension=1, tiled=True
        ).astype(jnp.float32),
        lax.psum_scatter(
            grad_norm_attn_out.astype(jnp.bfloat16), "dp", scatter_dimension=0, tiled=True
        ).astype(jnp.float32),
        lax.psum_scatter(
            grad_norm_ffn_in.astype(jnp.bfloat16), "dp", scatter_dimension=0, tiled=True
        ).astype(jnp.float32),
        lax.psum_scatter(
            grad_w_gate.astype(jnp.bfloat16), "dp", scatter_dimension=0, tiled=True
        ).astype(jnp.float32),
        lax.psum_scatter(
            grad_w_up.astype(jnp.bfloat16), "dp", scatter_dimension=0, tiled=True
        ).astype(jnp.float32),
        lax.psum_scatter(
            grad_w_down.astype(jnp.bfloat16), "dp", scatter_dimension=1, tiled=True
        ).astype(jnp.float32),
        lax.psum_scatter(
            grad_norm_ffn_out.astype(jnp.bfloat16), "dp", scatter_dimension=0, tiled=True
        ).astype(jnp.float32),
    )
    (
        sum_attn_in,
        sum_query,
        sum_key,
        sum_value,
        sum_out,
        sum_attn_out,
        sum_ffn_in,
        sum_gate,
        sum_up,
        sum_down,
        sum_ffn_out,
    ) = summed
    return (
        layer_output,
        input_grad,
        sum_attn_in,
        sum_query,
        sum_key,
        sum_value,
        sum_out,
        sum_attn_out,
        sum_ffn_in,
        sum_gate,
        sum_up,
        sum_down,
        sum_ffn_out,
    )


def solution(mesh):
    placed = (
        P("dp", None),
        P("dp", None),
        P("dp", None),
        P(),
        P("dp", "tensor"),
        P("dp", "tensor"),
        P("dp", "tensor"),
        P("tensor", "dp"),
        P(),
        P(),
        P("dp", "tensor"),
        P("dp", "tensor"),
        P("tensor", "dp"),
        P(),
    )
    return jax.shard_map(
        shards,
        mesh=mesh,
        in_specs=placed,
        out_specs=(
            P("dp", None),
            P("dp", None),
            P("dp"),
            P("dp", "tensor"),
            P("dp", "tensor"),
            P("dp", "tensor"),
            P("tensor", "dp"),
            P("dp"),
            P("dp"),
            P("dp", "tensor"),
            P("dp", "tensor"),
            P("tensor", "dp"),
            P("dp"),
        ),
        check_vma=False,
    )
```

profile of v0, /device:TPU:0, one launch (start us, length us, event | category | flops | bytes accessed | tf_op | source)
XLA Modules:
  0.0 1854.8 jit_solution(15311761673181839978)
XLA Ops:
  15.7 38.3 %all-gather.10.cloned.1.call-done = bf16[2304,256]{1,0:T(8,128)(2,1)} async-done(((bf16[288,256]{1,0:T(8,128)(2,1)}), bf16[2304,256]{1,0:T(8,128)(2,1)}) %all-gather.10.cloned.1.call-update) | async-done | bytes 1179664 | tf_op jit(solution)/shard_map/all_gather | solution.py:88
  54.0 2.7 fusion.94
  57.0 39.1 %all-gather.12.cloned.1.call-done = bf16[2304,256]{1,0:T(8,128)(2,1)} async-done(((bf16[288,256]{1,0:T(8,128)(2,1)}), bf16[2304,256]{1,0:T(8,128)(2,1)}) %all-gather.12.cloned.1.call-update) | async-done | bytes 1179664 | tf_op jit(solution)/shard_map/all_gather | solution.py:89
  98.0 50.8 %all-gather.8.cloned.1.call-done = bf16[2304,512]{1,0:T(8,128)(2,1)} async-done(((bf16[288,512]{1,0:T(8,128)(2,1)}), bf16[2304,512]{1,0:T(8,128)(2,1)}) %all-gather.8.cloned.1.call-update) | async-done | bytes 2359312 | tf_op jit(solution)/shard_map/all_gather | solution.py:87
  148.8 3.2 fusion.96
  154.2 47.0 %all-gather.14.cloned.1.call-done = bf16[512,2304]{0,1:T(8,128)(2,1)} async-done(((bf16[512,288]{0,1:T(8,128)(2,1)}), bf16[512,2304]{0,1:T(8,128)(2,1)}) %all-gather.14.cloned.1.call-update) | async-done | bytes 2359312 | tf_op jit(solution)/shard_map/all_gather | solution.py:90
  201.2 4.6 fusion.99
  208.5 70.8 %all-reduce.10.cloned.1.call-done = f32[384,2304]{1,0:T(8,128)} async-done(((f32[384,2304]{1,0:T(8,128)}), f32[384,2304]{1,0:T(8,128)}) %all-reduce.10.cloned.1.call-update) | async-done | bytes 3538960 | tf_op jit(solution)/shard_map/psum | solution.py:124
  279.3 2.5 multiply_reduce_fusion.8
  282.4 2.3 multiply_reduce_fusion.7
  287.5 146.2 %all-gather.16.cloned.1.call-done = bf16[2304,2304]{1,0:T(8,128)(2,1)} async-done(((bf16[288,2304]{1,0:T(8,128)(2,1)}), bf16[2304,2304]{1,0:T(8,128)(2,1)}) %all-gather.16.cloned.1.call-update) | async-done | bytes 10616848 | tf_op jit(solution)/shard_map/all_gather | solution.py:91
  433.6 10.6 fusion.100
  444.3 141.9 %all-gather.18.cloned.1.call-done = bf16[2304,2304]{1,0:T(8,128)(2,1)} async-done(((bf16[288,2304]{1,0:T(8,128)(2,1)}), bf16[2304,2304]{1,0:T(8,128)(2,1)}) %all-gather.18.cloned.1.call-update) | async-done | bytes 10616848 | tf_op jit(solution)/shard_map/all_gather | solution.py:92
  586.2 12.3 multiply_convert_fusion.1
  598.5 140.2 %all-gather.20.cloned.1.call-done = bf16[2304,2304]{0,1:T(8,128)(2,1)} async-done(((bf16[2304,288]{0,1:T(8,128)(2,1)}), bf16[2304,2304]{0,1:T(8,128)(2,1)}) %all-gather.20.cloned.1.call-update) | async-done | bytes 10616848 | tf_op jit(solution)/shard_map/all_gather | solution.py:93
  738.7 10.6 fusion.101
  750.8 71.7 %all-reduce.12.cloned.1.call-done = f32[384,2304]{1,0:T(8,128)} async-done(((f32[384,2304]{1,0:T(8,128)}), f32[384,2304]{1,0:T(8,128)}) %all-reduce.12.cloned.1.call-update) | async-done | bytes 3538960 | tf_op jit(solution)/shard_map/psum | solution.py:131
  822.5 2.5 multiply_reduce_fusion.6
  825.6 5.0 multiply_reduce_fusion
  830.6 13.1 multiply_convert_fusion
  843.8 7.7 fusion.102
  851.5 12.9 convolution_add_fusion.2
  864.7 3.5 fusion.24
  868.2 71.4 %all-reduce.14.cloned.1.call-done = f32[384,2304]{1,0:T(8,128)} async-done(((f32[384,2304]{1,0:T(8,128)}), f32[384,2304]{1,0:T(8,128)}) %all-reduce.14.cloned.1.call-update) | async-done | bytes 3538960 | tf_op jit(solution)/shard_map/psum | solution.py:145
  939.6 3.7 multiply_reduce_fusion.1
  943.8 4.1 multiply_reduce_fusion.2
  954.0 3.3 fusion.37
  957.3 3.3 fusion.34
  960.6 2.6 fusion.30
  969.4 2.0 convolution_convert_fusion.6
  974.0 3.0 convolution_convert_fusion.4
  977.1 4.4 convolution_convert_fusion.3
  981.6 9.9 convolution_convert_fusion.2
  992.9 8.3 convolution_convert_fusion.1
  1003.2 10.6 convolution_convert_fusion
  1016.0 3.9 fusion.6
  1019.9 38.9 %all-reduce.4 = (bf16[2304]{0:T(1024)(128)(2,1)}, bf16[2304]{0:T(1024)(128)(2,1)}, bf16[2304]{0:T(1024)(128)(2,1)}, bf16[2304]{0:T(1024)(128)(2,1)}) all-reduce(bf16[2304]{0:T(1024)(128)(2,1)} %get-tuple-element.19, bf16[2304]{0:T(1024)(128)(2,1)} %get-tuple-element.15, ...), channel_id=2, replica_groups=mesh['dp'=8,'tensor'=4] {'dp'}, use_global_device_ids=true, to_apply=%region_18.19.clone | all-reduce | flops 9216 | bytes 36864
  1062.2 4.8 fusion.16
  1067.0 16.9 reduce-scatter.10.cloned.1.call-done
  1085.6 65.6 %reduce-scatter.12.cloned.1.call-done = bf16[288,256]{1,0:T(8,128)(2,1)} async-done(((bf16[2304,256]{1,0:T(8,128)(2,1)}), bf16[288,256]{1,0:T(8,128)(2,1)}) %reduce-scatter.12.cloned.1.call-update) | async-done | bytes 147472 | tf_op jit(solution)/shard_map/reduce_scatter | solution.py:210
  1152.8 71.0 %reduce-scatter.8.cloned.1.call-done = bf16[288,512]{1,0:T(8,128)(2,1)} async-done(((bf16[2304,512]{1,0:T(8,128)(2,1)}), bf16[288,512]{1,0:T(8,128)(2,1)}) %reduce-scatter.8.cloned.1.call-update) | async-done | bytes 294928 | tf_op jit(solution)/shard_map/reduce_scatter | solution.py:204
  1225.7 70.9 %reduce-scatter.14.cloned.1.call-done = bf16[512,288]{0,1:T(8,128)(2,1)} async-done(((bf16[512,2304]{0,1:T(8,128)(2,1)}), bf16[512,288]{0,1:T(8,128)(2,1)}) %reduce-scatter.14.cloned.1.call-update) | async-done | bytes 294928 | tf_op jit(solution)/shard_map/reduce_scatter | solution.py:213
  1298.4 180.9 %reduce-scatter.16.cloned.1.call-done = bf16[288,2304]{1,0:T(8,128)(2,1)} async-done(((bf16[2304,2304]{1,0:T(8,128)(2,1)}), bf16[288,2304]{1,0:T(8,128)(2,1)}) %reduce-scatter.16.cloned.1.call-update) | async-done | bytes 1327120 | tf_op jit(solution)/shard_map/reduce_scatter | solution.py:222
  1479.4 3.0 convert_element_type.204
  1482.4 179.7 %reduce-scatter.18.cloned.1.call-done = bf16[288,2304]{1,0:T(8,128)(2,1)} async-done(((bf16[2304,2304]{1,0:T(8,128)(2,1)}), bf16[288,2304]{1,0:T(8,128)(2,1)}) %reduce-scatter.18.cloned.1.call-update) | async-done | bytes 1327120 | tf_op jit(solution)/shard_map/reduce_scatter | solution.py:225
  1662.1 3.0 convert_element_type.206
  1665.0 179.7 %reduce-scatter.20.cloned.1.call-done = bf16[2304,288]{0,1:T(8,128)(2,1)} async-done(((bf16[2304,2304]{0,1:T(8,128)(2,1)}), bf16[2304,288]{0,1:T(8,128)(2,1)}) %reduce-scatter.20.cloned.1.call-update) | async-done | bytes 1327120 | tf_op jit(solution)/shard_map/reduce_scatter | solution.py:228
  1844.7 3.0 convert_element_type.208
  (205 shorter events, 51.6 us)
Async XLA Ops:
  7.2 46.9 %all-gather.10.cloned.1.call-start = ((), (), s32[]{:S(2)}) async-start(), calls=%async_computation.8 | async-start | bytes 1327104 | tf_op jit(solution)/shard_map/all_gather | solution.py:88
  7.9 88.2 %all-gather.12.cloned.1.call-start = ((), (), s32[]{:S(2)}) async-start(), calls=%async_computation.9 | async-start | bytes 1327104 | tf_op jit(solution)/shard_map/all_gather | solution.py:89
  8.7 140.1 %all-gather.8.cloned.1.call-start = ((), (), s32[]{:S(2)}) async-start(), calls=%async_computation.7 | async-start | bytes 2654208 | tf_op jit(solution)/shard_map/all_gather | solution.py:87
  9.4 191.8 %all-gather.14.cloned.1.call-start = ((), (), s32[]{:S(2)}) async-start(), calls=%async_computation.10 | async-start | bytes 2654208 | tf_op jit(solution)/shard_map/all_gather | solution.py:90
  10.0 269.4 %all-reduce.10.cloned.1.call-start = ((), (), s32[]{:S(2)}) async-start(), calls=%async_computation.11 | async-start | bytes 7077888 | tf_op jit(solution)/shard_map/psum | solution.py:124
  14.1 134.7 %copy-start.50 = (f32[384]{0:T(512)}, f32[384]{0:T(512)S(1)}, u32[]{:S(2)}) copy-start(f32[384]{0:T(512)S(1)} %fusion.69) | copy-start | bytes 4612
  14.9 138.5 %copy-start.33 = (pred[384,384]{0,1:T(8,128)(4,1)}, pred[384,384]{0,1:T(8,128)(4,1)S(1)}, u32[]{:S(2)}) copy-start(pred[384,384]{0,1:T(8,128)(4,1)S(1)} %fusion.50) | copy-start | bytes 442372
  15.7 41.2 %copy-start.17 = (f32[384,128]{0,1:T(8,128)}, f32[384,128]{0,1:T(8,128)S(1)}, u32[]{:S(2)}) copy-start(f32[384,128]{0,1:T(8,128)S(1)} %get-tuple-element.44) | copy-start | bytes 589828
  15.7 41.2 %copy-start.19 = (f32[384,128]{0,1:T(8,128)}, f32[384,128]{0,1:T(8,128)S(1)}, u32[]{:S(2)}) copy-start(f32[384,128]{0,1:T(8,128)S(1)} %get-tuple-element.45) | copy-start | bytes 589828
  15.7 80.3 %copy-start.4 = (bf16[384,2304]{1,0:T(8,128)(2,1)S(1)}, bf16[384,2304]{1,0:T(8,128)(2,1)}, u32[]{:S(2)}) copy-start(bf16[384,2304]{1,0:T(8,128)(2,1)} %param.14) | copy-start | bytes 5308420
  15.7 80.3 %copy-start.37 = (f32[2304]{0:T(1024)S(1)}, f32[2304]{0:T(1024)}, u32[]{:S(2)}) copy-start(f32[2304]{0:T(1024)} %param.17) | copy-start | bytes 27652
  56.9 95.1 %copy-start.10 = (f32[384,256]{0,1:T(8,128)}, f32[384,256]{0,1:T(8,128)S(1)}, u32[]{:S(2)}) copy-start(f32[384,256]{0,1:T(8,128)S(1)} %get-tuple-element.42) | copy-start | bytes 1179652
  57.0 95.1 %copy-start.12 = (f32[384,256]{0,1:T(8,128)}, f32[384,256]{0,1:T(8,128)S(1)}, u32[]{:S(2)}) copy-start(f32[384,256]{0,1:T(8,128)S(1)} %get-tuple-element.43) | copy-start | bytes 1179652
  57.0 95.3 %copy-start.27 = (bf16[384,256,1]{0,1,2:T(8,128)(2,1)}, bf16[384,256,1]{0,1,2:T(8,128)(2,1)S(1)}, u32[]{:S(2)}) copy-start(bf16[384,256,1]{0,1,2:T(8,128)(2,1)S(1)} %get-tuple-element.41) | copy-start | bytes 589828
  98.0 55.4 %copy-start.31 = (bf16[384,256,1]{1,0,2:T(8,128)(2,1)}, bf16[384,256,1]{1,0,2:T(8,128)(2,1)S(1)}, u32[]{:S(2)}) copy-start(bf16[384,256,1]{1,0,2:T(8,128)(2,1)S(1)} %fusion.31) | copy-start | bytes 589828
  153.4 52.4 %copy-start.25 = (f32[2,384,384]{1,2,0:T(8,128)}, f32[2,384,384]{1,2,0:T(8,128)S(1)}, u32[]{:S(2)}) copy-start(f32[2,384,384]{1,2,0:T(8,128)S(1)} %fusion.20) | copy-start | bytes 3538948
  154.2 51.6 %copy-start.29 = (bf16[2,384,256]{1,2,0:T(8,128)(2,1)}, bf16[2,384,256]{1,2,0:T(8,128)(2,1)S(1)}, u32[]{:S(2)}) copy-start(bf16[2,384,256]{1,2,0:T(8,128)(2,1)S(1)} %convolution_convert_fusion.8) | copy-start | bytes 1179652
  205.8 76.6 %copy-start.34 = (f32[2304]{0:T(1024)S(1)}, f32[2304]{0:T(1024)}, u32[]{:S(2)}) copy-start(f32[2304]{0:T(1024)} %param.22) | copy-start | bytes 27652
  205.8 227.8 %all-gather.16.cloned.1.call-start = ((), (), s32[]{:S(2)}) async-start(), calls=%async_computation.12 | async-start | bytes 11943936 | tf_op jit(solution)/shard_map/all_gather | solution.py:91
  206.4 379.7 %all-gather.18.cloned.1.call-start = ((), (), s32[]{:S(2)}) async-start(), calls=%async_computation.13 | async-start | bytes 11943936 | tf_op jit(solution)/shard_map/all_gather | solution.py:92
  207.2 531.5 %all-gather.20.cloned.1.call-start = ((), (), s32[]{:S(2)}) async-start(), calls=%async_computation.14 | async-start | bytes 11943936 | tf_op jit(solution)/shard_map/all_gather | solution.py:93
  207.9 614.6 %all-reduce.12.cloned.1.call-start = ((), (), s32[]{:S(2)}) async-start(), calls=%async_computation.15 | async-start | bytes 7077888 | tf_op jit(solution)/shard_map/psum | solution.py:131
  749.3 190.3 %all-reduce.14.cloned.1.call-start = ((), (), s32[]{:S(2)}) async-start(), calls=%async_computation.16 | async-start | bytes 7077888 | tf_op jit(solution)/shard_map/psum | solution.py:145
  825.5 5.0 copy-start.53
  825.5 5.0 copy-start.9
  825.5 5.0 copy-start.52
  825.6 5.0 copy-start.55
  825.6 18.2 slice-start
  830.6 13.2 copy-start.54
  830.6 13.1 slice-start.1
  830.6 13.1 slice-start.2
  843.8 7.7 copy-start.56
  864.4 151.5 %all-reduce.16.cloned.1.call-start = ((), (), s32[]{:S(2)}) async-start(), calls=%async_computation.17 | async-start | bytes 3538944 | tf_op jit(solution)/shard_map/psum | solution.py:196
  939.6 4.2 copy-start.36
  939.6 4.2 copy-start.40
  952.4 4.8 copy-start.23
  957.3 6.0 copy-start.11
  957.3 6.0 copy-start.13
  969.3 114.6 %reduce-scatter.10.cloned.1.call-start = ((), (), s32[]{:S(2)}) async-start(), calls=%async_computation.19 | async-start | bytes 1327104 | tf_op jit(solution)/shard_map/reduce_scatter | solution.py:207
  971.4 179.7 %reduce-scatter.12.cloned.1.call-start = ((), (), s32[]{:S(2)}) async-start(), calls=%async_computation.20 | async-start | bytes 1327104 | tf_op jit(solution)/shard_map/reduce_scatter | solution.py:210
  973.5 250.3 %reduce-scatter.8.cloned.1.call-start = ((), (), s32[]{:S(2)}) async-start(), calls=%async_computation.18 | async-start | bytes 2654208 | tf_op jit(solution)/shard_map/reduce_scatter | solution.py:204
  977.0 4.6 copy-start.16
  977.0 319.6 %reduce-scatter.14.cloned.1.call-start = ((), (), s32[]{:S(2)}) async-start(), calls=%async_computation.21 | async-start | bytes 2654208 | tf_op jit(solution)/shard_map/reduce_scatter | solution.py:213
  981.5 497.9 %reduce-scatter.16.cloned.1.call-start = ((), (), s32[]{:S(2)}) async-start(), calls=%async_computation.22 | async-start | bytes 11943936 | tf_op jit(solution)/shard_map/reduce_scatter | solution.py:222
  991.5 670.6 %reduce-scatter.18.cloned.1.call-start = ((), (), s32[]{:S(2)}) async-start(), calls=%async_computation.23 | async-start | bytes 11943936 | tf_op jit(solution)/shard_map/reduce_scatter | solution.py:225
  1001.2 843.5 %reduce-scatter.20.cloned.1.call-start = ((), (), s32[]{:S(2)}) async-start(), calls=%async_computation.24 | async-start | bytes 11943936 | tf_op jit(solution)/shard_map/reduce_scatter | solution.py:228
  1013.9 47.6 %copy-start.49 = (f32[384]{0:T(512)S(1)}, f32[384]{0:T(512)}, u32[]{:S(2)}) copy-start(f32[384]{0:T(512)} %copy-done.48) | copy-start | bytes 4612
  1013.9 48.3 %copy-start.3 = (f32[384,2304]{1,0:T(8,128)S(1)}, f32[384,2304]{1,0:T(8,128)}, u32[]{:S(2)}) copy-start(f32[384,2304]{1,0:T(8,128)} %copy-done.2) | copy-start | bytes 10616836
  (31 other events, 71.3 us)
Sparse Core Ops, SparseCore 0:
  10.2 43.8 all-gather.9
  56.2 39.7 all-gather.11
  98.3 50.4 all-gather.7
  150.8 50.3 all-gather.13
  206.0 73.3 all-reduce.9
  281.4 152.2 all-gather.15
  435.8 150.2 all-gather.17
  588.3 150.2 all-gather.19
  749.4 72.9 all-reduce.11
  864.6 74.9 all-reduce.13
  969.5 46.1 all-reduce.15
  1018.9 64.9 reduce-scatter.9
  1087.3 63.8 reduce-scatter.11
  1155.1 68.6 reduce-scatter.7
  1227.7 68.8 reduce-scatter.13
  1300.0 179.2 reduce-scatter.15
  1482.8 179.1 reduce-scatter.17
  1665.5 179.1 reduce-scatter.19
where the time goes:
time: 1860 us; the launch traced here: 1850 us
  waiting for transfers between devices  1590 us (85%)
  matrix products  136 us (7%)
  other arithmetic  61 us (3%)
  blocking collectives  38.9 us (2%)
    reduce_scatter x1, waiting for transfers between devices, shards(): lax.psum_scatter(grad_w_gate.astype(jnp.bfloat16), 'dp', scatter_dimensio...  181 us
    reduce_scatter x1, waiting for transfers between devices, shards(): lax.psum_scatter(grad_w_down.astype(jnp.bfloat16), 'dp', scatter_dimensio...  180 us
    reduce_scatter x1, waiting for transfers between devices, shards(): lax.psum_scatter(grad_w_up.astype(jnp.bfloat16), 'dp', scatter_dimension=...  180 us
    all_gather x1, waiting for transfers between devices, shards(): lax.all_gather(w_gate, 'dp', axis=0, tiled=True)  146 us
    all_gather x1, waiting for transfers between devices, shards(): lax.all_gather(w_up, 'dp', axis=0, tiled=True)  142 us
    all_gather x1, waiting for transfers between devices, shards(): lax.all_gather(w_down, 'dp', axis=1, tiled=True)  140 us
    psum x1, waiting for transfers between devices, shards(): ffn_branch = lax.psum(matmul(hidden, down_full), 'tensor')  71.7 us
    psum x1, waiting for transfers between devices, shards(): lax.psum(right_product(grad_gate, gate_back) + right_product(grad_up, up_...  71.4 us
  transfers between devices with their start and end apart: 18, of which 17 were waited for; matrix products, arithmetic and copies ran while one was open for 6% of the time, Pallas kernels for 0%

commit v1 on v0

v1 whole, which is shorter than its diff:
```python
import functools
import math

import jax
import jax.numpy as jnp
from jax import lax
from jax.experimental import pallas as pl
from jax.experimental.pallas import tpu as pltpu
from jax.sharding import Mesh, PartitionSpec as P

H = 8
KV = 4
HD = 256


EPSILON = 1e-06
SOFT_CAP = 50.0
QUERY_SCALE = 0.0625
GELU_COEFF = 0.7978845608028654

MESH = pl.DeviceIdType.MESH


def rms_scale(values, scales):
    return values * lax.rsqrt(jnp.mean(values * values, axis=-1, keepdims=True) + EPSILON) * scales


def gelu_tanh(inputs):
    return (
        0.5 * inputs * (1.0 + jnp.tanh(GELU_COEFF * (inputs + 0.044715 * inputs * inputs * inputs)))
    )


def rotate_half(heads):
    middle = heads.shape[-1] // 2
    return jnp.concatenate([-heads[..., middle:], heads[..., :middle]], axis=-1)


def layout(lengths, row_count):
    seq_ends = jnp.cumsum(lengths)
    row_index = jnp.arange(row_count, dtype=jnp.int32)
    passed = (row_index[:, None] >= seq_ends[None, :]).astype(jnp.int32)
    segment = jnp.sum(passed, axis=1)
    is_live = row_index < seq_ends[-1]
    seq_ident = jnp.where(is_live, segment, lengths.shape[0] + row_index)
    offset = row_index - jnp.sum(passed * lengths[None, :], axis=1)
    allowed = (seq_ident[:, None] == seq_ident[None, :]) & (
        row_index[None, :] <= row_index[:, None]
    )
    middle = HD // 2
    inverse = jnp.exp(jnp.arange(middle, dtype=jnp.float32) * (-2.0 * math.log(10000.0) / HD))
    angles = offset.astype(jnp.float32)[:, None] * inverse[None, :]
    cosine = jnp.concatenate([jnp.cos(angles), jnp.cos(angles)], axis=1)
    sine_wave = jnp.concatenate([jnp.sin(angles), jnp.sin(angles)], axis=1)
    return (is_live, allowed, cosine, sine_wave)


def matmul(left, right):
    return jnp.dot(left, right, preferred_element_type=jnp.float32)


def left_product(left, right):
    return jnp.einsum("td,tc->dc", left, right, preferred_element_type=jnp.float32)


def right_product(left, right):
    return jnp.einsum("tc,dc->td", left, right, preferred_element_type=jnp.float32)


def capped_scores(query, keys):
    raw_scores = jnp.einsum("kgqd,ksd->kgqs", query, keys, preferred_element_type=jnp.float32)
    return SOFT_CAP * jnp.tanh(raw_scores / SOFT_CAP)


def pick(blocks, index):
    return lax.dynamic_index_in_dim(blocks, index, 0, keepdims=False)


def swap_blocks(blocks, axis):
    size = blocks.shape[0]
    here = lax.axis_index(axis)
    result = lax.dynamic_update_index_in_dim(
        jnp.zeros_like(blocks), pick(blocks, here), here, 0
    )
    for step in range(1, size):
        came = lax.ppermute(
            pick(blocks, lax.rem(here + step, size)),
            axis,
            [(i, (i + step) % size) for i in range(size)],
        )
        result = lax.dynamic_update_index_in_dim(
            result, came, lax.rem(here - step + size, size), 0
        )
    return result


def collect(block, axis, size):
    here = lax.axis_index(axis)
    result = jnp.zeros((size,) + block.shape, block.dtype)
    result = lax.dynamic_update_index_in_dim(result, block, here, 0)
    for step in range(1, size):
        came = lax.ppermute(block, axis, [(i, (i + step) % size) for i in range(size)])
        result = lax.dynamic_update_index_in_dim(
            result, came, lax.rem(here - step + size, size), 0
        )
    return result


def sum_blocks(blocks, axis):
    size = blocks.shape[0]
    here = lax.axis_index(axis)
    total = pick(blocks, here).astype(jnp.float32)
    for step in range(1, size):
        came = lax.ppermute(
            pick(blocks, lax.rem(here + step, size)),
            axis,
            [(i, (i + step) % size) for i in range(size)],
        )
        total = total + came.astype(jnp.float32)
    return total


def device_layout(lanes):
    _, inner, tensor = lanes
    cores = 2 if tensor % 2 == 0 else 1
    return {"inner": inner, "x": tensor // cores, "core": cores}


class Spot:
    def __init__(self, lanes, chain, levels):
        self.sizes = device_layout(lanes)
        self.chain, self.levels = chain, levels
        self.length = lanes[0] if chain else 1
        self.at_chain = lax.axis_index("outer")
        tensor = lax.axis_index("tensor")
        cores = self.sizes["core"]
        self.here = {
            "inner": lax.axis_index("inner"),
            "x": lax.div(tensor, cores),
            "core": lax.rem(tensor, cores),
        }
        self.step = self.at_chain if chain else 0
        self.slots = {}
        for level in levels:
            for shift in range(1, self.sizes[level]):
                self.slots[level, shift] = 2 + len(self.slots)

    def moved(self, **shifts):
        at = dict(self.here)
        for level, shift in shifts.items():
            at[level] = lax.rem(at[level] + shift, self.sizes[level])
        return at

    def device(self, at, chain_shift=0):
        return (
            self.at_chain + chain_shift,
            at["inner"],
            at["x"] * self.sizes["core"] + at["core"],
        )

    def flat(self, step, at):
        index = step
        for level in self.levels:
            index = index * self.sizes[level] + at[level]
        return index

    def greet(self):
        barrier = pltpu.get_barrier_semaphore()
        count = 0
        for level in self.levels:
            for shift in range(1, self.sizes[level]):
                pl.semaphore_signal(
                    barrier, device_id=self.device(self.moved(**{level: shift})), device_id_type=MESH
                )
                count += 1
        if self.length > 1:
            for shift, there in ((-1, self.step > 0), (1, self.step < self.length - 1)):
                count = count + there.astype(jnp.int32)

                @pl.when(there)
                def _(shift=shift):
                    pl.semaphore_signal(
                        barrier, device_id=self.device(self.here, shift), device_id_type=MESH
                    )

        pl.semaphore_wait(barrier, count)


def guarded(condition, action):
    if condition is None:
        action()
    else:
        pl.when(condition)(action)


def both(first, second):
    if first is None:
        return second
    return first if second is None else jnp.logical_and(first, second)


def gather_kernel(lanes, chain, levels, x_ref, o_ref, send_sem, recv_sem, local_sem):
    spot = Spot(lanes, chain, levels)
    length, step, here = spot.length, spot.step, spot.here
    started = []

    def send(condition, source, index, slot, device):
        def copy():
            return pltpu.make_async_remote_copy(
                src_ref=source,
                dst_ref=o_ref.at[index],
                send_sem=send_sem.at[slot, index],
                recv_sem=recv_sem.at[index],
                device_id=device,
                device_id_type=MESH,
            )

        guarded(condition, lambda: copy().start())
        started.append((condition, copy))

    def arrive(condition, index):
        def wait():
            pltpu.make_async_remote_copy(
                src_ref=o_ref.at[index],
                dst_ref=o_ref.at[index],
                send_sem=send_sem.at[0, index],
                recv_sem=recv_sem.at[index],
                device_id=spot.device(here),
                device_id_type=MESH,
            ).wait_recv()

        guarded(condition, wait)

    def spread(condition, source, index, first):
        for level in levels[first:]:
            for shift in range(1, spot.sizes[level]):
                send(
                    condition,
                    source,
                    index,
                    spot.slots[level, shift],
                    spot.device(spot.moved(**{level: shift})),
                )

    def around(distance):
        if distance == 0:
            return [(None, step)]
        return [(step - distance >= 0, step - distance), (step + distance < length, step + distance)]

    def clipped(position):
        return lax.rem(position + length, length) if length > 1 else position

    spot.greet()
    mine = spot.flat(step, here)
    local = pltpu.make_async_copy(x_ref, o_ref.at[mine], local_sem)
    local.start()
    if length > 1:
        send(step < length - 1, x_ref, mine, 1, spot.device(here, 1))
        send(step > 0, x_ref, mine, 0, spot.device(here, -1))
    spread(None, x_ref, mine, 0)

    def relay(distance):
        if len(levels) < 2:
            return
        level = levels[0]
        for there, position in around(distance):
            for shift in range(1, spot.sizes[level]):
                index = spot.flat(clipped(position), spot.moved(**{level: shift}))
                arrive(there, index)
                spread(there, o_ref.at[index], index, 1)

    for distance in range(1, length):
        for way, (there, position) in enumerate(around(distance)):
            index = spot.flat(clipped(position), here)
            arrive(there, index)
            onward = step < length - 1 if way == 0 else step > 0
            send(
                both(there, onward),
                o_ref.at[index],
                index,
                1 - way,
                spot.device(here, 1 if way == 0 else -1),
            )
            spread(there, o_ref.at[index], index, 0)
        relay(distance - 1)
    relay(length - 1)
    last = levels[-1]
    others = [{}]
    for level in levels[:-1]:
        others = [{**rest, level: shift} for rest in others for shift in range(spot.sizes[level])]
    for position in range(length):
        for rest in others:
            for shift in range(1, spot.sizes[last]):
                arrive(None, spot.flat(position, spot.moved(**{**rest, last: shift})))
    for condition, copy in started:
        guarded(condition, lambda copy=copy: copy().wait_send())
    local.wait()


def gather_blocks(block, lanes, chain, levels, collective_id):
    sizes = device_layout(lanes)
    count = (lanes[0] if chain else 1) * math.prod(sizes[level] for level in levels)
    slots = 2 + sum(sizes[level] - 1 for level in levels)
    return pl.pallas_call(
        functools.partial(gather_kernel, lanes, chain, levels),
        out_shape=jax.ShapeDtypeStruct((count,) + block.shape, block.dtype),
        in_specs=[pl.BlockSpec(memory_space=pltpu.VMEM)],
        out_specs=pl.BlockSpec(memory_space=pl.ANY),
        scratch_shapes=[
            pltpu.SemaphoreType.DMA((slots, count)),
            pltpu.SemaphoreType.DMA((count,)),
            pltpu.SemaphoreType.DMA,
        ],
        compiler_params=pltpu.CompilerParams(collective_id=collective_id, has_side_effects=True),
        cost_estimate=pl.CostEstimate(
            flops=0, bytes_accessed=20 * count * block.size, transcendentals=0
        ),
    )(block)


def add_into(target, parts, condition=None):
    rows = target.shape[0]
    tile = math.gcd(rows, 16)

    def action():
        def body(r, carry):
            window = pl.ds(pl.multiple_of(r * tile, tile), tile)
            total = parts[0][window, :].astype(jnp.float32)
            for part in parts[1:]:
                total = total + part[window, :].astype(jnp.float32)
            target[window, :] = total.astype(target.dtype)
            return carry

        lax.fori_loop(0, rows // tile, body, 0)

    guarded(condition, action)


def scatter_kernel(
    lanes, chain, levels, order, x_ref, o_ref, came0, came1, held0, held1, chained, sems, got0, got1, gotc
):
    spot = Spot(lanes, chain, levels)
    length, step, here = spot.length, spot.step, spot.here
    started = []

    def send(condition, source, target, send_at, recv_at, device):
        def copy():
            return pltpu.make_async_remote_copy(
                src_ref=source,
                dst_ref=target,
                send_sem=send_at,
                recv_sem=recv_at,
                device_id=device,
                device_id_type=MESH,
            )

        guarded(condition, lambda: copy().start())
        started.append((condition, copy))

    def arrive(condition, target, recv_at):
        def wait():
            pltpu.make_async_remote_copy(
                src_ref=target,
                dst_ref=target,
                send_sem=recv_at,
                recv_sem=recv_at,
                device_id=spot.device(here),
                device_id_type=MESH,
            ).wait_recv()

        guarded(condition, wait)

    visits = []
    for distance in range(length - 1, -1, -1):
        if distance == 0:
            visits.append((None, step, 0))
        else:
            visits.append(
                (step - distance >= 0, lax.rem(step - distance + length, length), -1)
            )
            visits.append((step + distance < length, lax.rem(step + distance, length), 1))

    spot.greet()
    first = order[0]
    second = order[1] if len(order) > 1 else None
    n_first = spot.sizes[first]
    n_second = spot.sizes[second] if second else 1

    def second_shifts(own):
        return [0] if own else list(range(1, n_second))

    for own in (False, True):
        for there, position, _ in visits:
            for other in second_shifts(own):
                for shift in range(1, n_first):
                    where = {first: shift}
                    if second:
                        where[second] = other
                    at = spot.moved(**where)
                    lane = position * n_second + (at[second] if second else 0)
                    send(
                        there,
                        x_ref.at[spot.flat(position, at)],
                        came0.at[shift - 1, lane],
                        sems.at[shift - 1, lane],
                        got0.at[shift - 1, lane],
                        spot.device(spot.moved(**{first: shift})),
                    )

    def first_sum(there, position, other):
        at = spot.moved(**({second: other} if second else {}))
        lane = position * n_second + (at[second] if second else 0)
        parts = [x_ref.at[spot.flat(position, at)]]
        for shift in range(1, n_first):
            arrive(there, came0.at[shift - 1, lane], got0.at[shift - 1, lane])
            parts.append(came0.at[shift - 1, lane])
        return parts

    for there, position, _ in visits:
        for other in second_shifts(False):
            parts = first_sum(there, position, other)
            add_into(held0.at[other - 1, position], parts, there)
            send(
                there,
                held0.at[other - 1, position],
                came1.at[other - 1, position],
                sems.at[n_first - 1 + other - 1, position],
                got1.at[other - 1, position],
                spot.device(spot.moved(**{second: other})),
            )
    base = n_first - 1 + n_second - 1
    for there, position, way in visits:
        parts = first_sum(there, position, 0)
        for other in second_shifts(False):
            arrive(there, came1.at[other - 1, position], got1.at[other - 1, position])
            parts.append(came1.at[other - 1, position])
        if way == 0:
            if length > 1:
                for side, exists in ((0, step > 0), (1, step < length - 1)):
                    arrive(exists, chained.at[side, position], gotc.at[side, position])

                def extra(sides):
                    return parts + [chained.at[side, position] for side in sides]

                inside = jnp.logical_and(step > 0, step < length - 1)
                add_into(o_ref, extra((0, 1)), inside)
                add_into(o_ref, extra((1,)), step == 0)
                add_into(o_ref, extra((0,)), step == length - 1)
            else:
                add_into(o_ref, parts)
        else:
            side = 1 if way == -1 else 0
            inner_link = step < length - 1 if way == -1 else step > 0
            with_more = both(there, inner_link)
            alone = both(there, jnp.logical_not(inner_link))
            arrive(with_more, chained.at[side, position], gotc.at[side, position])
            add_into(held1.at[position], parts + [chained.at[side, position]], with_more)
            add_into(held1.at[position], parts, alone)
            send(
                there,
                held1.at[position],
                chained.at[side, position],
                sems.at[base, position],
                gotc.at[side, position],
                spot.device(here, way),
            )
    for condition, copy in started:
        guarded(condition, lambda copy=copy: copy().wait_send())


def scatter_sum(blocks, lanes, chain, levels, order, collective_id, kind=jnp.float32):
    sizes = device_layout(lanes)
    length = lanes[0] if chain else 1
    rows, columns = blocks.shape[1:]
    low = blocks.dtype
    n_first = sizes[order[0]]
    n_second = sizes[order[1]] if len(order) > 1 else 1
    extra = max(n_first - 1, 1)
    further = max(n_second - 1, 1)
    return pl.pallas_call(
        functools.partial(scatter_kernel, lanes, chain, levels, order),
        out_shape=jax.ShapeDtypeStruct((rows, columns), kind),
        in_specs=[pl.BlockSpec(memory_space=pltpu.VMEM)],
        out_specs=pl.BlockSpec(memory_space=pltpu.VMEM),
        scratch_shapes=[
            pltpu.VMEM((extra, length * n_second, rows, columns), low),
            pltpu.VMEM((further, length, rows, columns), low),
            pltpu.VMEM((further, length, rows, columns), low),
            pltpu.VMEM((length, rows, columns), low),
            pltpu.VMEM((2, length, rows, columns), low),
            pltpu.SemaphoreType.DMA((n_first + n_second, length * n_second)),
            pltpu.SemaphoreType.DMA((extra, length * n_second)),
            pltpu.SemaphoreType.DMA((further, length)),
            pltpu.SemaphoreType.DMA((2, length)),
        ],
        compiler_params=pltpu.CompilerParams(collective_id=collective_id, has_side_effects=True),
        cost_estimate=pl.CostEstimate(
            flops=0, bytes_accessed=20 * blocks.size, transcendentals=0
        ),
    )(blocks)


def shards(
    lanes,
    layer_input,
    cotangent,
    seq_lengths,
    norm_attn_in,
    w_query,
    w_key,
    w_value,
    w_out,
    norm_attn_out,
    norm_ffn_in,
    w_gate,
    w_up,
    w_down,
    norm_ffn_out,
):
    outer, inner, tensor = lanes
    low = jnp.bfloat16
    dp = ("outer", "inner")
    shard_rows, width = w_gate.shape
    part = width // outer
    query_cols, key_cols = w_query.shape[1], w_key.shape[1]
    qkv_cols = query_cols + 2 * key_cols

    attn_shard = jnp.concatenate([w_query, w_key, w_value, w_out.T], axis=1)
    attn_full = gather_blocks(attn_shard, lanes, True, ("inner",), 0)
    attn_full = attn_full.reshape(-1, attn_shard.shape[1])
    down_turned = w_down.T
    ffn_shard = jnp.stack(
        [
            jnp.concatenate(
                [item[:, i * part : (i + 1) * part] for item in (w_gate, w_up, down_turned)],
                axis=1,
            )
            for i in range(outer)
        ]
    )
    ffn_mine = swap_blocks(ffn_shard, "outer")
    attn_full, ffn_mine = lax.optimization_barrier((attn_full, ffn_mine))
    ffn_full = collect(ffn_mine, "inner", inner).transpose(1, 0, 2, 3).reshape(-1, 3 * part)

    row_count = layer_input.shape[0]
    split_rows = row_count // tensor
    first_row = lax.axis_index("tensor") * split_rows

    def own_rows(array):
        return lax.dynamic_slice_in_dim(array, first_row, split_rows, 0)

    is_live, allowed, cosine, sine_wave = layout(seq_lengths[0], row_count)
    kv_heads = key_cols // HD
    groups = H // KV
    layer_float = layer_input.astype(jnp.float32)
    h_attn = rms_scale(layer_float, norm_attn_in).astype(low)
    projected = matmul(h_attn, attn_full[:, :qkv_cols])
    query_pre = (
        projected[:, :query_cols].reshape(row_count, kv_heads, groups, HD).transpose(1, 2, 0, 3)
    )
    query = ((query_pre * cosine + rotate_half(query_pre) * sine_wave) * QUERY_SCALE).astype(low)
    key_pre = (
        projected[:, query_cols : query_cols + key_cols]
        .reshape(row_count, kv_heads, HD)
        .transpose(1, 0, 2)
    )
    keys = (key_pre * cosine + rotate_half(key_pre) * sine_wave).astype(low)
    values = (
        projected[:, query_cols + key_cols :]
        .astype(low)
        .reshape(row_count, kv_heads, HD)
        .transpose(1, 0, 2)
    )
    capped = capped_scores(query, keys)
    expo = jnp.where(allowed, jnp.exp(capped), 0.0)
    log_total = jnp.log(jnp.sum(expo, axis=-1, keepdims=True))
    weights = jnp.where(allowed, jnp.exp(capped - log_total), 0.0)
    probs = weights.astype(low)
    mixed = jnp.einsum("kgqs,ksd->kgqd", probs, values, preferred_element_type=jnp.float32).astype(
        low
    )
    mixed_flat = mixed.transpose(2, 0, 1, 3).reshape(row_count, -1)
    out_turned = attn_full[:, qkv_cols:]
    attn_branch = scatter_sum(
        right_product(mixed_flat, out_turned).astype(low).reshape(tensor, split_rows, -1),
        lanes,
        False,
        ("x", "core"),
        ("core", "x"),
        1,
    )
    layer_own = own_rows(layer_float)
    resid = layer_own + rms_scale(attn_branch, norm_attn_out)
    h_ffn = rms_scale(resid, norm_ffn_in).astype(low)

    h_all = gather_blocks(h_ffn, lanes, True, ("x", "core"), 2).reshape(-1, h_ffn.shape[1])
    gate_up = matmul(h_all, ffn_full[:, : 2 * part])
    gate_pre, up_pre = gate_up[:, :part], gate_up[:, part:]
    gelu_gate = gelu_tanh(gate_pre)
    hidden = (gelu_gate * up_pre).astype(low)
    down_full = ffn_full[:, 2 * part :]
    ffn_branch = scatter_sum(
        right_product(hidden, down_full).astype(low).reshape(outer * tensor, split_rows, -1),
        lanes,
        True,
        ("x", "core"),
        ("core", "x"),
        3,
    )
    output_own = (resid + rms_scale(ffn_branch, norm_ffn_out)).astype(low)

    grad_out = own_rows(cotangent).astype(jnp.float32) * own_rows(
        is_live.astype(jnp.float32)[:, None]
    )
    _, pull_four = jax.vjp(rms_scale, ffn_branch, norm_ffn_out)
    grad_ffn_float, grad_norm_ffn_out = pull_four(grad_out)
    grad_ffn_all = gather_blocks(grad_ffn_float.astype(low), lanes, True, ("x", "core"), 4)
    grad_ffn_all = grad_ffn_all.reshape(-1, h_ffn.shape[1])
    grad_hidden = matmul(grad_ffn_all, down_full)
    grad_up = (grad_hidden * gelu_gate).astype(low)
    _, pull_gelu = jax.vjp(gelu_tanh, gate_pre)
    grad_gate = pull_gelu(grad_hidden * up_pre)[0].astype(low)
    grad_both = jnp.concatenate([grad_gate, grad_up], axis=1)
    grad_h_part = right_product(grad_both, ffn_full[:, : 2 * part]).astype(low)
    grad_h_ffn = scatter_sum(
        grad_h_part.reshape(outer * tensor, split_rows, -1),
        lanes,
        True,
        ("x", "core"),
        ("core", "x"),
        5,
    )
    grad_w_ffn = jnp.concatenate(
        [
            left_product(h_all, grad_both).astype(low),
            left_product(grad_ffn_all, hidden).astype(low),
        ],
        axis=1,
    )
    grad_w_ffn = grad_w_ffn.reshape(outer, inner, shard_rows, 3 * part).transpose(1, 0, 2, 3)
    grad_w_ffn = sum_blocks(grad_w_ffn, "inner").astype(low)
    grad_w_ffn = swap_blocks(grad_w_ffn, "outer").astype(jnp.float32)
    sum_gate, sum_up, sum_down = (
        jnp.concatenate([grad_w_ffn[i, :, j * part : (j + 1) * part] for i in range(outer)], axis=1)
        for j in range(3)
    )
    sum_down = sum_down.T

    _, pull_three = jax.vjp(rms_scale, resid, norm_ffn_in)
    grad_resid_part, grad_norm_ffn_in = pull_three(grad_h_ffn)
    grad_resid = grad_out + grad_resid_part
    _, pull_two = jax.vjp(rms_scale, attn_branch, norm_attn_out)
    grad_attn_float, grad_norm_attn_out = pull_two(grad_resid)
    grad_attn_branch = gather_blocks(
        grad_attn_float.astype(low), lanes, False, ("x", "core"), 6
    ).reshape(row_count, -1)
    grad_mixed = matmul(grad_attn_branch, out_turned).astype(low)
    grad_mixed = grad_mixed.reshape(row_count, kv_heads, groups, HD).transpose(1, 2, 0, 3)
    grad_values = jnp.einsum(
        "kgqs,kgqd->ksd", probs, grad_mixed, preferred_element_type=jnp.float32
    ).astype(low)
    grad_probs = jnp.einsum(
        "kgqd,ksd->kgqs", grad_mixed, values, preferred_element_type=jnp.float32
    )
    row_delta = jnp.sum(weights * grad_probs, axis=-1, keepdims=True)
    tanh_part = capped / SOFT_CAP
    grad_scores = (weights * (grad_probs - row_delta) * (1.0 - tanh_part * tanh_part)).astype(low)
    grad_query_raw = jnp.einsum(
        "kgqs,ksd->kgqd", grad_scores, keys, preferred_element_type=jnp.float32
    )
    grad_query = (
        (grad_query_raw * cosine - rotate_half(grad_query_raw) * sine_wave) * QUERY_SCALE
    ).astype(low)
    grad_keys_raw = jnp.einsum(
        "kgqs,kgqd->ksd", grad_scores, query, preferred_element_type=jnp.float32
    )
    grad_keys = (grad_keys_raw * cosine - rotate_half(grad_keys_raw) * sine_wave).astype(low)
    grad_qkv = jnp.concatenate(
        [
            grad_query.transpose(2, 0, 1, 3).reshape(row_count, -1),
            grad_keys.transpose(1, 0, 2).reshape(row_count, -1),
            grad_values.transpose(1, 0, 2).reshape(row_count, -1),
        ],
        axis=1,
    )
    grad_a_part = right_product(grad_qkv, attn_full[:, :qkv_cols]).astype(low)
    grad_h_attn = scatter_sum(
        grad_a_part.reshape(tensor, split_rows, -1),
        lanes,
        False,
        ("x", "core"),
        ("core", "x"),
        7,
    )
    _, pull_one = jax.vjp(rms_scale, layer_own, norm_attn_in)
    grad_input_part, grad_norm_attn_in = pull_one(grad_h_attn)
    input_own = grad_resid + grad_input_part

    layer_output = lax.all_gather(output_own, "tensor", axis=0, tiled=True)
    input_grad = lax.all_gather(input_own.astype(low), "tensor", axis=0, tiled=True)
    norm_rows = jnp.stack(
        [grad_norm_attn_in, grad_norm_attn_out, grad_norm_ffn_in, grad_norm_ffn_out]
    )
    norm_all = lax.all_gather(norm_rows, (*dp, "tensor"), axis=0, tiled=False)
    input_grad = input_grad.astype(jnp.float32)
    position = lax.axis_index("outer") * inner + lax.axis_index("inner")
    norm_all = lax.dynamic_slice_in_dim(norm_all, position * shard_rows, shard_rows, 2)
    sum_attn_in, sum_attn_out, sum_ffn_in, sum_ffn_out = (
        item for item in jnp.sum(norm_all, axis=0)
    )

    grad_w_attn = jnp.concatenate(
        [
            left_product(h_attn, grad_qkv).astype(low),
            left_product(grad_attn_branch, mixed_flat).astype(low),
        ],
        axis=1,
    )
    sum_last = scatter_sum(
        grad_w_attn.reshape(outer * inner, shard_rows, -1),
        lanes,
        True,
        ("inner",),
        ("inner",),
        8,
    )
    sum_out = sum_last[:, qkv_cols:].T
    sum_query = sum_last[:, :query_cols]
    sum_key = sum_last[:, query_cols : query_cols + key_cols]
    sum_value = sum_last[:, query_cols + key_cols : qkv_cols]
    return (
        layer_output,
        input_grad,
        sum_attn_in,
        sum_query,
        sum_key,
        sum_value,
        sum_out,
        sum_attn_out,
        sum_ffn_in,
        sum_gate,
        sum_up,
        sum_down,
        sum_ffn_out,
    )


def solution(mesh):
    dp_size, tensor = mesh.shape["dp"], mesh.shape["tensor"]
    outer = math.gcd(4, dp_size)
    lanes = (outer, dp_size // outer, tensor)
    split = Mesh(mesh.devices.reshape(lanes), ("outer", "inner", "tensor"))
    dp = ("outer", "inner")

    def run(*args):
        return jax.shard_map(
            lambda *blocks: shards(lanes, *blocks),
            mesh=split,
            in_specs=(
                P(dp, None),
                P(dp, None),
                P(dp, None),
                P(),
                P(dp, "tensor"),
                P(dp, "tensor"),
                P(dp, "tensor"),
                P("tensor", dp),
                P(),
                P(),
                P(dp, "tensor"),
                P(dp, "tensor"),
                P("tensor", dp),
                P(),
            ),
            out_specs=(
                P(dp, None),
                P(dp, None),
                P(dp),
                P(dp, "tensor"),
                P(dp, "tensor"),
                P(dp, "tensor"),
                P("tensor", dp),
                P(dp),
                P(dp),
                P(dp, "tensor"),
                P(dp, "tensor"),
                P("tensor", dp),
                P(dp),
            ),
            check_vma=False,
        )(*args)

    return run
```

time: 1860 us -> 941 us (0.51)
  the two profiles are of different devices: /device:TPU:0 before, /device:TPU:26 now
where the time goes in v1:
time: 941 us; the launch traced here: 931 us
  Pallas kernels  504 us (54%)
  waiting for transfers between devices  138 us (15%)
  matrix products  103 us (11%)
  local copies, waits for them, and re-layouts  97.6 us (10%)
  other arithmetic  67.5 us (7%)
  between operations  15 us (2%)
    pallas_call x4, Pallas kernels, gather_blocks(): pl.pallas_call(functools.partial(gather_kernel, lanes, chain, levels), ou...  269 us
    pallas_call x5, Pallas kernels, scatter_sum(): pl.pallas_call(functools.partial(scatter_kernel, lanes, chain, levels, or...  235 us
    ppermute x1, waiting for transfers between devices, sum_blocks(): lax.ppermute(pick(blocks, lax.rem(here + step, size)), axis, [(i, (i + st...  83.4 us
    ppermute x6, waiting for transfers between devices, swap_blocks(): lax.ppermute(pick(blocks, lax.rem(here + step, size)), axis, [(i, (i + st...  53.8 us
    dot_general x4, matrix products, matmul(): return jnp.dot(left, right, preferred_element_type=jnp.float32)  31.9 us
    dot_general x4, matrix products, right_product(): jnp.einsum('tc,dc->td', left, right, preferred_element_type=jnp.float32)  29.3 us
    dot_general x4, matrix products, left_product(): jnp.einsum('td,tc->dc', left, right, preferred_element_type=jnp.float32)  27.2 us
  transfers between devices with their start and end apart: 11, of which 2 were waited for; matrix products, arithmetic and copies ran while one was open for 12% of the time, Pallas kernels for 33%

profile of v1, /device:TPU:26, one launch (start us, length us, event | category | flops | bytes accessed | tf_op | source)
XLA Modules:
  0.0 931.2 jit_solution(9639210566980750388)
XLA Ops:
  7.3 2.7 fusion.103
  19.2 3.2 concatenate.81
  39.4 157.8 %shard_map.237 = bf16[8,288,1536]{2,1,0:T(8,128)(2,1)} custom-call(bf16[288,1536]{1,0:T(8,128)(2,1)} %pad_maximum_fusion.6.x_ref), custom_call_target="tpu_custom_call" | custom-call | bytes 70778880 | tf_op jit(solution)/shard_map/pallas_call | solution.py:304
  207.5 4.4 fusion.7
  220.4 4.2 convolution_convert_fusion.7
  224.6 15.4 %shard_map.238 = f32[96,2304]{1,0:T(8,128)} custom-call(bf16[4,96,2304]{2,1,0:T(8,128)(2,1)} %bitcast.192), custom_call_target="tpu_custom_call" | custom-call | bytes 17694720 | tf_op jit(solution)/shard_map/pallas_call | solution.py:480
  244.0 51.9 %shard_map.239 = bf16[16,96,2304]{2,1,0:T(8,128)(2,1)} custom-call(bf16[96,2304]{1,0:T(8,128)(2,1)} %multiply_convert_fusion.3.x_ref), custom_call_target="tpu_custom_call" | custom-call | bytes 70778880 | tf_op jit(solution)/shard_map/pallas_call | solution.py:304
  295.9 3.3 fusion.25
  299.8 2.8 bitcast_dynamic-update-slice_fusion.1
  302.6 2.8 bitcast_dynamic-update-slice_fusion
  305.8 11.3 %fusion.4 = f32[1536,1152]{0,1:T(8,128)} fusion(bf16[1536,2304]{1,0:T(8,128)(2,1)S(1)} %bitcast.172, bf16[2304,1728]{1,0:T(8,128)(2,1)S(1)} %bitcast.163), kind=kOutput, calls=%fused_computation.15 | convolution fusion | flops 8153726976 | bytes 19464192 | tf_op jit(solution)/shard_map/dot_general | solution.py:59
  317.1 4.3 multiply_convert_fusion.1
  321.4 7.8 convolution_convert_fusion.1
  329.2 64.3 %shard_map.240 = f32[96,2304]{1,0:T(8,128)} custom-call(bf16[16,96,2304]{2,1,0:T(8,128)(2,1)} %bitcast.182), custom_call_target="tpu_custom_call" | custom-call | bytes 70778880 | tf_op jit(solution)/shard_map/pallas_call | solution.py:480
  397.2 2.8 fusion.43
  400.0 44.1 %shard_map.241 = bf16[16,96,2304]{2,1,0:T(8,128)(2,1)} custom-call(bf16[96,2304]{1,0:T(8,128)(2,1)} %get-tuple-element.73.x_ref), custom_call_target="tpu_custom_call" | custom-call | bytes 70778880 | tf_op jit(solution)/shard_map/pallas_call | solution.py:304
  444.1 12.9 %fusion.12 = (bf16[1536,576]{0,1:T(8,128)(2,1)S(1)}, bf16[1536,576]{0,1:T(8,128)(2,1)}) fusion(f32[1536,1152]{0,1:T(8,128)} %fusion.4, bf16[1536,2304]{1,0:T(8,128)(2,1)} %bitcast.173, bf16[2304,1728]{1,0:T(8,128)(2,1)} %bitcast.165), kind=kOutput, calls=%fused_computation.31 | convolution fusion | flops 4101636096 | bytes 20643840 | tf_op jit(solution)/shard_map/dot_general | solution.py:59
  457.1 5.5 convolution_convert_fusion.4
  462.6 14.2 %convolution_convert_fusion.2 = bf16[2304,1152]{0,1:T(8,128)(2,1)} fusion(bf16[1536,2304]{1,0:T(8,128)(2,1)} %bitcast.169, bf16[1536,576]{0,1:T(8,128)(2,1)S(1)} %copy-done.41, bf16[1536,576]{0,1:T(8,128)(2,1)S(1)} %get-tuple-element.34), kind=kOutput, calls=%fused_computation.4 | convolution fusion | flops 8163459072 | bytes 15925248 | tf_op jit(solution)/shard_map/td,tc->dc/dot_general | solution.py:63
  476.8 11.4 %convolution_convert_fusion = bf16[1536,2304]{1,0:T(8,128)(2,1)} fusion(bf16[2304,1728]{1,0:T(8,128)(2,1)S(1)} %bitcast.168, bf16[1536,576]{0,1:T(8,128)(2,1)S(1)} %copy-done.42, bf16[1536,576]{0,1:T(8,128)(2,1)S(1)} %get-tuple-element.34), kind=kOutput, calls=%fused_computation.2 | convolution fusion | flops 8164343808 | bytes 15925248 | tf_op jit(solution)/shard_map/tc,dc->td/dot_general | solution.py:67
  488.1 54.6 %shard_map.242 = f32[96,2304]{1,0:T(8,128)} custom-call(bf16[16,96,2304]{2,1,0:T(8,128)(2,1)} %bitcast.181), custom_call_target="tpu_custom_call" | custom-call | bytes 70778880 | tf_op jit(solution)/shard_map/pallas_call | solution.py:480
  544.8 2.4 multiply_reduce_fusion.4
  549.1 15.6 %shard_map.243 = bf16[4,96,2304]{2,1,0:T(8,128)(2,1)} custom-call(bf16[96,2304]{1,0:T(8,128)(2,1)} %fusion.45.x_ref), custom_call_target="tpu_custom_call" | custom-call | bytes 17694720 | tf_op jit(solution)/shard_map/pallas_call | solution.py:304
  564.7 3.3 fusion.30
  570.6 3.4 fusion.40
  574.0 3.4 fusion.37
  577.4 3.2 fusion.34
  581.7 6.0 convolution_convert_fusion.6
  587.7 17.0 %shard_map.244 = f32[96,2304]{1,0:T(8,128)} custom-call(bf16[4,96,2304]{2,1,0:T(8,128)(2,1)} %bitcast.191), custom_call_target="tpu_custom_call" | custom-call | bytes 17694720 | tf_op jit(solution)/shard_map/pallas_call | solution.py:480
  609.6 6.9 pad_maximum_fusion
  616.5 11.6 %copy.109 = bf16[2304,1728]{1,0:T(8,128)(2,1)} copy(bf16[2304,1728]{0,1:T(8,128)(2,1)} %pad_maximum_fusion) | data formatting | bytes 15925248 | tf_op jit(solution)/shard_map/concatenate | solution.py:633
  628.2 4.5 dynamic-slice_bitcast_fusion
  635.7 4.7 convolution_convert_fusion.3
  640.4 2.8 convolution_convert_fusion.5
  643.2 83.4 %collective-permute-done.4 = bf16[4,288,1728]{2,1,0:T(8,128)(2,1)} collective-permute-done((bf16[4,288,1728]{2,1,0:T(8,128)(2,1)}, bf16[4,288,1728]{2,1,0:T(8,128)(2,1)}, u32[]{:S(2)}, u32[]{:S(2)}) %collective-permute-start.4) | collective-permute-done | bytes 3981344 | tf_op jit(solution)/shard_map/ppermute | solution.py:114
  726.6 4.4 fusion.2
  735.3 5.0 pad_maximum_fusion.1
  740.3 10.3 %copy.108 = bf16[2304,1536]{1,0:T(8,128)(2,1)} copy(bf16[2304,1536]{0,1:T(8,128)(2,1)} %pad_maximum_fusion.1) | data formatting | bytes 14155776 | tf_op jit(solution)/shard_map/concatenate | solution.py:712
  750.6 83.4 %shard_map.245 = f32[288,1536]{1,0:T(8,128)} custom-call(bf16[8,288,1536]{2,1,0:T(8,128)(2,1)} %bitcast.162), custom_call_target="tpu_custom_call" | custom-call | bytes 70778880 | tf_op jit(solution)/shard_map/pallas_call | solution.py:480
  837.5 2.4 slice_bitcast_fusion.12
  841.7 3.5 convert_element_type.156
  848.0 53.8 %collective-permute-done.6 = bf16[288,1728]{1,0:T(8,128)(2,1)S(1)} collective-permute-done((bf16[288,1728]{1,0:T(8,128)(2,1)S(1)}, bf16[288,1728]{1,0:T(8,128)(2,1)S(1)}, u32[]{:S(2)}, u32[]{:S(2)}) %collective-permute-start.6) | collective-permute-done | bytes 995360 | tf_op jit(solution)/shard_map/ppermute | solution.py:86
  903.9 2.8 convert_element_type.165
  906.7 3.3 slice_bitcast_fusion
  910.1 4.5 concatenate.100
  914.6 4.5 concatenate.99
  919.1 2.4 concatenate.98
  921.5 2.8 copy.136
  (191 shorter events, 83.3 us)
Async XLA Ops:
  7.2 832.7 %all-gather.10.cloned.1.call-start = ((), (), s32[]{:S(2)}) async-start(), calls=%async_computation.2 | async-start | bytes 1216512 | tf_op jit(solution)/shard_map/all_gather | solution.py:704
  26.3 4.6 copy-start.37
  26.3 9.1 copy-start.24
  26.3 9.1 copy-start.25
  26.3 9.1 copy-start.26
  28.1 172.6 %collective-permute-start = (bf16[288,1728]{1,0:T(8,128)(2,1)}, bf16[288,1728]{1,0:T(8,128)(2,1)}, u32[]{:S(2)}, u32[]{:S(2)}) collective-permute-start(bf16[288,1728]{1,0:T(8,128)(2,1)} %get-tuple-element.54), channel_id=1, source_target_pairs={{0,8},{8,16},{16,24},{24,0},{1,9},{9,17},{17,25},{25,1},{2,10},{10... | collective-permute-start | bytes 2985992 | tf_op jit(solution)/shard_map/ppermute | solution.py:86
  28.3 174.7 %collective-permute-start.1 = (bf16[288,1728]{1,0:T(8,128)(2,1)}, bf16[288,1728]{1,0:T(8,128)(2,1)}, u32[]{:S(2)}, u32[]{:S(2)}) collective-permute-start(bf16[288,1728]{1,0:T(8,128)(2,1)} %get-tuple-element.53), channel_id=1, source_target_pairs={{0,16},{8,24},{16,0},{24,8},{1,17},{9,25},{17,1},{25,9},{2,18},{10... | collective-permute-start | bytes 2985992 | tf_op jit(solution)/shard_map/ppermute | solution.py:86
  30.0 175.3 %collective-permute-start.2 = (bf16[288,1728]{1,0:T(8,128)(2,1)S(1)}, bf16[288,1728]{1,0:T(8,128)(2,1)}, u32[]{:S(2)}, u32[]{:S(2)}) collective-permute-start(bf16[288,1728]{1,0:T(8,128)(2,1)S(1)} %get-tuple-element.52), channel_id=1, source_target_pairs={{0,24},{8,0},{16,8},{24,16},{1,25},{9,1},{17,9},{25,17},{2,26},{10... | collective-permute-start | bytes 2985992 | tf_op jit(solution)/shard_map/ppermute | solution.py:86
  39.4 159.8 %copy-start.32 = (f32[384]{0:T(512)S(1)}, f32[384]{0:T(512)}, u32[]{:S(2)}) copy-start(f32[384]{0:T(512)} %get-tuple-element.88) | copy-start | bytes 4612
  197.1 10.4 %copy-start.31 = (f32[2304]{0:T(1024)S(1)}, f32[2304]{0:T(1024)}, u32[]{:S(2)}) copy-start(f32[2304]{0:T(1024)} %param.17) | copy-start | bytes 27652
  212.8 89.9 %collective-permute-start.3 = (bf16[4,288,1728]{2,1,0:T(8,128)(2,1)}, bf16[4,288,1728]{2,1,0:T(8,128)(2,1)}, u32[]{:S(2)}, u32[]{:S(2)}) collective-permute-start(bf16[4,288,1728]{2,1,0:T(8,128)(2,1)} %bitcast_dynamic-update-slice_fusion.5), channel_id=1, source_target_pairs={{0,4},{4,0},{1,5},{5,1},{2,6},{6,2},{3,7},{7,3},{8,12},{12,8},{9,1... | collective-permute-start | bytes 11943944 | tf_op jit(solution)/shard_map/ppermute | solution.py:102
  217.9 6.6 copy-start.16
  218.3 6.3 copy-start.18
  220.4 19.5 %copy-start.39 = (bf16[2,384,256]{1,2,0:T(8,128)(2,1)}, bf16[2,384,256]{1,2,0:T(8,128)(2,1)S(1)}, u32[]{:S(2)}) copy-start(bf16[2,384,256]{1,2,0:T(8,128)(2,1)S(1)} %convolution_convert_fusion.8) | copy-start | bytes 1179652
  220.4 20.9 %copy-start.29 = (f32[2304]{0:T(1024)S(1)}, f32[2304]{0:T(1024)}, u32[]{:S(2)}) copy-start(f32[2304]{0:T(1024)} %param.22) | copy-start | bytes 27652
  224.6 18.5 %copy-start.28 = (f32[2304]{0:T(1024)S(1)}, f32[2304]{0:T(1024)}, u32[]{:S(2)}) copy-start(f32[2304]{0:T(1024)} %param.23) | copy-start | bytes 27652
  243.1 52.8 %copy-start.34 = (f32[96]{0:T(128)}, f32[96]{0:T(128)S(1)}, u32[]{:S(2)}) copy-start(f32[96]{0:T(128)S(1)} %get-tuple-element.56) | copy-start | bytes 1156
  299.8 5.7 slice-start.2
  305.4 16.0 %copy-start.2 = (bf16[2,4,288,1728]{3,2,0,1:T(8,128)(2,1)}, bf16[2,4,288,1728]{3,2,0,1:T(8,128)(2,1)S(1)}, u32[]{:S(2)}) copy-start(bf16[2,4,288,1728]{3,2,0,1:T(8,128)(2,1)S(1)} %bitcast_dynamic-update-slice_fusion) | copy-start | bytes 23887876
  321.4 7.8 copy-start.12
  329.2 65.7 %copy-start.30 = (f32[2304]{0:T(1024)S(1)}, f32[2304]{0:T(1024)}, u32[]{:S(2)}) copy-start(f32[2304]{0:T(1024)} %param.27) | copy-start | bytes 27652
  329.2 65.7 %copy-start.33 = (f32[96]{0:T(128)S(1)}, f32[96]{0:T(128)}, u32[]{:S(2)}) copy-start(f32[96]{0:T(128)} %dynamic-slice.9) | copy-start | bytes 1156
  444.1 13.0 %copy-start.6 = (bf16[16,96,2304]{2,1,0:T(8,128)(2,1)S(1)}, bf16[16,96,2304]{2,1,0:T(8,128)(2,1)}, u32[]{:S(2)}) copy-start(bf16[16,96,2304]{2,1,0:T(8,128)(2,1)} %shard_map.241) | copy-start | bytes 21233668
  444.1 12.9 %copy-start.13 = (bf16[1536,576]{0,1:T(8,128)(2,1)S(1)}, bf16[1536,576]{0,1:T(8,128)(2,1)}, u32[]{:S(2)}) copy-start(bf16[1536,576]{0,1:T(8,128)(2,1)} %copy-done.12) | copy-start | bytes 5308420
  457.0 5.6 copy-start.41
  457.0 19.7 %slice-start = ((s8[8257536]{0:T(1024)(128)(4,1)}), s8[4194304]{0:T(1024)(128)(4,1)S(1)}, s32[]{:S(2)}) async-start(s8[8257536]{0:T(1024)(128)(4,1)} %bitcast.166), calls=%async_computation.3 | async-start | bytes 8388608
  462.6 14.2 %slice-start.1 = ((s8[8257536]{0:T(1024)(128)(4,1)}), s8[4063232]{0:T(1024)(128)(4,1)S(1)}, s32[]{:S(2)}) async-start(s8[8257536]{0:T(1024)(128)(4,1)} %bitcast.166), calls=%async_computation.4 | async-start | bytes 8126464
  462.6 14.2 %copy-start.42 = (bf16[1536,576]{0,1:T(8,128)(2,1)S(1)}, bf16[1536,576]{0,1:T(8,128)(2,1)}, u32[]{:S(2)}) copy-start(bf16[1536,576]{0,1:T(8,128)(2,1)} %get-tuple-element.35) | copy-start | bytes 5308420
  488.1 56.6 %copy-start = (f32[96,2304]{1,0:T(8,128)S(1)}, f32[96,2304]{1,0:T(8,128)}, u32[]{:S(2)}) copy-start(f32[96,2304]{1,0:T(8,128)} %shard_map.238) | copy-start | bytes 2654212
  564.7 5.9 copy-start.22
  568.0 6.0 copy-start.17
  574.0 6.6 copy-start.11
  581.7 6.0 copy-start.23
  581.7 23.0 %copy-start.1 = (f32[384,2304]{1,0:T(8,128)S(1)}, f32[384,2304]{1,0:T(8,128)}, u32[]{:S(2)}) copy-start(f32[384,2304]{1,0:T(8,128)} %convert_element_type.127) | copy-start | bytes 10616836
  609.6 232.1 %all-gather.8.cloned.1.call-start = ((), (), s32[]{:S(2)}) async-start(), calls=%async_computation.1 | async-start | bytes 2211840 | tf_op jit(solution)/shard_map/all_gather | solution.py:700
  628.2 5.7 copy-start.35
  628.2 5.7 copy-start.36
  628.2 5.7 copy-start.4
  628.2 5.7 copy-start.5
  632.7 93.9 %collective-permute-start.4 = (bf16[4,288,1728]{2,1,0:T(8,128)(2,1)}, bf16[4,288,1728]{2,1,0:T(8,128)(2,1)}, u32[]{:S(2)}, u32[]{:S(2)}) collective-permute-start(bf16[4,288,1728]{2,1,0:T(8,128)(2,1)} %dynamic-slice_bitcast_fusion), channel_id=1, source_target_pairs={{0,4},{4,0},{1,5},{5,1},{2,6},{6,2},{3,7},{7,3},{8,12},{12,8},{9,1... | collective-permute-start | bytes 11943944 | tf_op jit(solution)/shard_map/ppermute | solution.py:114
  635.0 210.2 %all-gather.6.cloned.1.call-start = ((), (), s32[]{:S(2)}) async-start(), calls=%async_computation | async-start | bytes 2211840 | tf_op jit(solution)/shard_map/all_gather | solution.py:699
  635.7 4.7 copy-start.9
  635.7 4.7 copy-start.40
  735.2 110.5 %collective-permute-start.5 = (bf16[288,1728]{1,0:T(8,128)(2,1)}, bf16[288,1728]{1,0:T(8,128)(2,1)}, u32[]{:S(2)}, u32[]{:S(2)}) collective-permute-start(bf16[288,1728]{1,0:T(8,128)(2,1)} %get-tuple-element.50), channel_id=1, source_target_pairs={{0,8},{8,16},{16,24},{24,0},{1,9},{9,17},{17,25},{25,1},{2,10},{10... | collective-permute-start | bytes 2985992 | tf_op jit(solution)/shard_map/ppermute | solution.py:86
  750.6 83.4 %copy-start.20 = (bf16[288,1728]{1,0:T(8,128)(2,1)S(1)}, bf16[288,1728]{1,0:T(8,128)(2,1)}, u32[]{:S(2)}) copy-start(bf16[288,1728]{1,0:T(8,128)(2,1)} %get-tuple-element.49) | copy-start | bytes 2985988
  834.0 67.8 %collective-permute-start.6 = (bf16[288,1728]{1,0:T(8,128)(2,1)S(1)}, bf16[288,1728]{1,0:T(8,128)(2,1)S(1)}, u32[]{:S(2)}, u32[]{:S(2)}) collective-permute-start(bf16[288,1728]{1,0:T(8,128)(2,1)S(1)} %copy-done.20), channel_id=1, source_target_pairs={{0,16},{8,24},{16,0},{24,8},{1,17},{9,25},{17,1},{25,9},{2,18},{10... | collective-permute-start | bytes 2985992 | tf_op jit(solution)/shard_map/ppermute | solution.py:86
  837.5 7.7 copy-start.19
  845.2 57.6 %collective-permute-start.7 = (bf16[288,1728]{1,0:T(8,128)(2,1)S(1)}, bf16[288,1728]{1,0:T(8,128)(2,1)S(1)}, u32[]{:S(2)}, u32[]{:S(2)}) collective-permute-start(bf16[288,1728]{1,0:T(8,128)(2,1)S(1)} %copy-done.19), channel_id=1, source_target_pairs={{0,24},{8,0},{16,8},{24,16},{1,25},{9,1},{17,9},{25,17},{2,26},{10... | collective-permute-start | bytes 2985992 | tf_op jit(solution)/shard_map/ppermute | solution.py:86
  (10 other events, 26.1 us)
Sparse Core Ops, SparseCore 0:
  609.7 54.8 all-gather.9
  666.7 19.8 all-gather.7
  688.1 20.7 all-gather.5

commit v2 on v1

--- a/solution.py
+++ b/solution.py
@@ -57,10 +57,6 @@
 
 def matmul(left, right):
     return jnp.dot(left, right, preferred_element_type=jnp.float32)
-
-
-def left_product(left, right):
-    return jnp.einsum("td,tc->dc", left, right, preferred_element_type=jnp.float32)
 
 
 def right_product(left, right):
@@ -500,6 +496,293 @@
     )(blocks)
 
 
+def weight_grads_kernel(h_ref, g_ref, both_ref, hidden_ref, o_ref):
+    turned = (((0,), (0,)), ((), ()))
+    wide = both_ref.shape[1]
+    o_ref[:, :wide] = lax.dot_general(
+        h_ref[...], both_ref[...], turned, preferred_element_type=jnp.float32
+    ).astype(o_ref.dtype)
+    o_ref[:, wide:] = lax.dot_general(
+        g_ref[...], hidden_ref[...], turned, preferred_element_type=jnp.float32
+    ).astype(o_ref.dtype)
+
+
+def weight_grads(h_all, g_all, both, hidden):
+    tokens, width = h_all.shape
+    tile = math.gcd(width, 384)
+    columns = both.shape[1] + hidden.shape[1]
+    return pl.pallas_call(
+        weight_grads_kernel,
+        grid=(width // tile,),
+        out_shape=jax.ShapeDtypeStruct((width, columns), h_all.dtype),
+        in_specs=[
+            pl.BlockSpec((tokens, tile), lambda i: (0, i)),
+            pl.BlockSpec((tokens, tile), lambda i: (0, i)),
+            pl.BlockSpec(both.shape, lambda i: (0, 0)),
+            pl.BlockSpec(hidden.shape, lambda i: (0, 0)),
+        ],
+        out_specs=pl.BlockSpec((tile, columns), lambda i: (i, 0)),
+        cost_estimate=pl.CostEstimate(
+            flops=2 * tokens * width * columns,
+            bytes_accessed=4 * tokens * width + 2 * width * columns,
+            transcendentals=0,
+        ),
+    )(h_all, g_all, both, hidden)
+
+
+def unpack_kernel(part, x_ref, gate_ref, up_ref, down_ref):
+    for i in range(x_ref.shape[0]):
+        columns = slice(i * part, (i + 1) * part)
+        for j, target in enumerate((gate_ref, up_ref, down_ref)):
+            target[:, columns] = x_ref[i, :, j * part : (j + 1) * part].astype(jnp.float32)
+
+
+def unpack(blocks, part):
+    count, rows, columns = blocks.shape
+    tile = math.gcd(rows, 48)
+    width = count * part
+    return pl.pallas_call(
+        functools.partial(unpack_kernel, part),
+        grid=(rows // tile,),
+        out_shape=[jax.ShapeDtypeStruct((rows, width), jnp.float32)] * 3,
+        in_specs=[pl.BlockSpec((count, tile, columns), lambda i: (0, i, 0))],
+        out_specs=[pl.BlockSpec((tile, width), lambda i: (i, 0))] * 3,
+    )(blocks)
+
+
+def finish_kernel(
+    lanes, h_ref, a_ref, qkv_ref, mixed_ref, strip_ref, tail_ref,
+    o_ref, tails_ref,
+    made, came, held, chained, shared, total,
+    send0, got0, sendc, gotc, sendt, gott, sends, gots, local_sem,
+):
+    outer, inner, tensor = lanes
+    step = lax.axis_index("outer")
+    row = lax.axis_index("inner")
+    lane = lax.axis_index("tensor")
+    rows = h_ref.shape[0] // (outer * inner)
+    extra = strip_ref.shape[1]
+    wide = qkv_ref.shape[1]
+    left, right = step > 0, step < outer - 1
+
+    def peer_row(shift):
+        return lax.rem(row + shift, inner)
+
+    def peer_lane(shift):
+        return lax.rem(lane + shift, tensor)
+
+    barrier = pltpu.get_barrier_semaphore()
+    for shift in range(1, inner):
+        pl.semaphore_signal(barrier, device_id=(step, peer_row(shift), lane), device_id_type=MESH)
+    for shift in range(1, tensor):
+        pl.semaphore_signal(barrier, device_id=(step, row, peer_lane(shift)), device_id_type=MESH)
+    for there, move in ((left, -1), (right, 1)):
+
+        @pl.when(there)
+        def _(move=move):
+            pl.semaphore_signal(barrier, device_id=(step + move, row, lane), device_id_type=MESH)
+
+    pl.semaphore_wait(
+        barrier, inner + tensor - 2 + left.astype(jnp.int32) + right.astype(jnp.int32)
+    )
+
+    def make(index):
+        window = pl.ds(pl.multiple_of(index * rows, rows), rows)
+        made[index, :rows, :wide] = jnp.dot(
+            h_ref[window, :], qkv_ref[...], preferred_element_type=jnp.float32
+        ).astype(made.dtype)
+        made[index, :rows, wide:] = jnp.dot(
+            a_ref[window, :], mixed_ref[...], preferred_element_type=jnp.float32
+        ).astype(made.dtype)
+        made[index, rows:, :] = strip_ref[index]
+
+    def remote(source, target, send_at, recv_at, device):
+        return pltpu.make_async_remote_copy(
+            src_ref=source,
+            dst_ref=target,
+            send_sem=send_at,
+            recv_sem=recv_at,
+            device_id=device,
+            device_id_type=MESH,
+        )
+
+    upper = (step * 2 >= outer).astype(jnp.int32)
+
+    def place(j):
+        return upper * j + (1 - upper) * (outer - 1 - j)
+
+    def row_copy(k):
+        shift = 1 + lax.div(k, outer)
+        position = place(lax.rem(k, outer))
+        there = peer_row(shift)
+        return position * inner + there, remote(
+            made.at[position * inner + there],
+            came.at[shift - 1, position],
+            send0.at[shift - 1, position],
+            got0.at[shift - 1, position],
+            (step, there, lane),
+        )
+
+    def first(k, carry):
+        index, copy = row_copy(k)
+        make(index)
+        copy.start()
+        return carry
+
+    lax.fori_loop(0, outer * (inner - 1), first, 0)
+
+    def tail_copy(shift):
+        return remote(
+            tail_ref,
+            tails_ref.at[lane],
+            sendt.at[shift - 1],
+            gott.at[shift - 1],
+            (step, row, peer_lane(shift)),
+        )
+
+    local = pltpu.make_async_copy(tail_ref, tails_ref.at[lane], local_sem)
+    local.start()
+    for shift in range(1, tensor):
+        tail_copy(shift).start()
+
+    def second(j, carry):
+        make(place(j) * inner + row)
+        return carry
+
+    lax.fori_loop(0, outer, second, 0)
+
+    visits = []
+    for distance in range(outer - 1, -1, -1):
+        if distance == 0:
+            visits.append((None, step, 0))
+        else:
+            visits.append((step - distance >= 0, lax.rem(step - distance + outer, outer), -1))
+            visits.append((step + distance < outer, lax.rem(step + distance, outer), 1))
+
+    started = []
+    for there, position, way in visits:
+        parts = [made.at[position * inner + row]]
+        for shift in range(1, inner):
+            target = came.at[shift - 1, position]
+            guarded(
+                there,
+                remote(
+                    target,
+                    target,
+                    send0.at[shift - 1, position],
+                    got0.at[shift - 1, position],
+                    (step, row, lane),
+                ).wait_recv,
+            )
+            parts.append(target)
+
+        def linked(side, position=position):
+            target = chained.at[side, position]
+            return remote(
+                target, target, sendc.at[position], gotc.at[side, position], (step, row, lane)
+            )
+
+        if way == 0:
+            for side, exists in ((0, left), (1, right)):
+                guarded(exists, linked(side).wait_recv)
+            inside = jnp.logical_and(left, right)
+            add_into(total, parts + [chained.at[0, position], chained.at[1, position]], inside)
+            add_into(total, parts + [chained.at[1, position]], jnp.logical_not(left))
+            add_into(total, parts + [chained.at[0, position]], jnp.logical_not(right))
+        else:
+            side = 1 if way == -1 else 0
+            link = right if way == -1 else left
+            more, alone = jnp.logical_and(there, link), jnp.logical_and(there, jnp.logical_not(link))
+            guarded(more, linked(side).wait_recv)
+            add_into(held.at[position], parts + [chained.at[side, position]], more)
+            add_into(held.at[position], parts, alone)
+            copy = remote(
+                held.at[position],
+                chained.at[side, position],
+                sendc.at[position],
+                gotc.at[side, position],
+                (step + way, row, lane),
+            )
+            guarded(there, copy.start)
+            started.append((there, copy))
+
+    strip = total.at[pl.ds(rows, extra), :]
+    small = [
+        remote(
+            strip,
+            shared.at[shift - 1],
+            sends.at[shift - 1],
+            gots.at[shift - 1],
+            (step, row, peer_lane(shift)),
+        )
+        for shift in range(1, tensor)
+    ]
+    for copy in small:
+        copy.start()
+    o_ref[pl.ds(0, rows), :] = total[pl.ds(0, rows), :]
+    summed = total[pl.ds(rows, extra), :]
+    for shift in range(1, tensor):
+        small[shift - 1].wait_recv()
+        summed = summed + shared[shift - 1]
+    o_ref[pl.ds(rows, extra), :] = summed
+
+    for shift in range(1, tensor):
+        small[shift - 1].wait_send()
+        tail_copy(shift).wait()
+    for there, copy in started:
+        guarded(there, copy.wait_send)
+
+    def drain(k, carry):
+        row_copy(k)[1].wait_send()
+        return carry
+
+    lax.fori_loop(0, outer * (inner - 1), drain, 0)
+    local.wait()
+
+
+def finish(lanes, h_turned, a_turned, grad_qkv, mixed, strips, tail, collective_id):
+    outer, inner, tensor = lanes
+    low = h_turned.dtype
+    count, extra, columns = strips.shape
+    rows = h_turned.shape[0] // count
+    block = (rows + extra, columns)
+    peers = max(inner - 1, 1)
+    vmem = pl.BlockSpec(memory_space=pltpu.VMEM)
+    dma = pltpu.SemaphoreType.DMA
+    return pl.pallas_call(
+        functools.partial(finish_kernel, lanes),
+        out_shape=[
+            jax.ShapeDtypeStruct(block, jnp.float32),
+            jax.ShapeDtypeStruct((tensor,) + tail.shape, low),
+        ],
+        in_specs=[vmem] * 6,
+        out_specs=[vmem, pl.BlockSpec(memory_space=pl.ANY)],
+        scratch_shapes=[
+            pltpu.VMEM((count,) + block, low),
+            pltpu.VMEM((peers, outer) + block, low),
+            pltpu.VMEM((outer,) + block, low),
+            pltpu.VMEM((2, outer) + block, low),
+            pltpu.VMEM((tensor - 1, extra, columns), jnp.float32),
+            pltpu.VMEM(block, jnp.float32),
+            dma((peers, outer)),
+            dma((peers, outer)),
+            dma((outer,)),
+            dma((2, outer)),
+            dma((tensor - 1,)),
+            dma((tensor - 1,)),
+            dma((tensor - 1,)),
+            dma((tensor - 1,)),
+            dma,
+        ],
+        compiler_params=pltpu.CompilerParams(collective_id=collective_id, has_side_effects=True),
+        cost_estimate=pl.CostEstimate(
+            flops=2 * h_turned.size * columns,
+            bytes_accessed=20 * count * rows * columns,
+            transcendentals=0,
+        ),
+    )(h_turned, a_turned, grad_qkv, mixed, strips, tail)
+
+
 def shards(
     lanes,
     layer_input,
@@ -519,7 +802,6 @@
 ):
     outer, inner, tensor = lanes
     low = jnp.bfloat16
-    dp = ("outer", "inner")
     shard_rows, width = w_gate.shape
     part = width // outer
     query_cols, key_cols = w_query.shape[1], w_key.shape[1]
@@ -630,20 +912,11 @@
         ("core", "x"),
         5,
     )
-    grad_w_ffn = jnp.concatenate(
-        [
-            left_product(h_all, grad_both).astype(low),
-            left_product(grad_ffn_all, hidden).astype(low),
-        ],
-        axis=1,
-    )
+    grad_w_ffn = weight_grads(h_all, grad_ffn_all, grad_both, hidden)
     grad_w_ffn = grad_w_ffn.reshape(outer, inner, shard_rows, 3 * part).transpose(1, 0, 2, 3)
     grad_w_ffn = sum_blocks(grad_w_ffn, "inner").astype(low)
-    grad_w_ffn = swap_blocks(grad_w_ffn, "outer").astype(jnp.float32)
-    sum_gate, sum_up, sum_down = (
-        jnp.concatenate([grad_w_ffn[i, :, j * part : (j + 1) * part] for i in range(outer)], axis=1)
-        for j in range(3)
-    )
+    grad_w_ffn = swap_blocks(grad_w_ffn, "outer")
+    sum_gate, sum_up, sum_down = unpack(grad_w_ffn, part)
     sum_down = sum_down.T
 
     _, pull_three = jax.vjp(rms_scale, resid, norm_ffn_in)
@@ -696,34 +969,23 @@
     grad_input_part, grad_norm_attn_in = pull_one(grad_h_attn)
     input_own = grad_resid + grad_input_part
 
-    layer_output = lax.all_gather(output_own, "tensor", axis=0, tiled=True)
-    input_grad = lax.all_gather(input_own.astype(low), "tensor", axis=0, tiled=True)
     norm_rows = jnp.stack(
         [grad_norm_attn_in, grad_norm_attn_out, grad_norm_ffn_in, grad_norm_ffn_out]
     )
-    norm_all = lax.all_gather(norm_rows, (*dp, "tensor"), axis=0, tiled=False)
-    input_grad = input_grad.astype(jnp.float32)
-    position = lax.axis_index("outer") * inner + lax.axis_index("inner")
-    norm_all = lax.dynamic_slice_in_dim(norm_all, position * shard_rows, shard_rows, 2)
+    strips = norm_rows.reshape(4, outer * inner, shard_rows).transpose(1, 0, 2)
+    strips = strips.reshape(outer * inner, 1, -1).astype(low)
+    attn_cols = attn_shard.shape[1]
+    strips = jnp.pad(strips, ((0, 0), (0, 15), (0, attn_cols - strips.shape[2])))
+    tail = jnp.concatenate([output_own, input_own.astype(low)], axis=0)
+    sum_last, tails = finish(
+        lanes, h_attn.T, grad_attn_branch.T, grad_qkv, mixed_flat, strips, tail, 8
+    )
+    layer_output = tails[:, :split_rows].reshape(row_count, -1)
+    input_grad = tails[:, split_rows:].reshape(row_count, -1).astype(jnp.float32)
     sum_attn_in, sum_attn_out, sum_ffn_in, sum_ffn_out = (
-        item for item in jnp.sum(norm_all, axis=0)
-    )
-
-    grad_w_attn = jnp.concatenate(
-        [
-            left_product(h_attn, grad_qkv).astype(low),
-            left_product(grad_attn_branch, mixed_flat).astype(low),
-        ],
-        axis=1,
-    )
-    sum_last = scatter_sum(
-        grad_w_attn.reshape(outer * inner, shard_rows, -1),
-        lanes,
-        True,
-        ("inner",),
-        ("inner",),
-        8,
-    )
+        sum_last[shard_rows, i * shard_rows : (i + 1) * shard_rows] for i in range(4)
+    )
+    sum_last = sum_last[:shard_rows]
     sum_out = sum_last[:, qkv_cols:].T
     sum_query = sum_last[:, :query_cols]
     sum_key = sum_last[:, query_cols : query_cols + key_cols]

time: 941 us -> 907 us (0.964)
  the two profiles are of different devices: /device:TPU:26 before, /device:TPU:9 now
where the time goes in v2:
time: 907 us; the launch traced here: 897 us
  Pallas kernels  579 us (64%)
  waiting for transfers between devices  82 us (9%)
  matrix products  77.8 us (9%)
  local copies, waits for them, and re-layouts  70.6 us (8%)
  other arithmetic  69.9 us (8%)
  starting transfers between devices  15.7 us (2%)
    pallas_call x4, Pallas kernels, gather_blocks(): pl.pallas_call(functools.partial(gather_kernel, lanes, chain, levels), ou...  268 us
    pallas_call x1, Pallas kernels, finish(): pl.pallas_call(functools.partial(finish_kernel, lanes), out_shape=[jax.Sh...  143 us
    pallas_call x4, Pallas kernels, scatter_sum(): pl.pallas_call(functools.partial(scatter_kernel, lanes, chain, levels, or...  142 us
    ppermute x6, waiting for transfers between devices, swap_blocks(): lax.ppermute(pick(blocks, lax.rem(here + step, size)), axis, [(i, (i + st...  82 us
    dot_general x4, matrix products, right_product(): jnp.einsum('tc,dc->td', left, right, preferred_element_type=jnp.float32)  32.3 us
    dot_general x4, matrix products, matmul(): return jnp.dot(left, right, preferred_element_type=jnp.float32)  30.4 us
    pallas_call x1, Pallas kernels, weight_grads(): pl.pallas_call(weight_grads_kernel, grid=(width // tile,), out_shape=jax....  20.3 us
  transfers between devices with their start and end apart: 8, of which 3 were waited for; matrix products, arithmetic and copies ran while one was open for 10% of the time, Pallas kernels for 43%

profile of v2, /device:TPU:9, one launch (start us, length us, event | category | flops | bytes accessed | tf_op | source)
XLA Modules:
  0.0 896.7 jit_solution(7615381979968679820)
XLA Ops:
  0.7 2.7 fusion.101
  3.4 2.3 fusion.99
  5.7 2.3 concatenate.71
  8.0 2.2 concatenate.68
  10.3 2.4 concatenate.69
  12.7 3.2 concatenate.70
  17.5 2.2 broadcast.202.clone
  34.5 138.1 %shard_map.237 = bf16[8,288,1536]{2,1,0:T(8,128)(2,1)} custom-call(bf16[288,1536]{1,0:T(8,128)(2,1)} %pad_maximum_fusion.2.x_ref), custom_call_target="tpu_custom_call" | custom-call | bytes 70778880 | tf_op jit(solution)/shard_map/pallas_call | solution.py:300
  172.6 2.2 copy.110.h_ref
  179.1 2.2 bitcast_dynamic-update-slice_fusion.7
  181.3 2.3 bitcast_dynamic-update-slice_fusion.6
  183.6 2.3 bitcast_dynamic-update-slice_fusion.5
  185.8 4.4 fusion.7
  196.3 2.4 convolution_convert_fusion.4
  199.7 4.0 convolution_convert_fusion.3
  203.7 18.7 %shard_map.238 = f32[96,2304]{1,0:T(8,128)} custom-call(bf16[4,96,2304]{2,1,0:T(8,128)(2,1)} %bitcast.169), custom_call_target="tpu_custom_call" | custom-call | bytes 17694720 | tf_op jit(solution)/shard_map/pallas_call | solution.py:476
  226.5 66.5 %shard_map.239 = bf16[16,96,2304]{2,1,0:T(8,128)(2,1)} custom-call(bf16[96,2304]{1,0:T(8,128)(2,1)} %multiply_convert_fusion.3.x_ref), custom_call_target="tpu_custom_call" | custom-call | bytes 70778880 | tf_op jit(solution)/shard_map/pallas_call | solution.py:300
  293.1 3.5 fusion.25
  297.1 2.8 bitcast_dynamic-update-slice_fusion.1
  300.0 2.8 bitcast_dynamic-update-slice_fusion
  303.2 9.4 %fusion.4 = f32[1536,1152]{1,0:T(8,128)S(1)} fusion(bf16[1536,2304]{1,0:T(8,128)(2,1)S(1)} %bitcast.149, bf16[2304,1728]{1,0:T(8,128)(2,1)S(1)} %bitcast.142), kind=kOutput, calls=%fused_computation.11 | convolution fusion | flops 8153726976 | bytes 19464192 | tf_op jit(solution)/shard_map/dot_general | solution.py:59
  312.6 12.2 %multiply_convert_fusion.1.hidden_ref = bf16[1536,576]{1,0:T(8,128)(2,1)S(1)} fusion(f32[1536,1152]{1,0:T(8,128)S(1)} %fusion.4), kind=kLoop, calls=%fused_computation.29 | loop fusion | flops 8847360 | bytes 8847360 | tf_op jit(solution)/shard_map/convert_element_type | solution.py:882
  324.8 7.8 convolution_convert_fusion.1
  332.6 51.5 %shard_map.240 = f32[96,2304]{1,0:T(8,128)} custom-call(bf16[16,96,2304]{2,1,0:T(8,128)(2,1)} %bitcast.161), custom_call_target="tpu_custom_call" | custom-call | bytes 70778880 | tf_op jit(solution)/shard_map/pallas_call | solution.py:476
  385.6 3.0 multiply_reduce_fusion.3
  390.8 47.3 %shard_map.241 = bf16[16,96,2304]{2,1,0:T(8,128)(2,1)} custom-call(bf16[96,2304]{1,0:T(8,128)(2,1)} %fusion.43.x_ref), custom_call_target="tpu_custom_call" | custom-call | bytes 70778880 | tf_op jit(solution)/shard_map/pallas_call | solution.py:300
  438.1 13.2 %fusion.12 = (bf16[1536,576]{1,0:T(8,128)(2,1)S(1)}, bf16[1536,576]{1,0:T(8,128)(2,1)S(1)}) fusion(f32[1536,1152]{1,0:T(8,128)} %copy-done.4, bf16[1536,2304]{1,0:T(8,128)(2,1)} %bitcast.150, bf16[2304,1728]{1,0:T(8,128)(2,1)} %bitcast.144), kind=kOutput, calls=%fused_computation.25 | convolution fusion | flops 4101636096 | bytes 21430272 | tf_op jit(solution)/shard_map/dot_general | solution.py:59
  451.4 2.9 pad_maximum_fusion.1.both_ref
  454.3 20.3 %shard_map.246 = bf16[2304,1728]{1,0:T(8,128)(2,1)} custom-call(bf16[1536,2304]{1,0:T(8,128)(2,1)} %bitcast.146, bf16[1536,2304]{1,0:T(8,128)(2,1)} %bitcast.151, bf16[1536,1152]{1,0:T(8,128)(2,1)} %pad_maximum_fusion.1.both_ref, bf16[1536,576]{1,0:T(8,128)(2,1)} %copy-done.9), custom_call_target="tpu_custom_call" | custom-call | flops 12230590464 | bytes 22118400 | tf_op jit(solution)/shard_map/pallas_call | solution.py:514
  474.7 14.5 %convolution_convert_fusion = bf16[1536,2304]{1,0:T(8,128)(2,1)} fusion(bf16[1536,1152]{1,0:T(8,128)(2,1)} %pad_maximum_fusion.1.both_ref, bf16[2304,1728]{1,0:T(8,128)(2,1)} %bitcast.145), kind=kOutput, calls=%fused_computation.2 | convolution fusion | flops 8157265920 | bytes 15925248 | tf_op jit(solution)/shard_map/tc,dc->td/dot_general | solution.py:63
  489.2 55.0 %shard_map.242 = f32[96,2304]{1,0:T(8,128)} custom-call(bf16[16,96,2304]{2,1,0:T(8,128)(2,1)} %bitcast.160), custom_call_target="tpu_custom_call" | custom-call | bytes 70778880 | tf_op jit(solution)/shard_map/pallas_call | solution.py:476
  546.2 2.4 multiply_reduce_fusion.5
  550.6 15.7 %shard_map.243 = bf16[4,96,2304]{2,1,0:T(8,128)(2,1)} custom-call(bf16[96,2304]{1,0:T(8,128)(2,1)} %fusion.45.x_ref), custom_call_target="tpu_custom_call" | custom-call | bytes 17694720 | tf_op jit(solution)/shard_map/pallas_call | solution.py:300
  566.3 3.4 fusion.30
  570.7 2.3 fusion.74
  573.0 3.0 fusion.40
  576.0 3.7 fusion.37
  579.8 4.4 dynamic-slice_bitcast_fusion
  590.7 3.3 fusion.34
  594.1 6.0 convolution_convert_fusion.2
  600.1 16.5 %shard_map.244 = f32[96,2304]{1,0:T(8,128)} custom-call(bf16[4,96,2304]{2,1,0:T(8,128)(2,1)} %bitcast.170), custom_call_target="tpu_custom_call" | custom-call | bytes 17694720 | tf_op jit(solution)/shard_map/pallas_call | solution.py:476
  634.2 142.6 %shard_map.245 = (f32[304,1536]{1,0:T(8,128)}, bf16[4,192,2304]{2,1,0:T(8,128)(2,1)}) custom-call(bf16[2304,384]{1,0:T(8,128)(2,1)} %copy.110.h_ref, bf16[2304,384]{1,0:T(8,128)(2,1)} %bitcast.168, bf16[384,1024]{1,0:T(8,128)(2,1)} %pad_maximum_fusion.4.qkv_ref, bf16[384,512]{1,0:T(8,128)(2,1)} %copy.126.mixed_ref, bf16[8,16,1536]{2,1,0:T(8,128)(2,1)} %pad.4.strip_ref, ...), custom_call_target="tpu_custom_call" | custom-call | flops 2717908992 | bytes 70778880 | tf_op jit(solution)/shard_map/pallas_call | solution.py:752
  776.9 3.5 fusion.97
  780.3 4.4 fusion.2
  788.2 9.3 %collective-permute-start.5 = (bf16[288,1728]{1,0:T(8,128)(2,1)S(1)}, bf16[288,1728]{1,0:T(8,128)(2,1)S(1)}, u32[]{:S(2)}, u32[]{:S(2)}) collective-permute-start(bf16[288,1728]{1,0:T(8,128)(2,1)S(1)} %get-tuple-element.48), channel_id=1, source_target_pairs={{0,8},{8,16},{16,24},{24,0},{1,9},{9,17},{17,25},{25,1},{2,10},{10... | collective-permute-start | bytes 2985992 | tf_op jit(solution)/shard_map/ppermute | solution.py:82
  804.6 59.6 %collective-permute-done.5 = bf16[288,1728]{1,0:T(8,128)(2,1)S(1)} collective-permute-done((bf16[288,1728]{1,0:T(8,128)(2,1)S(1)}, bf16[288,1728]{1,0:T(8,128)(2,1)S(1)}, u32[]{:S(2)}, u32[]{:S(2)}) %collective-permute-start.5) | collective-permute-done | bytes 995360 | tf_op jit(solution)/shard_map/ppermute | solution.py:82
  865.3 21.1 %collective-permute-done.6 = bf16[288,1728]{1,0:T(8,128)(2,1)S(1)} collective-permute-done((bf16[288,1728]{1,0:T(8,128)(2,1)S(1)}, bf16[288,1728]{1,0:T(8,128)(2,1)S(1)}, u32[]{:S(2)}, u32[]{:S(2)}) %collective-permute-start.6) | collective-permute-done | bytes 995360 | tf_op jit(solution)/shard_map/ppermute | solution.py:82
  889.7 6.6 shard_map.247
  (163 shorter events, 80.3 us)
Async XLA Ops:
  0.6 2.8 copy-start.14
  0.7 2.8 copy-start.15
  19.7 5.8 copy-start.1
  19.7 6.3 copy-start.36
  19.7 7.1 copy-start.30
  21.8 157.3 %collective-permute-start = (bf16[288,1728]{1,0:T(8,128)(2,1)}, bf16[288,1728]{1,0:T(8,128)(2,1)}, u32[]{:S(2)}, u32[]{:S(2)}) collective-permute-start(bf16[288,1728]{1,0:T(8,128)(2,1)} %get-tuple-element.52), channel_id=1, source_target_pairs={{0,8},{8,16},{16,24},{24,0},{1,9},{9,17},{17,25},{25,1},{2,10},{10... | collective-permute-start | bytes 2985992 | tf_op jit(solution)/shard_map/ppermute | solution.py:82
  23.1 158.3 %collective-permute-start.1 = (bf16[288,1728]{1,0:T(8,128)(2,1)}, bf16[288,1728]{1,0:T(8,128)(2,1)}, u32[]{:S(2)}, u32[]{:S(2)}) collective-permute-start(bf16[288,1728]{1,0:T(8,128)(2,1)} %get-tuple-element.51), channel_id=1, source_target_pairs={{0,16},{8,24},{16,0},{24,8},{1,17},{9,25},{17,1},{25,9},{2,18},{10... | collective-permute-start | bytes 2985992 | tf_op jit(solution)/shard_map/ppermute | solution.py:82
  24.1 159.5 %collective-permute-start.2 = (bf16[288,1728]{1,0:T(8,128)(2,1)}, bf16[288,1728]{1,0:T(8,128)(2,1)}, u32[]{:S(2)}, u32[]{:S(2)}) collective-permute-start(bf16[288,1728]{1,0:T(8,128)(2,1)} %get-tuple-element.50), channel_id=1, source_target_pairs={{0,24},{8,0},{16,8},{24,16},{1,25},{9,1},{17,9},{25,17},{2,26},{10... | collective-permute-start | bytes 2985992 | tf_op jit(solution)/shard_map/ppermute | solution.py:82
  26.0 1.4 copy-start.33
  190.2 4.1 copy-start.8
  190.2 3.3 copy-start.11
  191.1 108.9 %collective-permute-start.3 = (bf16[4,288,1728]{2,1,0:T(8,128)(2,1)}, bf16[4,288,1728]{2,1,0:T(8,128)(2,1)}, u32[]{:S(2)}, u32[]{:S(2)}) collective-permute-start(bf16[4,288,1728]{2,1,0:T(8,128)(2,1)} %bitcast_dynamic-update-slice_fusion.5), channel_id=1, source_target_pairs={{0,4},{4,0},{1,5},{5,1},{2,6},{6,2},{3,7},{7,3},{8,12},{12,8},{9,1... | collective-permute-start | bytes 11943944 | tf_op jit(solution)/shard_map/ppermute | solution.py:98
  194.4 1.6 copy-start.25
  196.0 7.7 copy-start.18
  196.3 7.4 copy-start.23
  199.7 24.1 %copy-start.29 = (f32[2304]{0:T(1024)S(1)}, f32[2304]{0:T(1024)}, u32[]{:S(2)}) copy-start(f32[2304]{0:T(1024)} %param.22) | copy-start | bytes 27652
  203.7 21.9 %copy-start.28 = (f32[2304]{0:T(1024)S(1)}, f32[2304]{0:T(1024)}, u32[]{:S(2)}) copy-start(f32[2304]{0:T(1024)} %param.23) | copy-start | bytes 27652
  225.5 67.5 %copy-start.35 = (f32[96]{0:T(128)}, f32[96]{0:T(128)S(1)}, u32[]{:S(2)}) copy-start(f32[96]{0:T(128)S(1)} %get-tuple-element.56) | copy-start | bytes 1156
  226.5 66.6 %copy-start.27 = (pred[384,384]{0,1:T(8,128)(4,1)S(1)}, pred[384,384]{0,1:T(8,128)(4,1)}, u32[]{:S(2)}) copy-start(pred[384,384]{0,1:T(8,128)(4,1)} %fusion.59) | copy-start | bytes 442372
  297.1 5.7 slice-start
  300.0 3.2 slice-start.1
  302.8 22.0 %copy-start.5 = (bf16[2,4,288,1728]{3,2,0,1:T(8,128)(2,1)}, bf16[2,4,288,1728]{3,2,0,1:T(8,128)(2,1)S(1)}, u32[]{:S(2)}) copy-start(bf16[2,4,288,1728]{3,2,0,1:T(8,128)(2,1)S(1)} %bitcast_dynamic-update-slice_fusion) | copy-start | bytes 23887876
  312.6 12.2 %copy-start.4 = (f32[1536,1152]{1,0:T(8,128)}, f32[1536,1152]{1,0:T(8,128)S(1)}, u32[]{:S(2)}) copy-start(f32[1536,1152]{1,0:T(8,128)S(1)} %fusion.4) | copy-start | bytes 21233668
  324.8 7.8 copy-start.9
  332.6 53.0 %copy-start.32 = (f32[2304]{0:T(1024)S(1)}, f32[2304]{0:T(1024)}, u32[]{:S(2)}) copy-start(f32[2304]{0:T(1024)} %param.27) | copy-start | bytes 27652
  332.6 53.0 %copy-start.34 = (f32[96]{0:T(128)S(1)}, f32[96]{0:T(128)}, u32[]{:S(2)}) copy-start(f32[96]{0:T(128)} %dynamic-slice.9) | copy-start | bytes 1156
  384.2 4.5 copy-start.2
  489.2 57.0 %copy-start = (f32[96,2304]{1,0:T(8,128)S(1)}, f32[96,2304]{1,0:T(8,128)}, u32[]{:S(2)}) copy-start(f32[96,2304]{1,0:T(8,128)} %shard_map.238) | copy-start | bytes 2654212
  548.6 1.0 copy-start.6
  566.3 6.7 copy-start.24
  566.3 6.7 copy-start.26
  569.7 6.3 copy-start.19
  569.9 0.7 copy-start.20
  584.1 1.0 copy-start.16
  584.1 1.8 copy-start.7
  584.1 196.2 %collective-permute-start.4 = (bf16[4,288,1728]{2,1,0:T(8,128)(2,1)}, bf16[4,288,1728]{2,1,0:T(8,128)(2,1)}, u32[]{:S(2)}, u32[]{:S(2)}) collective-permute-start(bf16[4,288,1728]{2,1,0:T(8,128)(2,1)} %dynamic-slice_bitcast_fusion), channel_id=1, source_target_pairs={{0,4},{4,0},{1,5},{5,1},{2,6},{6,2},{3,7},{7,3},{8,12},{12,8},{9,1... | collective-permute-start | bytes 11943944 | tf_op jit(solution)/shard_map/ppermute | solution.py:110
  585.1 3.0 copy-start.22
  585.1 3.9 copy-start.12
  585.1 3.9 copy-start.17
  585.1 5.6 copy-start.21
  594.1 22.5 %copy-start.3 = (f32[384,2304]{1,0:T(8,128)S(1)}, f32[384,2304]{1,0:T(8,128)}, u32[]{:S(2)}) copy-start(f32[384,2304]{1,0:T(8,128)} %convert_element_type.132) | copy-start | bytes 10616836
  594.1 22.6 %copy-start.31 = (f32[2304]{0:T(1024)S(1)}, f32[2304]{0:T(1024)}, u32[]{:S(2)}) copy-start(f32[2304]{0:T(1024)} %param.17) | copy-start | bytes 27652
  627.0 6.2 copy-start.10
  788.2 11.4 %copy-start.13 = (f32[304,1536]{1,0:T(8,128)S(1)}, f32[304,1536]{1,0:T(8,128)}, u32[]{:S(2)}) copy-start(f32[304,1536]{1,0:T(8,128)} %get-tuple-element.23) | copy-start | bytes 5603332
  788.2 76.0 %collective-permute-start.5 = (bf16[288,1728]{1,0:T(8,128)(2,1)S(1)}, bf16[288,1728]{1,0:T(8,128)(2,1)S(1)}, u32[]{:S(2)}, u32[]{:S(2)}) collective-permute-start(bf16[288,1728]{1,0:T(8,128)(2,1)S(1)} %get-tuple-element.48), channel_id=1, source_target_pairs={{0,8},{8,16},{16,24},{24,0},{1,9},{9,17},{17,25},{25,1},{2,10},{10... | collective-permute-start | bytes 2985992 | tf_op jit(solution)/shard_map/ppermute | solution.py:82
  800.3 86.1 %collective-permute-start.6 = (bf16[288,1728]{1,0:T(8,128)(2,1)S(1)}, bf16[288,1728]{1,0:T(8,128)(2,1)S(1)}, u32[]{:S(2)}, u32[]{:S(2)}) collective-permute-start(bf16[288,1728]{1,0:T(8,128)(2,1)S(1)} %get-tuple-element.47), channel_id=1, source_target_pairs={{0,16},{8,24},{16,0},{24,8},{1,17},{9,25},{17,1},{25,9},{2,18},{10... | collective-permute-start | bytes 2985992 | tf_op jit(solution)/shard_map/ppermute | solution.py:82
  803.7 85.0 %collective-permute-start.7 = (bf16[288,1728]{1,0:T(8,128)(2,1)S(1)}, bf16[288,1728]{1,0:T(8,128)(2,1)S(1)}, u32[]{:S(2)}, u32[]{:S(2)}) collective-permute-start(bf16[288,1728]{1,0:T(8,128)(2,1)S(1)} %get-tuple-element.46), channel_id=1, source_target_pairs={{0,24},{8,0},{16,8},{24,16},{1,25},{9,1},{17,9},{25,17},{2,26},{10... | collective-permute-start | bytes 2985992 | tf_op jit(solution)/shard_map/ppermute | solution.py:82

commit v3 on v2

--- a/solution.py
+++ b/solution.py
@@ -68,52 +68,41 @@
     return SOFT_CAP * jnp.tanh(raw_scores / SOFT_CAP)
 
 
-def pick(blocks, index):
-    return lax.dynamic_index_in_dim(blocks, index, 0, keepdims=False)
-
-
-def swap_blocks(blocks, axis):
-    size = blocks.shape[0]
-    here = lax.axis_index(axis)
-    result = lax.dynamic_update_index_in_dim(
-        jnp.zeros_like(blocks), pick(blocks, here), here, 0
-    )
-    for step in range(1, size):
-        came = lax.ppermute(
-            pick(blocks, lax.rem(here + step, size)),
-            axis,
-            [(i, (i + step) % size) for i in range(size)],
-        )
-        result = lax.dynamic_update_index_in_dim(
-            result, came, lax.rem(here - step + size, size), 0
-        )
-    return result
-
-
-def collect(block, axis, size):
-    here = lax.axis_index(axis)
-    result = jnp.zeros((size,) + block.shape, block.dtype)
-    result = lax.dynamic_update_index_in_dim(result, block, here, 0)
-    for step in range(1, size):
-        came = lax.ppermute(block, axis, [(i, (i + step) % size) for i in range(size)])
-        result = lax.dynamic_update_index_in_dim(
-            result, came, lax.rem(here - step + size, size), 0
-        )
-    return result
-
-
-def sum_blocks(blocks, axis):
-    size = blocks.shape[0]
-    here = lax.axis_index(axis)
-    total = pick(blocks, here).astype(jnp.float32)
-    for step in range(1, size):
-        came = lax.ppermute(
-            pick(blocks, lax.rem(here + step, size)),
-            axis,
-            [(i, (i + step) % size) for i in range(size)],
-        )
-        total = total + came.astype(jnp.float32)
-    return total
+def shifted(block, axis, size, step):
+    return lax.ppermute(block, axis, [(i, (i + step) % size) for i in range(size)])
+
+
+def pack_kernel(part, g_ref, u_ref, d_ref, *o_refs):
+    count = len(o_refs)
+    here = lax.axis_index("outer")
+    tile = math.gcd(g_ref.shape[0], 16)
+    for step, o_ref in enumerate(o_refs):
+        for source in range(count):
+
+            @pl.when(lax.rem(here + step, count) == source)
+            def _(o_ref=o_ref, source=source):
+                def body(r, carry):
+                    window = pl.ds(pl.multiple_of(r * tile, tile), tile)
+                    for j, ref in enumerate((g_ref, u_ref, d_ref)):
+                        o_ref[window, j * part : (j + 1) * part] = ref[
+                            window, source * part : (source + 1) * part
+                        ]
+                    return carry
+
+                lax.fori_loop(0, g_ref.shape[0] // tile, body, 0)
+
+
+def pack(count, part, gate, up, down_turned):
+    vmem = pl.BlockSpec(memory_space=pltpu.VMEM)
+    return pl.pallas_call(
+        functools.partial(pack_kernel, part),
+        out_shape=[jax.ShapeDtypeStruct((gate.shape[0], 3 * part), gate.dtype)] * count,
+        in_specs=[vmem] * 3,
+        out_specs=[vmem] * count,
+        cost_estimate=pl.CostEstimate(
+            flops=0, bytes_accessed=12 * gate.size, transcendentals=0
+        ),
+    )(gate, up, down_turned)
 
 
 def device_layout(lanes):
@@ -195,7 +184,12 @@
     return first if second is None else jnp.logical_and(first, second)
 
 
-def gather_kernel(lanes, chain, levels, x_ref, o_ref, send_sem, recv_sem, local_sem):
+def gather_kernel(lanes, chain, levels, places, *refs):
+    held_refs, refs = refs[1 : 1 + len(places)], refs[:1] + refs[1 + len(places) :]
+    if places:
+        x_ref, o_ref, placed_ref, send_sem, recv_sem, local_sem, place_sem = refs
+    else:
+        x_ref, o_ref, send_sem, recv_sem, local_sem = refs
     spot = Spot(lanes, chain, levels)
     length, step, here = spot.length, spot.step, spot.here
     started = []
@@ -254,6 +248,18 @@
         send(step < length - 1, x_ref, mine, 1, spot.device(here, 1))
         send(step > 0, x_ref, mine, 0, spot.device(here, -1))
     spread(None, x_ref, mine, 0)
+
+    outer, inner, _ = lanes
+    moves = []
+    for number, (back, turn) in enumerate(places):
+        index = lax.rem(lax.axis_index("outer") - back + outer, outer) * inner
+        index = index + lax.rem(lax.axis_index("inner") - turn + inner, inner)
+        moves.append(
+            pltpu.make_async_copy(
+                held_refs[number], placed_ref.at[index], place_sem.at[number]
+            )
+        )
+        moves[-1].start()
 
     def relay(distance):
         if len(levels) < 2:
@@ -290,28 +296,41 @@
                 arrive(None, spot.flat(position, spot.moved(**{**rest, last: shift})))
     for condition, copy in started:
         guarded(condition, lambda copy=copy: copy().wait_send())
+    for move in moves:
+        move.wait()
     local.wait()
 
 
-def gather_blocks(block, lanes, chain, levels, collective_id):
+def gather_blocks(block, lanes, chain, levels, collective_id, held=None):
+    held = held or {}
+    places = tuple(held)
+    blocks = [held[key] for key in places]
     sizes = device_layout(lanes)
     count = (lanes[0] if chain else 1) * math.prod(sizes[level] for level in levels)
     slots = 2 + sum(sizes[level] - 1 for level in levels)
-    return pl.pallas_call(
-        functools.partial(gather_kernel, lanes, chain, levels),
-        out_shape=jax.ShapeDtypeStruct((count,) + block.shape, block.dtype),
-        in_specs=[pl.BlockSpec(memory_space=pltpu.VMEM)],
-        out_specs=pl.BlockSpec(memory_space=pl.ANY),
-        scratch_shapes=[
-            pltpu.SemaphoreType.DMA((slots, count)),
-            pltpu.SemaphoreType.DMA((count,)),
-            pltpu.SemaphoreType.DMA,
-        ],
+    out_shape = [jax.ShapeDtypeStruct((count,) + block.shape, block.dtype)]
+    scratch = [
+        pltpu.SemaphoreType.DMA((slots, count)),
+        pltpu.SemaphoreType.DMA((count,)),
+        pltpu.SemaphoreType.DMA,
+    ]
+    if held:
+        out_shape.append(
+            jax.ShapeDtypeStruct((lanes[0] * lanes[1],) + blocks[0].shape, blocks[0].dtype)
+        )
+        scratch.append(pltpu.SemaphoreType.DMA((len(blocks),)))
+    results = pl.pallas_call(
+        functools.partial(gather_kernel, lanes, chain, levels, places),
+        out_shape=out_shape,
+        in_specs=[pl.BlockSpec(memory_space=pltpu.VMEM)] * (1 + len(blocks)),
+        out_specs=[pl.BlockSpec(memory_space=pl.ANY)] * len(out_shape),
+        scratch_shapes=scratch,
         compiler_params=pltpu.CompilerParams(collective_id=collective_id, has_side_effects=True),
         cost_estimate=pl.CostEstimate(
             flops=0, bytes_accessed=20 * count * block.size, transcendentals=0
         ),
-    )(block)
+    )(block, *blocks)
+    return results if held else results[0]
 
 
 def add_into(target, parts, condition=None):
@@ -530,24 +549,33 @@
     )(h_all, g_all, both, hidden)
 
 
-def unpack_kernel(part, x_ref, gate_ref, up_ref, down_ref):
-    for i in range(x_ref.shape[0]):
-        columns = slice(i * part, (i + 1) * part)
-        for j, target in enumerate((gate_ref, up_ref, down_ref)):
-            target[:, columns] = x_ref[i, :, j * part : (j + 1) * part].astype(jnp.float32)
+def unpack_kernel(part, *refs):
+    blocks, targets = refs[:-3], refs[-3:]
+    count = len(blocks)
+    here = lax.axis_index("outer")
+    for step, x_ref in enumerate(blocks):
+        for source in range(count):
+
+            @pl.when(lax.rem(here - step + count, count) == source)
+            def _(x_ref=x_ref, source=source):
+                for j, target in enumerate(targets):
+                    target[:, source * part : (source + 1) * part] = x_ref[
+                        :, j * part : (j + 1) * part
+                    ].astype(jnp.float32)
 
 
 def unpack(blocks, part):
-    count, rows, columns = blocks.shape
+    count = len(blocks)
+    rows, columns = blocks[0].shape
     tile = math.gcd(rows, 48)
     width = count * part
     return pl.pallas_call(
         functools.partial(unpack_kernel, part),
         grid=(rows // tile,),
         out_shape=[jax.ShapeDtypeStruct((rows, width), jnp.float32)] * 3,
-        in_specs=[pl.BlockSpec((count, tile, columns), lambda i: (0, i, 0))],
+        in_specs=[pl.BlockSpec((tile, columns), lambda i: (i, 0))] * count,
         out_specs=[pl.BlockSpec((tile, width), lambda i: (i, 0))] * 3,
-    )(blocks)
+    )(*blocks)
 
 
 def finish_kernel(
@@ -606,10 +634,15 @@
             device_id_type=MESH,
         )
 
-    upper = (step * 2 >= outer).astype(jnp.int32)
+    orders = [sorted(range(outer), key=lambda p, at=at: -abs(p - at)) for at in range(outer)]
 
     def place(j):
-        return upper * j + (1 - upper) * (outer - 1 - j)
+        position = 0
+        for at in range(outer):
+            for number in range(outer):
+                chosen = (step == at).astype(jnp.int32) * (j == number).astype(jnp.int32)
+                position = position + chosen * orders[at][number]
+        return position
 
     def row_copy(k):
         shift = 1 + lax.div(k, outer)
@@ -810,19 +843,25 @@
     attn_shard = jnp.concatenate([w_query, w_key, w_value, w_out.T], axis=1)
     attn_full = gather_blocks(attn_shard, lanes, True, ("inner",), 0)
     attn_full = attn_full.reshape(-1, attn_shard.shape[1])
-    down_turned = w_down.T
-    ffn_shard = jnp.stack(
-        [
-            jnp.concatenate(
-                [item[:, i * part : (i + 1) * part] for item in (w_gate, w_up, down_turned)],
-                axis=1,
-            )
-            for i in range(outer)
-        ]
-    )
-    ffn_mine = swap_blocks(ffn_shard, "outer")
-    attn_full, ffn_mine = lax.optimization_barrier((attn_full, ffn_mine))
-    ffn_full = collect(ffn_mine, "inner", inner).transpose(1, 0, 2, 3).reshape(-1, 3 * part)
+    ffn_parts = pack(outer, part, w_gate, w_up, w_down.T)
+    early = [step for step in range(1, outer) if step % 2 == 1]
+    late = [step for step in range(1, outer) if step % 2 == 0]
+    across = {0: ffn_parts[0]}
+    for step in early:
+        across[step] = shifted(ffn_parts[step], "outer", outer, step)
+    beside = {(0, turn): shifted(across[0], "inner", inner, turn) for turn in range(1, inner)}
+    held = {step: ffn_parts[step] for step in late}
+    attn_full, across, held = lax.optimization_barrier((attn_full, across, held))
+    for step in late:
+        across[step] = shifted(held[step], "outer", outer, step)
+    for step in early:
+        for turn in range(1, inner):
+            beside[step, turn] = shifted(across[step], "inner", inner, turn)
+    for step in late:
+        for turn in range(1, inner):
+            beside[step, turn] = shifted(across[step], "inner", inner, turn)
+    for step in range(outer):
+        beside[step, 0] = across[step]
 
     row_count = layer_input.shape[0]
     split_rows = row_count // tensor
@@ -875,7 +914,21 @@
     resid = layer_own + rms_scale(attn_branch, norm_attn_out)
     h_ffn = rms_scale(resid, norm_ffn_in).astype(low)
 
-    h_all = gather_blocks(h_ffn, lanes, True, ("x", "core"), 2).reshape(-1, h_ffn.shape[1])
+    last = [(step, turn) for step in late for turn in range(1, inner)]
+    h_all, ffn_full = gather_blocks(
+        h_ffn,
+        lanes,
+        True,
+        ("x", "core"),
+        2,
+        {key: item for key, item in beside.items() if key not in last},
+    )
+    h_all = h_all.reshape(-1, h_ffn.shape[1])
+    for step, turn in last:
+        place = lax.rem(lax.axis_index("outer") - step + outer, outer) * inner
+        place = place + lax.rem(lax.axis_index("inner") - turn + inner, inner)
+        ffn_full = lax.dynamic_update_slice(ffn_full, beside[step, turn][None], (place, 0, 0))
+    ffn_full = ffn_full.reshape(-1, 3 * part)
     gate_up = matmul(h_all, ffn_full[:, : 2 * part])
     gate_pre, up_pre = gate_up[:, :part], gate_up[:, part:]
     gelu_gate = gelu_tanh(gate_pre)
@@ -913,20 +966,58 @@
         5,
     )
     grad_w_ffn = weight_grads(h_all, grad_ffn_all, grad_both, hidden)
-    grad_w_ffn = grad_w_ffn.reshape(outer, inner, shard_rows, 3 * part).transpose(1, 0, 2, 3)
-    grad_w_ffn = sum_blocks(grad_w_ffn, "inner").astype(low)
-    grad_w_ffn = swap_blocks(grad_w_ffn, "outer")
-    sum_gate, sum_up, sum_down = unpack(grad_w_ffn, part)
-    sum_down = sum_down.T
+    grad_w_ffn = grad_w_ffn.reshape(outer, inner, shard_rows, 3 * part)
+    here, row = lax.axis_index("outer"), lax.axis_index("inner")
+
+    def grad_block(step, turn):
+        place = (lax.rem(here + step, outer), lax.rem(row + turn, inner), 0, 0)
+        return lax.dynamic_slice(grad_w_ffn, place, (1, 1, shard_rows, 3 * part))[0, 0]
+
+    half = max(outer // 2, 1)
+    groups_of_steps = (range(1, 1 + half), [*range(1 + half, outer), 0])
+    outgoing = [
+        {(step, turn): grad_block(step, turn) for step in steps for turn in range(1, inner)}
+        for steps in groups_of_steps
+    ]
+    grad_h_ffn, outgoing[1] = lax.optimization_barrier((grad_h_ffn, outgoing[1]))
+
+    def start_rows(number):
+        return {
+            key: shifted(item, "inner", inner, key[1]) for key, item in outgoing[number].items()
+        }
+
+    def sum_rows(number, came):
+        summed = {}
+        for step in groups_of_steps[number]:
+            total = grad_block(step, 0).astype(jnp.float32)
+            for turn in range(1, inner):
+                total = total + came[step, turn].astype(jnp.float32)
+            summed[step] = total.astype(low)
+        return summed
+
+    def send_rows(summed):
+        return {
+            step: shifted(item, "outer", outer, step) if step else item
+            for step, item in summed.items()
+        }
+
+    rows_now = sum_rows(0, start_rows(0))
+    rows_later = start_rows(1)
 
     _, pull_three = jax.vjp(rms_scale, resid, norm_ffn_in)
     grad_resid_part, grad_norm_ffn_in = pull_three(grad_h_ffn)
     grad_resid = grad_out + grad_resid_part
     _, pull_two = jax.vjp(rms_scale, attn_branch, norm_attn_out)
     grad_attn_float, grad_norm_attn_out = pull_two(grad_resid)
+    grad_attn_own, rows_now = lax.optimization_barrier((grad_attn_float.astype(low), rows_now))
+    summed = send_rows(rows_now)
     grad_attn_branch = gather_blocks(
-        grad_attn_float.astype(low), lanes, False, ("x", "core"), 6
+        grad_attn_own, lanes, False, ("x", "core"), 6
     ).reshape(row_count, -1)
+    grad_attn_branch, rows_later = lax.optimization_barrier((grad_attn_branch, rows_later))
+    summed.update(send_rows(sum_rows(1, rows_later)))
+    sum_gate, sum_up, sum_down = unpack([summed[step] for step in range(outer)], part)
+    sum_down = sum_down.T
     grad_mixed = matmul(grad_attn_branch, out_turned).astype(low)
     grad_mixed = grad_mixed.reshape(row_count, kv_heads, groups, HD).transpose(1, 2, 0, 3)
     grad_values = jnp.einsum(

time: 907 us -> 761 us (0.84)
  the two profiles are of different devices: /device:TPU:9 before, /device:TPU:0 now
where the time goes in v3:
time: 761 us; the launch traced here: 751 us
  Pallas kernels  511 us (67%)
  matrix products  84.1 us (11%)
  waiting for transfers between devices  63.3 us (8%)
  other arithmetic  48.3 us (6%)
  local copies, waits for them, and re-layouts  25.9 us (3%)
  starting transfers between devices  17.4 us (2%)
    pallas_call x4, Pallas kernels, gather_blocks(): pl.pallas_call(functools.partial(gather_kernel, lanes, chain, levels, pla...  229 us
    pallas_call x4, Pallas kernels, scatter_sum(): pl.pallas_call(functools.partial(scatter_kernel, lanes, chain, levels, or...  138 us
    pallas_call x1, Pallas kernels, finish(): pl.pallas_call(functools.partial(finish_kernel, lanes), out_shape=[jax.Sh...  106 us
    ppermute x14, waiting for transfers between devices, shifted(): lax.ppermute(block, axis, [(i, (i + step) % size) for i in range(size)])  63.3 us
    dot_general x4, matrix products, right_product(): jnp.einsum('tc,dc->td', left, right, preferred_element_type=jnp.float32)  34.8 us
    dot_general x4, matrix products, matmul(): return jnp.dot(left, right, preferred_element_type=jnp.float32)  34.2 us
    pallas_call x1, Pallas kernels, weight_grads(): pl.pallas_call(weight_grads_kernel, grid=(width // tile,), out_shape=jax....  20.4 us
    ppermute x14, starting transfers between devices, shifted(): lax.ppermute(block, axis, [(i, (i + step) % size) for i in range(size)])  17.4 us
  transfers between devices with their start and end apart: 14, of which 4 were waited for; matrix products, arithmetic and copies ran while one was open for 8% of the time, Pallas kernels for 49%

profile of v3, /device:TPU:0, one launch (start us, length us, event | category | flops | bytes accessed | tf_op | source)
XLA Modules:
  0.0 751.4 jit_solution(17457580680414941499)
XLA Ops:
  0.7 10.0 %shard_map.238 = (bf16[288,1728]{1,0:T(8,128)(2,1)}, bf16[288,1728]{1,0:T(8,128)(2,1)}, bf16[288,1728]{1,0:T(8,128)(2,1)}, bf16[288,1728]{1,0:T(8,128)(2,1)}) custom-call(bf16[288,2304]{1,0:T(8,128)(2,1)} %g_ref.1, bf16[288,2304]{1,0:T(8,128)(2,1)} %u_ref.1, bf16[288,2304]{1,0:T(8,128)(2,1)} %bitcast.141), custom_call_target="tpu_custom_call" | custom-call | bytes 7962624 | tf_op jit(solution)/shard_map/pallas_call | solution.py:97
  10.6 3.1 collective-permute-start
  13.7 2.0 collective-permute-start.1
  15.7 1.7 collective-permute-start.2
  17.9 2.0 convert_element_type.168
  20.9 120.0 %shard_map.237 = bf16[8,288,1536]{2,1,0:T(8,128)(2,1)} custom-call(bf16[288,1536]{1,0:T(8,128)(2,1)} %pad_maximum_fusion.1.refs_0_), custom_call_target="tpu_custom_call" | custom-call | bytes 70778880 | tf_op jit(solution)/shard_map/pallas_call | solution.py:322
  142.2 2.2 copy.105.h_ref
  148.2 4.5 fusion.6
  157.7 2.5 convolution_convert_fusion.4
  160.2 4.1 convolution_convert_fusion.3
  164.4 17.1 %shard_map.239 = f32[96,2304]{1,0:T(8,128)} custom-call(bf16[4,96,2304]{2,1,0:T(8,128)(2,1)} %bitcast.136), custom_call_target="tpu_custom_call" | custom-call | bytes 17694720 | tf_op jit(solution)/shard_map/pallas_call | solution.py:495
  187.5 39.1 %collective-permute-done.5.refs_6_ = bf16[288,1728]{1,0:T(8,128)(2,1)} collective-permute-done((bf16[288,1728]{1,0:T(8,128)(2,1)}, bf16[288,1728]{1,0:T(8,128)(2,1)}, u32[]{:S(2)}, u32[]{:S(2)}) %collective-permute-start.5) | collective-permute-done | bytes 995360 | tf_op jit(solution)/shard_map/ppermute | solution.py:72
  227.1 3.3 fusion.28
  232.0 47.0 %shard_map.240 = (bf16[16,96,2304]{2,1,0:T(8,128)(2,1)}, bf16[8,288,1728]{2,1,0:T(8,128)(2,1)}) custom-call(bf16[96,2304]{1,0:T(8,128)(2,1)} %multiply_convert_fusion.3.refs_0_, bf16[288,1728]{1,0:T(8,128)(2,1)} %collective-permute-done.2.refs_1_, bf16[288,1728]{1,0:T(8,128)(2,1)} %collective-permute-done.3.refs_2_, ...), custom_call_target="tpu_custom_call" | custom-call | bytes 70778880 | tf_op jit(solution)/shard_map/pallas_call | solution.py:322
  279.1 2.3 bitcast_dynamic-update-slice_fusion
  281.3 13.1 %fusion.3 = f32[1536,1152]{1,0:T(8,128)S(1)} fusion(bf16[1536,2304]{1,0:T(8,128)(2,1)} %bitcast.152, bf16[2304,1728]{1,0:T(8,128)(2,1)} %bitcast.148), kind=kOutput, calls=%fused_computation.9 | convolution fusion | flops 8153726976 | bytes 19464192 | tf_op jit(solution)/shard_map/dot_general | solution.py:59
  297.3 10.3 %convolution_convert_fusion.1 = bf16[1536,2304]{1,0:T(8,128)(2,1)} fusion(bf16[1536,576]{1,0:T(8,128)(2,1)S(1)} %multiply_convert_fusion.1.hidden_ref, bf16[2304,1728]{1,0:T(8,128)(2,1)} %bitcast.149), kind=kOutput, calls=%fused_computation.3 | convolution fusion | flops 4080402432 | bytes 11796480 | tf_op jit(solution)/shard_map/tc,dc->td/dot_general | solution.py:63
  307.7 52.5 %shard_map.241 = f32[96,2304]{1,0:T(8,128)} custom-call(bf16[16,96,2304]{2,1,0:T(8,128)(2,1)} %bitcast.131), custom_call_target="tpu_custom_call" | custom-call | bytes 70778880 | tf_op jit(solution)/shard_map/pallas_call | solution.py:495
  361.6 2.5 multiply_reduce_fusion.3
  364.2 2.1 fusion.46.refs_0_
  366.3 48.1 %shard_map.242 = bf16[16,96,2304]{2,1,0:T(8,128)(2,1)} custom-call(bf16[96,2304]{1,0:T(8,128)(2,1)} %fusion.46.refs_0_), custom_call_target="tpu_custom_call" | custom-call | bytes 70778880 | tf_op jit(solution)/shard_map/pallas_call | solution.py:322
  414.4 13.2 %fusion.11 = (bf16[1536,576]{1,0:T(8,128)(2,1)S(1)}, bf16[1536,576]{1,0:T(8,128)(2,1)S(1)}) fusion(f32[1536,1152]{1,0:T(8,128)} %copy-done.4, bf16[1536,2304]{1,0:T(8,128)(2,1)} %bitcast.120, bf16[2304,1728]{1,0:T(8,128)(2,1)} %bitcast.150), kind=kOutput, calls=%fused_computation.19 | convolution fusion | flops 4101636096 | bytes 21430272 | tf_op jit(solution)/shard_map/dot_general | solution.py:59
  427.6 2.9 pad_maximum_fusion.both_ref
  430.5 20.4 %shard_map.244 = bf16[2304,1728]{1,0:T(8,128)(2,1)} custom-call(bf16[1536,2304]{1,0:T(8,128)(2,1)} %bitcast.153, bf16[1536,2304]{1,0:T(8,128)(2,1)} %bitcast.121, bf16[1536,1152]{1,0:T(8,128)(2,1)} %pad_maximum_fusion.both_ref, bf16[1536,576]{1,0:T(8,128)(2,1)} %copy-done.14), custom_call_target="tpu_custom_call" | custom-call | flops 12230590464 | bytes 22118400 | tf_op jit(solution)/shard_map/pallas_call | solution.py:533
  450.9 14.6 %convolution_convert_fusion = bf16[1536,2304]{1,0:T(8,128)(2,1)} fusion(bf16[1536,1152]{1,0:T(8,128)(2,1)} %pad_maximum_fusion.both_ref, bf16[2304,1728]{1,0:T(8,128)(2,1)} %bitcast.151), kind=kOutput, calls=%fused_computation.2 | convolution fusion | flops 8157265920 | bytes 15925248 | tf_op jit(solution)/shard_map/tc,dc->td/dot_general | solution.py:63
  465.5 2.1 dynamic-slice_bitcast_fusion
  469.6 53.5 %shard_map.243 = f32[96,2304]{1,0:T(8,128)} custom-call(bf16[16,96,2304]{2,1,0:T(8,128)(2,1)} %bitcast.130), custom_call_target="tpu_custom_call" | custom-call | bytes 70778880 | tf_op jit(solution)/shard_map/pallas_call | solution.py:495
  524.7 1.7 multiply_reduce_fusion.5
  526.8 1.7 collective-permute-start.9
  531.6 3.9 fusion.22
  535.5 13.8 %shard_map.245 = bf16[4,96,2304]{2,1,0:T(8,128)(2,1)} custom-call(bf16[96,2304]{1,0:T(8,128)(2,1)} %fusion.48.refs_0_), custom_call_target="tpu_custom_call" | custom-call | bytes 17694720 | tf_op jit(solution)/shard_map/pallas_call | solution.py:322
  549.3 3.2 collective-permute-done.10
  552.5 20.4 %collective-permute-done.9 = bf16[288,1728]{1,0:T(8,128)(2,1)} collective-permute-done((bf16[288,1728]{1,0:T(8,128)(2,1)}, bf16[288,1728]{1,0:T(8,128)(2,1)}, u32[]{:S(2)}, u32[]{:S(2)}) %collective-permute-start.9) | collective-permute-done | bytes 995360 | tf_op jit(solution)/shard_map/ppermute | solution.py:72
  572.9 3.4 fusion.33
  577.8 3.4 fusion.43
  581.2 3.3 fusion.40
  584.6 3.2 fusion.37
  589.0 5.7 convolution_convert_fusion.2
  595.7 2.2 copy.90
  597.9 4.2 fusion.20
  602.1 2.5 collective-permute-start.13
  605.9 14.8 %shard_map.246 = f32[96,2304]{1,0:T(8,128)} custom-call(bf16[4,96,2304]{2,1,0:T(8,128)(2,1)} %bitcast.135), custom_call_target="tpu_custom_call" | custom-call | bytes 17694720 | tf_op jit(solution)/shard_map/pallas_call | solution.py:495
  620.7 2.1 multiply_reduce_fusion.2
  626.2 2.1 pad_maximum_fusion.2.tail_ref
  629.1 105.6 %shard_map.247 = (f32[304,1536]{1,0:T(8,128)}, bf16[4,192,2304]{2,1,0:T(8,128)(2,1)}) custom-call(bf16[2304,384]{1,0:T(8,128)(2,1)} %copy.105.h_ref, bf16[2304,384]{1,0:T(8,128)(2,1)} %bitcast.134, bf16[384,1024]{1,0:T(8,128)(2,1)} %pad_maximum_fusion.3.qkv_ref, bf16[384,512]{1,0:T(8,128)(2,1)} %copy.120.mixed_ref, bf16[8,16,1536]{2,1,0:T(8,128)(2,1)} %pad.4.strip_ref, ...), custom_call_target="tpu_custom_call" | custom-call | flops 2717908992 | bytes 70778880 | tf_op jit(solution)/shard_map/pallas_call | solution.py:785
  734.7 3.6 fusion.100
  740.9 2.1 bitcast_convert_fusion
  743.1 8.1 %shard_map.248 = (f32[288,2304]{1,0:T(8,128)}, f32[288,2304]{1,0:T(8,128)}, f32[288,2304]{1,0:T(8,128)}) custom-call(bf16[288,1728]{1,0:T(8,128)(2,1)} %get-tuple-element.83.refs_0_, bf16[288,1728]{1,0:T(8,128)(2,1)} %collective-permute-done.11.refs_1_, bf16[288,1728]{1,0:T(8,128)(2,1)} %collective-permute-done.12.refs_2_, ...), custom_call_target="tpu_custom_call" | custom-call | tf_op jit(solution)/shard_map/pallas_call | solution.py:572
  (158 shorter events, 42.6 us)
Async XLA Ops:
  0.6 16.8 %copy-start.1 = (bf16[384,2304]{1,0:T(8,128)(2,1)S(1)}, bf16[384,2304]{1,0:T(8,128)(2,1)}, u32[]{:S(2)}) copy-start(bf16[384,2304]{1,0:T(8,128)(2,1)} %param.14) | copy-start | bytes 5308420
  10.6 137.5 %collective-permute-start = (bf16[288,1728]{1,0:T(8,128)(2,1)}, bf16[288,1728]{1,0:T(8,128)(2,1)}, u32[]{:S(2)}, u32[]{:S(2)}) collective-permute-start(bf16[288,1728]{1,0:T(8,128)(2,1)} %get-tuple-element.39), channel_id=1, source_target_pairs={{0,8},{8,16},{16,24},{24,0},{1,9},{9,17},{17,25},{25,1},{2,10},{10... | collective-permute-start | bytes 2985992 | tf_op jit(solution)/shard_map/ppermute | solution.py:72
  13.7 134.5 %collective-permute-start.1 = (bf16[288,1728]{1,0:T(8,128)(2,1)}, bf16[288,1728]{1,0:T(8,128)(2,1)}, u32[]{:S(2)}, u32[]{:S(2)}) collective-permute-start(bf16[288,1728]{1,0:T(8,128)(2,1)} %get-tuple-element.40), channel_id=1, source_target_pairs={{0,24},{8,0},{16,8},{24,16},{1,25},{9,1},{17,9},{25,17},{2,26},{10... | collective-permute-start | bytes 2985992 | tf_op jit(solution)/shard_map/ppermute | solution.py:72
  15.7 215.6 %collective-permute-start.2 = (bf16[288,1728]{1,0:T(8,128)(2,1)}, bf16[288,1728]{1,0:T(8,128)(2,1)}, u32[]{:S(2)}, u32[]{:S(2)}) collective-permute-start(bf16[288,1728]{1,0:T(8,128)(2,1)} %get-tuple-element.45.refs_4_), channel_id=1, source_target_pairs={{0,4},{4,0},{1,5},{5,1},{2,6},{6,2},{3,7},{7,3},{8,12},{12,8},{9,1... | collective-permute-start | bytes 2985992 | tf_op jit(solution)/shard_map/ppermute | solution.py:72
  17.9 2.1 copy-start.26
  17.9 2.1 copy-start.27
  17.9 2.1 copy-start.29
  17.9 2.0 copy-start.30
  20.9 120.1 %copy-start.37 = (s32[1,8]{1,0:T(1,128)S(1)}, s32[1,8]{1,0:T(1,128)}, u32[]{:S(2)}) copy-start(s32[1,8]{1,0:T(1,128)} %param.16) | copy-start | bytes 100
  20.9 120.8 %copy-start.34 = (f32[2304]{0:T(1024)S(1)}, f32[2304]{0:T(1024)}, u32[]{:S(2)}) copy-start(f32[2304]{0:T(1024)} %param.17) | copy-start | bytes 27652
  148.2 4.6 copy-start.15
  148.2 4.6 copy-start.17
  153.8 1.8 copy-start.22
  153.8 1.2 slice-start
  155.4 2.3 copy-start.12
  160.2 4.2 copy-start.24
  164.4 18.6 %copy-start.25 = (bf16[2,384,256]{1,2,0:T(8,128)(2,1)S(1)}, bf16[2,384,256]{1,2,0:T(8,128)(2,1)}, u32[]{:S(2)}) copy-start(bf16[2,384,256]{1,2,0:T(8,128)(2,1)} %copy-done.24) | copy-start | bytes 1179652
  164.4 21.6 %copy-start.33 = (f32[2304]{0:T(1024)S(1)}, f32[2304]{0:T(1024)}, u32[]{:S(2)}) copy-start(f32[2304]{0:T(1024)} %param.22) | copy-start | bytes 27652
  181.5 4.5 copy-start
  181.5 45.6 %copy-start.31 = (pred[384,384]{0,1:T(8,128)(4,1)S(1)}, pred[384,384]{0,1:T(8,128)(4,1)}, u32[]{:S(2)}) copy-start(pred[384,384]{0,1:T(8,128)(4,1)} %fusion.62) | copy-start | bytes 442372
  181.5 45.1 %collective-permute-start.5 = (bf16[288,1728]{1,0:T(8,128)(2,1)}, bf16[288,1728]{1,0:T(8,128)(2,1)}, u32[]{:S(2)}, u32[]{:S(2)}) collective-permute-start(bf16[288,1728]{1,0:T(8,128)(2,1)} %get-tuple-element.46), channel_id=1, source_target_pairs={{0,16},{8,24},{16,0},{24,8},{1,17},{9,25},{17,1},{25,9},{2,18},{10... | collective-permute-start | bytes 2985992 | tf_op jit(solution)/shard_map/ppermute | solution.py:72
  183.9 47.4 %collective-permute-start.3 = (bf16[288,1728]{1,0:T(8,128)(2,1)}, bf16[288,1728]{1,0:T(8,128)(2,1)}, u32[]{:S(2)}, u32[]{:S(2)}) collective-permute-start(bf16[288,1728]{1,0:T(8,128)(2,1)} %collective-permute-done.refs_5_), channel_id=1, source_target_pairs={{0,4},{4,0},{1,5},{5,1},{2,6},{6,2},{3,7},{7,3},{8,12},{12,8},{9,1... | collective-permute-start | bytes 2985992 | tf_op jit(solution)/shard_map/ppermute | solution.py:72
  184.4 47.6 %collective-permute-start.4 = (bf16[288,1728]{1,0:T(8,128)(2,1)}, bf16[288,1728]{1,0:T(8,128)(2,1)}, u32[]{:S(2)}, u32[]{:S(2)}) collective-permute-start(bf16[288,1728]{1,0:T(8,128)(2,1)} %collective-permute-done.1.refs_7_), channel_id=1, source_target_pairs={{0,4},{4,0},{1,5},{5,1},{2,6},{6,2},{3,7},{7,3},{8,12},{12,8},{9,1... | collective-permute-start | bytes 2985992 | tf_op jit(solution)/shard_map/ppermute | solution.py:72
  187.5 43.9 %copy-start.36 = (f32[96]{0:T(128)}, f32[96]{0:T(128)S(1)}, u32[]{:S(2)}) copy-start(f32[96]{0:T(128)S(1)} %get-tuple-element.92) | copy-start | bytes 1156
  187.5 42.9 %copy-start.32 = (f32[2304]{0:T(1024)S(1)}, f32[2304]{0:T(1024)}, u32[]{:S(2)}) copy-start(f32[2304]{0:T(1024)} %param.23) | copy-start | bytes 27652
  226.6 52.5 %collective-permute-start.6 = (bf16[288,1728]{1,0:T(8,128)(2,1)}, bf16[288,1728]{1,0:T(8,128)(2,1)}, u32[]{:S(2)}, u32[]{:S(2)}) collective-permute-start(bf16[288,1728]{1,0:T(8,128)(2,1)} %collective-permute-done.5.refs_6_), channel_id=1, source_target_pairs={{0,4},{4,0},{1,5},{5,1},{2,6},{6,2},{3,7},{7,3},{8,12},{12,8},{9,1... | collective-permute-start | bytes 2985992 | tf_op jit(solution)/shard_map/ppermute | solution.py:72
  294.4 2.9 copy-start.4
  297.3 10.3 %copy-start.14 = (bf16[1536,576]{1,0:T(8,128)(2,1)}, bf16[1536,576]{1,0:T(8,128)(2,1)S(1)}, u32[]{:S(2)}) copy-start(bf16[1536,576]{1,0:T(8,128)(2,1)S(1)} %multiply_convert_fusion.1.hidden_ref) | copy-start | bytes 5308420
  307.7 54.0 %copy-start.35 = (f32[2304]{0:T(1024)S(1)}, f32[2304]{0:T(1024)}, u32[]{:S(2)}) copy-start(f32[2304]{0:T(1024)} %param.27) | copy-start | bytes 27652
  360.2 4.0 copy-start.2
  450.9 14.6 %copy-start.5 = (bf16[2304,1728]{1,0:T(8,128)(2,1)S(1)}, bf16[2304,1728]{1,0:T(8,128)(2,1)}, u32[]{:S(2)}) copy-start(bf16[2304,1728]{1,0:T(8,128)(2,1)} %shard_map.244) | copy-start | bytes 23887876
  467.6 64.0 %collective-permute-start.7 = (bf16[288,1728]{1,0:T(8,128)(2,1)}, bf16[288,1728]{1,0:T(8,128)(2,1)}, u32[]{:S(2)}, u32[]{:S(2)}) collective-permute-start(bf16[288,1728]{1,0:T(8,128)(2,1)} %get-tuple-element.87), channel_id=1, source_target_pairs={{0,4},{4,0},{1,5},{5,1},{2,6},{6,2},{3,7},{7,3},{8,12},{12,8},{9,1... | collective-permute-start | bytes 2985992 | tf_op jit(solution)/shard_map/ppermute | solution.py:72
  468.0 63.6 %collective-permute-start.8 = (bf16[288,1728]{1,0:T(8,128)(2,1)}, bf16[288,1728]{1,0:T(8,128)(2,1)}, u32[]{:S(2)}, u32[]{:S(2)}) collective-permute-start(bf16[288,1728]{1,0:T(8,128)(2,1)} %get-tuple-element.86), channel_id=1, source_target_pairs={{0,4},{4,0},{1,5},{5,1},{2,6},{6,2},{3,7},{7,3},{8,12},{12,8},{9,1... | collective-permute-start | bytes 2985992 | tf_op jit(solution)/shard_map/ppermute | solution.py:72
  523.1 1.6 copy-start.9
  526.4 9.1 %copy-start.6 = (f32[96,2304]{1,0:T(8,128)}, f32[96,2304]{1,0:T(8,128)S(1)}, u32[]{:S(2)}) copy-start(f32[96,2304]{1,0:T(8,128)S(1)} %get-tuple-element.77) | copy-start | bytes 2654212
  526.4 26.1 %collective-permute-start.10 = (bf16[288,1728]{1,0:T(8,128)(2,1)}, bf16[288,1728]{1,0:T(8,128)(2,1)}, u32[]{:S(2)}, u32[]{:S(2)}) collective-permute-start(bf16[288,1728]{1,0:T(8,128)(2,1)} %get-tuple-element.52), channel_id=1, source_target_pairs={{0,4},{4,0},{1,5},{5,1},{2,6},{6,2},{3,7},{7,3},{8,12},{12,8},{9,1... | collective-permute-start | bytes 2985992 | tf_op jit(solution)/shard_map/ppermute | solution.py:72
  526.8 46.0 %collective-permute-start.9 = (bf16[288,1728]{1,0:T(8,128)(2,1)}, bf16[288,1728]{1,0:T(8,128)(2,1)}, u32[]{:S(2)}, u32[]{:S(2)}) collective-permute-start(bf16[288,1728]{1,0:T(8,128)(2,1)} %get-tuple-element.51), channel_id=1, source_target_pairs={{0,4},{4,0},{1,5},{5,1},{2,6},{6,2},{3,7},{7,3},{8,12},{12,8},{9,1... | collective-permute-start | bytes 2985992 | tf_op jit(solution)/shard_map/ppermute | solution.py:72
  572.9 3.6 copy-start.13
  576.2 1.6 copy-start.23
  576.5 4.7 copy-start.21
  589.0 6.7 copy-start.10
  597.9 22.8 %copy-start.3 = (f32[384,2304]{1,0:T(8,128)S(1)}, f32[384,2304]{1,0:T(8,128)}, u32[]{:S(2)}) copy-start(f32[384,2304]{1,0:T(8,128)} %convert_element_type.168) | copy-start | bytes 10616836
  602.1 141.0 %collective-permute-start.13 = (bf16[288,1728]{1,0:T(8,128)(2,1)}, bf16[288,1728]{1,0:T(8,128)(2,1)}, u32[]{:S(2)}, u32[]{:S(2)}) collective-permute-start(bf16[288,1728]{1,0:T(8,128)(2,1)} %get-tuple-element.82), channel_id=1, source_target_pairs={{0,24},{8,0},{16,8},{24,16},{1,25},{9,1},{17,9},{25,17},{2,26},{10... | collective-permute-start | bytes 2985992 | tf_op jit(solution)/shard_map/ppermute | solution.py:72
  604.6 138.4 %collective-permute-start.11 = (bf16[288,1728]{1,0:T(8,128)(2,1)}, bf16[288,1728]{1,0:T(8,128)(2,1)}, u32[]{:S(2)}, u32[]{:S(2)}) collective-permute-start(bf16[288,1728]{1,0:T(8,128)(2,1)} %get-tuple-element.57), channel_id=1, source_target_pairs={{0,8},{8,16},{16,24},{24,0},{1,9},{9,17},{17,25},{25,1},{2,10},{10... | collective-permute-start | bytes 2985992 | tf_op jit(solution)/shard_map/ppermute | solution.py:72
  604.6 138.4 %collective-permute-start.12 = (bf16[288,1728]{1,0:T(8,128)(2,1)}, bf16[288,1728]{1,0:T(8,128)(2,1)}, u32[]{:S(2)}, u32[]{:S(2)}) collective-permute-start(bf16[288,1728]{1,0:T(8,128)(2,1)} %get-tuple-element.58), channel_id=1, source_target_pairs={{0,16},{8,24},{16,0},{24,8},{1,17},{9,25},{17,1},{25,9},{2,18},{10... | collective-permute-start | bytes 2985992 | tf_op jit(solution)/shard_map/ppermute | solution.py:72
  620.7 2.8 copy-start.7
  620.7 2.8 copy-start.8
  734.7 3.6 copy-start.19
  (6 other events, 5.4 us)

commit v4 on v3

--- a/solution.py
+++ b/solution.py
@@ -513,6 +513,199 @@
             flops=0, bytes_accessed=20 * blocks.size, transcendentals=0
         ),
     )(blocks)
+
+
+def product_scatter_kernel(
+    lanes, chain, columns, left_ref, right_ref, o_ref,
+    made, came0, came1, held0, held1, chained, send0, send1, sendc, got0, got1, gotc,
+):
+    spot = Spot(lanes, chain, ("x", "core"))
+    length, step, here = spot.length, spot.step, spot.here
+    n_x, n_core = spot.sizes["x"], spot.sizes["core"]
+    rows = o_ref.shape[0]
+    begin, end = columns
+    started = []
+
+    def remote(source, target, send_at, recv_at, device):
+        return pltpu.make_async_remote_copy(
+            src_ref=source,
+            dst_ref=target,
+            send_sem=send_at,
+            recv_sem=recv_at,
+            device_id=device,
+            device_id_type=MESH,
+        )
+
+    def arrive(condition, target, recv_at):
+        copy = remote(target, target, recv_at, recv_at, spot.device(here))
+        guarded(condition, copy.wait_recv)
+
+    span = n_x * n_core
+
+    def make(position):
+        window = pl.ds(pl.multiple_of(position * span * rows, span * rows), span * rows)
+        product = lax.dot_general(
+            left_ref[window, :],
+            right_ref[:, begin:end],
+            (((1,), (1,)), ((), ())),
+            preferred_element_type=jnp.float32,
+        ).astype(made.dtype)
+        for lane in range(span):
+            made[position * span + lane] = product[lane * rows : (lane + 1) * rows]
+
+    orders = [sorted(range(length), key=lambda p, at=at: -abs(p - at)) for at in range(length)]
+
+    def place(j):
+        position = 0
+        for at in range(length):
+            for number in range(length):
+                chosen = (step == at).astype(jnp.int32) * (j == number).astype(jnp.int32)
+                position = position + chosen * orders[at][number]
+        return position
+
+    def core_copy(position, x_shift, shift):
+        at_x = spot.moved(x=x_shift)["x"]
+        peer = spot.moved(core=shift)
+        lane = position * n_x + at_x
+        return remote(
+            made.at[lane * n_core + peer["core"]],
+            came0.at[shift - 1, lane],
+            send0.at[shift - 1, lane],
+            got0.at[shift - 1, lane],
+            spot.device(peer),
+        )
+
+    def x_copy(position, shift):
+        return remote(
+            held0.at[shift - 1, position],
+            came1.at[shift - 1, position],
+            send1.at[shift - 1, position],
+            got1.at[shift - 1, position],
+            spot.device(spot.moved(x=shift)),
+        )
+
+    def core_parts(there, position, shift_x):
+        lane = position * n_x + spot.moved(x=shift_x)["x"]
+        parts = [made.at[lane * n_core + here["core"]]]
+        for shift in range(1, n_core):
+            arrive(there, came0.at[shift - 1, lane], got0.at[shift - 1, lane])
+            parts.append(came0.at[shift - 1, lane])
+        return parts
+
+    spot.greet()
+
+    def produce(j, carry):
+        @pl.when(j < length)
+        def _():
+            position = place(j)
+            make(position)
+            for x_shift in (*range(1, n_x), 0):
+                for shift in range(1, n_core):
+                    core_copy(position, x_shift, shift).start()
+
+        @pl.when(j > 0)
+        def _():
+            position = place(j - 1)
+            for shift in range(1, n_x):
+                add_into(held0.at[shift - 1, position], core_parts(None, position, shift))
+                x_copy(position, shift).start()
+
+        return carry
+
+    lax.fori_loop(0, length + 1, produce, 0)
+
+    visits = []
+    for distance in range(length - 1, -1, -1):
+        if distance == 0:
+            visits.append((None, step, 0))
+        else:
+            visits.append(
+                (step - distance >= 0, lax.rem(step - distance + length, length), -1)
+            )
+            visits.append((step + distance < length, lax.rem(step + distance, length), 1))
+
+    for there, position, way in visits:
+        parts = core_parts(there, position, 0)
+        for shift in range(1, n_x):
+            arrive(there, came1.at[shift - 1, position], got1.at[shift - 1, position])
+            parts.append(came1.at[shift - 1, position])
+        if length == 1:
+            add_into(o_ref, parts)
+        elif way == 0:
+            left, right = step > 0, step < length - 1
+            for side, exists in ((0, left), (1, right)):
+                arrive(exists, chained.at[side, position], gotc.at[side, position])
+            sides = [chained.at[0, position], chained.at[1, position]]
+            add_into(o_ref, parts + sides, jnp.logical_and(left, right))
+            add_into(o_ref, parts + sides[1:], jnp.logical_not(left))
+            add_into(o_ref, parts + sides[:1], jnp.logical_not(right))
+        else:
+            side = 1 if way == -1 else 0
+            link = step < length - 1 if way == -1 else step > 0
+            more = jnp.logical_and(there, link)
+            alone = jnp.logical_and(there, jnp.logical_not(link))
+            arrive(more, chained.at[side, position], gotc.at[side, position])
+            add_into(held1.at[position], parts + [chained.at[side, position]], more)
+            add_into(held1.at[position], parts, alone)
+            copy = remote(
+                held1.at[position],
+                chained.at[side, position],
+                sendc.at[position],
+                gotc.at[side, position],
+                spot.device(here, way),
+            )
+            guarded(there, copy.start)
+            started.append((there, copy))
+    for condition, copy in started:
+        guarded(condition, copy.wait_send)
+
+    def drain(position, carry):
+        for x_shift in range(n_x):
+            for shift in range(1, n_core):
+                core_copy(position, x_shift, shift).wait_send()
+        for shift in range(1, n_x):
+            x_copy(position, shift).wait_send()
+        return carry
+
+    lax.fori_loop(0, length, drain, 0)
+
+
+def product_scatter(left, right, columns, lanes, chain, collective_id):
+    sizes = device_layout(lanes)
+    length = lanes[0] if chain else 1
+    n_x, n_core = sizes["x"], sizes["core"]
+    count = length * n_x * n_core
+    block = (left.shape[0] // count, right.shape[0])
+    low = left.dtype
+    more_core, more_x = max(n_core - 1, 1), max(n_x - 1, 1)
+    vmem = pl.BlockSpec(memory_space=pltpu.VMEM)
+    dma = pltpu.SemaphoreType.DMA
+    return pl.pallas_call(
+        functools.partial(product_scatter_kernel, lanes, chain, columns),
+        out_shape=jax.ShapeDtypeStruct(block, jnp.float32),
+        in_specs=[vmem, vmem],
+        out_specs=vmem,
+        scratch_shapes=[
+            pltpu.VMEM((count,) + block, low),
+            pltpu.VMEM((more_core, length * n_x) + block, low),
+            pltpu.VMEM((more_x, length) + block, low),
+            pltpu.VMEM((more_x, length) + block, low),
+            pltpu.VMEM((length,) + block, low),
+            pltpu.VMEM((2, length) + block, low),
+            dma((more_core, length * n_x)),
+            dma((more_x, length)),
+            dma((length,)),
+            dma((more_core, length * n_x)),
+            dma((more_x, length)),
+            dma((2, length)),
+        ],
+        compiler_params=pltpu.CompilerParams(collective_id=collective_id, has_side_effects=True),
+        cost_estimate=pl.CostEstimate(
+            flops=2 * left.size * right.shape[0],
+            bytes_accessed=40 * left.shape[0] * right.shape[0],
+            transcendentals=0,
+        ),
+    )(left, right)
 
 
 def weight_grads_kernel(h_ref, g_ref, both_ref, hidden_ref, o_ref):
@@ -934,14 +1127,7 @@
     gelu_gate = gelu_tanh(gate_pre)
     hidden = (gelu_gate * up_pre).astype(low)
     down_full = ffn_full[:, 2 * part :]
-    ffn_branch = scatter_sum(
-        right_product(hidden, down_full).astype(low).reshape(outer * tensor, split_rows, -1),
-        lanes,
-        True,
-        ("x", "core"),
-        ("core", "x"),
-        3,
-    )
+    ffn_branch = product_scatter(hidden, ffn_full, (2 * part, 3 * part), lanes, True, 3)
     output_own = (resid + rms_scale(ffn_branch, norm_ffn_out)).astype(low)
 
     grad_out = own_rows(cotangent).astype(jnp.float32) * own_rows(
@@ -956,15 +1142,7 @@
     _, pull_gelu = jax.vjp(gelu_tanh, gate_pre)
     grad_gate = pull_gelu(grad_hidden * up_pre)[0].astype(low)
     grad_both = jnp.concatenate([grad_gate, grad_up], axis=1)
-    grad_h_part = right_product(grad_both, ffn_full[:, : 2 * part]).astype(low)
-    grad_h_ffn = scatter_sum(
-        grad_h_part.reshape(outer * tensor, split_rows, -1),
-        lanes,
-        True,
-        ("x", "core"),
-        ("core", "x"),
-        5,
-    )
+    grad_h_ffn = product_scatter(grad_both, ffn_full, (0, 2 * part), lanes, True, 5)
     grad_w_ffn = weight_grads(h_all, grad_ffn_all, grad_both, hidden)
     grad_w_ffn = grad_w_ffn.reshape(outer, inner, shard_rows, 3 * part)
     here, row = lax.axis_index("outer"), lax.axis_index("inner")
@@ -1014,10 +1192,6 @@
     grad_attn_branch = gather_blocks(
         grad_attn_own, lanes, False, ("x", "core"), 6
     ).reshape(row_count, -1)
-    grad_attn_branch, rows_later = lax.optimization_barrier((grad_attn_branch, rows_later))
-    summed.update(send_rows(sum_rows(1, rows_later)))
-    sum_gate, sum_up, sum_down = unpack([summed[step] for step in range(outer)], part)
-    sum_down = sum_down.T
     grad_mixed = matmul(grad_attn_branch, out_turned).astype(low)
     grad_mixed = grad_mixed.reshape(row_count, kv_heads, groups, HD).transpose(1, 2, 0, 3)
     grad_values = jnp.einsum(
@@ -1029,6 +1203,10 @@
     row_delta = jnp.sum(weights * grad_probs, axis=-1, keepdims=True)
     tanh_part = capped / SOFT_CAP
     grad_scores = (weights * (grad_probs - row_delta) * (1.0 - tanh_part * tanh_part)).astype(low)
+    grad_scores, rows_later = lax.optimization_barrier((grad_scores, rows_later))
+    summed.update(send_rows(sum_rows(1, rows_later)))
+    sum_gate, sum_up, sum_down = unpack([summed[step] for step in range(outer)], part)
+    sum_down = sum_down.T
     grad_query_raw = jnp.einsum(
         "kgqs,ksd->kgqd", grad_scores, keys, preferred_element_type=jnp.float32
     )

time: 761 us -> 766 us (level)
  waiting for transfers between devices: 63.3 us -> 95.8 us
  matrix products: 84.1 us -> 51.7 us
    pallas_call x0 -> x2, Pallas kernels: none -> 108 us  [product_scatter(): pl.pallas_call(functools.partial(product_scatter_kernel, lanes, chain, co...]
    pallas_call x4 -> x2, Pallas kernels: 138 us -> 32.7 us  [scatter_sum(): pl.pallas_call(functools.partial(scatter_kernel, lanes, chain, levels, or...]
    ppermute x14, waiting for transfers between devices: 63.3 us -> 95.8 us  [shifted(): lax.ppermute(block, axis, [(i, (i + step) % size) for i in range(size)])]
    dot_general x4 -> x2, matrix products: 34.8 us -> 9.71 us  [right_product(): jnp.einsum('tc,dc->td', left, right, preferred_element_type=jnp.float32)]
  transfers between devices with their start and end apart: 14 -> 14, of which waited for: 4 -> 5; matrix products, arithmetic and copies ran while one was open for 8% -> 8% of each run, Pallas kernels for 49% -> 42%
where the time goes in v4:
time: 766 us; the launch traced here: 757 us
  Pallas kernels  512 us (67%)
  waiting for transfers between devices  95.8 us (13%)
  matrix products  51.7 us (7%)
  other arithmetic  48.1 us (6%)
  local copies, waits for them, and re-layouts  29.8 us (4%)
  starting transfers between devices  17.3 us (2%)
    pallas_call x4, Pallas kernels, gather_blocks(): pl.pallas_call(functools.partial(gather_kernel, lanes, chain, levels, pla...  228 us
    pallas_call x2, Pallas kernels, product_scatter(): pl.pallas_call(functools.partial(product_scatter_kernel, lanes, chain, co...  108 us
    pallas_call x1, Pallas kernels, finish(): pl.pallas_call(functools.partial(finish_kernel, lanes), out_shape=[jax.Sh...  105 us
    ppermute x14, waiting for transfers between devices, shifted(): lax.ppermute(block, axis, [(i, (i + step) % size) for i in range(size)])  95.8 us
    dot_general x4, matrix products, matmul(): return jnp.dot(left, right, preferred_element_type=jnp.float32)  34.1 us
    pallas_call x2, Pallas kernels, scatter_sum(): pl.pallas_call(functools.partial(scatter_kernel, lanes, chain, levels, or...  32.7 us
    pallas_call x1, Pallas kernels, weight_grads(): pl.pallas_call(weight_grads_kernel, grid=(width // tile,), out_shape=jax....  20.4 us
    ppermute x14, starting transfers between devices, shifted(): lax.ppermute(block, axis, [(i, (i + step) % size) for i in range(size)])  17.3 us
  transfers between devices with their start and end apart: 14, of which 5 were waited for; matrix products, arithmetic and copies ran while one was open for 8% of the time, Pallas kernels for 42%

profile of v4, /device:TPU:0, one launch (start us, length us, event | category | flops | bytes accessed | tf_op | source)
XLA Modules:
  0.0 756.8 jit_solution(11292369095874939773)
XLA Ops:
  0.7 10.0 %shard_map.238 = (bf16[288,1728]{1,0:T(8,128)(2,1)}, bf16[288,1728]{1,0:T(8,128)(2,1)}, bf16[288,1728]{1,0:T(8,128)(2,1)}, bf16[288,1728]{1,0:T(8,128)(2,1)}) custom-call(bf16[288,2304]{1,0:T(8,128)(2,1)} %g_ref.1, bf16[288,2304]{1,0:T(8,128)(2,1)} %u_ref.1, bf16[288,2304]{1,0:T(8,128)(2,1)} %bitcast.146), custom_call_target="tpu_custom_call" | custom-call | bytes 7962624 | tf_op jit(solution)/shard_map/pallas_call | solution.py:97
  10.6 3.1 collective-permute-start
  13.7 2.0 collective-permute-start.1
  15.7 1.7 collective-permute-start.2
  17.9 2.0 convert_element_type.164
  20.9 120.0 %shard_map.237 = bf16[8,288,1536]{2,1,0:T(8,128)(2,1)} custom-call(bf16[288,1536]{1,0:T(8,128)(2,1)} %pad_maximum_fusion.1.refs_0_), custom_call_target="tpu_custom_call" | custom-call | bytes 70778880 | tf_op jit(solution)/shard_map/pallas_call | solution.py:322
  142.2 2.2 copy.105.h_ref
  148.7 4.5 fusion.5
  156.7 2.4 convolution_convert_fusion.2
  159.1 4.0 convolution_convert_fusion.1
  163.1 17.0 %shard_map.239 = f32[96,2304]{1,0:T(8,128)} custom-call(bf16[4,96,2304]{2,1,0:T(8,128)(2,1)} %bitcast.144), custom_call_target="tpu_custom_call" | custom-call | bytes 17694720 | tf_op jit(solution)/shard_map/pallas_call | solution.py:495
  186.8 38.5 %collective-permute-done.5.refs_6_ = bf16[288,1728]{1,0:T(8,128)(2,1)} collective-permute-done((bf16[288,1728]{1,0:T(8,128)(2,1)}, bf16[288,1728]{1,0:T(8,128)(2,1)}, u32[]{:S(2)}, u32[]{:S(2)}) %collective-permute-start.5) | collective-permute-done | bytes 995360 | tf_op jit(solution)/shard_map/ppermute | solution.py:72
  225.8 2.7 fusion.26
  230.7 47.0 %shard_map.240 = (bf16[16,96,2304]{2,1,0:T(8,128)(2,1)}, bf16[8,288,1728]{2,1,0:T(8,128)(2,1)}) custom-call(bf16[96,2304]{1,0:T(8,128)(2,1)} %multiply_convert_fusion.3.refs_0_, bf16[288,1728]{1,0:T(8,128)(2,1)} %collective-permute-done.2.refs_1_, bf16[288,1728]{1,0:T(8,128)(2,1)} %collective-permute-done.3.refs_2_, ...), custom_call_target="tpu_custom_call" | custom-call | bytes 70778880 | tf_op jit(solution)/shard_map/pallas_call | solution.py:322
  277.7 2.3 bitcast_dynamic-update-slice_fusion
  280.0 13.1 %fusion.2 = f32[1536,1152]{1,0:T(8,128)S(1)} fusion(bf16[1536,2304]{1,0:T(8,128)(2,1)} %bitcast.157, bf16[2304,1728]{1,0:T(8,128)(2,1)} %bitcast.153), kind=kOutput, calls=%fused_computation.6 | convolution fusion | flops 8153726976 | bytes 19464192 | tf_op jit(solution)/shard_map/dot_general | solution.py:59
  293.1 2.9 copy-done.3
  296.0 2.8 multiply_convert_fusion.1.left_ref.hidden_ref
  298.8 53.9 %shard_map.241 = f32[96,2304]{1,0:T(8,128)} custom-call(bf16[1536,576]{1,0:T(8,128)(2,1)} %multiply_convert_fusion.1.left_ref.hidden_ref, bf16[2304,1728]{1,0:T(8,128)(2,1)} %bitcast.154), custom_call_target="tpu_custom_call" | custom-call | flops 4076863488 | bytes 141557760 | tf_op jit(solution)/shard_map/pallas_call | solution.py:683
  354.1 2.5 multiply_reduce_fusion.3
  356.7 2.1 fusion.39.refs_0_
  358.8 47.1 %shard_map.242 = bf16[16,96,2304]{2,1,0:T(8,128)(2,1)} custom-call(bf16[96,2304]{1,0:T(8,128)(2,1)} %fusion.39.refs_0_), custom_call_target="tpu_custom_call" | custom-call | bytes 70778880 | tf_op jit(solution)/shard_map/pallas_call | solution.py:322
  405.9 13.2 %fusion.10 = (bf16[1536,576]{1,0:T(8,128)(2,1)S(1)}, bf16[1536,576]{1,0:T(8,128)(2,1)S(1)}) fusion(f32[1536,1152]{1,0:T(8,128)} %copy-done.3, bf16[1536,2304]{1,0:T(8,128)(2,1)} %bitcast.127, bf16[2304,1728]{1,0:T(8,128)(2,1)} %bitcast.155), kind=kOutput, calls=%fused_computation.16 | convolution fusion | flops 4101636096 | bytes 21430272 | tf_op jit(solution)/shard_map/dot_general | solution.py:59
  419.1 2.9 pad_maximum_fusion.left_ref.both_ref
  422.0 20.4 %shard_map.244 = bf16[2304,1728]{1,0:T(8,128)(2,1)} custom-call(bf16[1536,2304]{1,0:T(8,128)(2,1)} %bitcast.158, bf16[1536,2304]{1,0:T(8,128)(2,1)} %bitcast.128, bf16[1536,1152]{1,0:T(8,128)(2,1)} %pad_maximum_fusion.left_ref.both_ref, bf16[1536,576]{1,0:T(8,128)(2,1)} %multiply_convert_fusion.1.left_ref.hidden_ref), custom_call_target="tpu_custom_call" | custom-call | flops 12230590464 | bytes 22118400 | tf_op jit(solution)/shard_map/pallas_call | solution.py:726
  442.4 53.8 %shard_map.243 = f32[96,2304]{1,0:T(8,128)} custom-call(bf16[1536,1152]{1,0:T(8,128)(2,1)} %pad_maximum_fusion.left_ref.both_ref, bf16[2304,1728]{1,0:T(8,128)(2,1)} %bitcast.156), custom_call_target="tpu_custom_call" | custom-call | flops 8153726976 | bytes 141557760 | tf_op jit(solution)/shard_map/pallas_call | solution.py:683
  496.2 4.3 dynamic-slice_bitcast_fusion
  502.9 1.7 multiply_reduce_fusion.5
  509.7 16.9 %collective-permute-done.7 = bf16[288,1728]{1,0:T(8,128)(2,1)} collective-permute-done((bf16[288,1728]{1,0:T(8,128)(2,1)}, bf16[288,1728]{1,0:T(8,128)(2,1)}, u32[]{:S(2)}, u32[]{:S(2)}) %collective-permute-start.7) | collective-permute-done | bytes 995360 | tf_op jit(solution)/shard_map/ppermute | solution.py:72
  526.5 22.1 %collective-permute-done.8 = bf16[288,1728]{1,0:T(8,128)(2,1)} collective-permute-done((bf16[288,1728]{1,0:T(8,128)(2,1)}, bf16[288,1728]{1,0:T(8,128)(2,1)}, u32[]{:S(2)}, u32[]{:S(2)}) %collective-permute-start.8) | collective-permute-done | bytes 995360 | tf_op jit(solution)/shard_map/ppermute | solution.py:72
  548.7 3.9 fusion.20
  552.6 14.2 %shard_map.245 = bf16[4,96,2304]{2,1,0:T(8,128)(2,1)} custom-call(bf16[96,2304]{1,0:T(8,128)(2,1)} %fusion.41.refs_0_), custom_call_target="tpu_custom_call" | custom-call | bytes 17694720 | tf_op jit(solution)/shard_map/pallas_call | solution.py:322
  566.8 3.4 fusion.31
  570.5 2.5 fusion.34
  573.0 17.0 %collective-permute-done.9 = bf16[288,1728]{1,0:T(8,128)(2,1)} collective-permute-done((bf16[288,1728]{1,0:T(8,128)(2,1)}, bf16[288,1728]{1,0:T(8,128)(2,1)}, u32[]{:S(2)}, u32[]{:S(2)}) %collective-permute-start.9) | collective-permute-done | bytes 995360 | tf_op jit(solution)/shard_map/ppermute | solution.py:72
  590.8 2.0 fusion.36
  593.9 5.7 convolution_convert_fusion
  600.7 2.2 copy.90
  602.9 4.2 fusion.18
  607.0 1.7 collective-permute-start.13
  609.0 1.7 collective-permute-start.12
  610.7 15.7 %shard_map.246 = f32[96,2304]{1,0:T(8,128)} custom-call(bf16[4,96,2304]{2,1,0:T(8,128)(2,1)} %bitcast.143), custom_call_target="tpu_custom_call" | custom-call | bytes 17694720 | tf_op jit(solution)/shard_map/pallas_call | solution.py:495
  626.5 2.1 multiply_reduce_fusion.2
  632.0 2.1 pad_maximum_fusion.2.tail_ref
  634.9 105.2 %shard_map.247 = (f32[304,1536]{1,0:T(8,128)}, bf16[4,192,2304]{2,1,0:T(8,128)(2,1)}) custom-call(bf16[2304,384]{1,0:T(8,128)(2,1)} %copy.105.h_ref, bf16[2304,384]{1,0:T(8,128)(2,1)} %bitcast.142, bf16[384,1024]{1,0:T(8,128)(2,1)} %pad_maximum_fusion.3.qkv_ref, bf16[384,512]{1,0:T(8,128)(2,1)} %copy.120.mixed_ref, bf16[8,16,1536]{2,1,0:T(8,128)(2,1)} %pad.4.strip_ref, ...), custom_call_target="tpu_custom_call" | custom-call | flops 2717908992 | bytes 70778880 | tf_op jit(solution)/shard_map/pallas_call | solution.py:978
  740.1 3.6 fusion.95
  746.3 2.1 bitcast_convert_fusion
  748.5 8.1 %shard_map.248 = (f32[288,2304]{1,0:T(8,128)}, f32[288,2304]{1,0:T(8,128)}, f32[288,2304]{1,0:T(8,128)}) custom-call(bf16[288,1728]{1,0:T(8,128)(2,1)} %get-tuple-element.83.refs_0_, bf16[288,1728]{1,0:T(8,128)(2,1)} %collective-permute-done.11.refs_1_, bf16[288,1728]{1,0:T(8,128)(2,1)} %collective-permute-done.12.refs_2_, ...), custom_call_target="tpu_custom_call" | custom-call | tf_op jit(solution)/shard_map/pallas_call | solution.py:765
  (166 shorter events, 38.7 us)
Async XLA Ops:
  0.6 16.8 %copy-start.1 = (bf16[384,2304]{1,0:T(8,128)(2,1)S(1)}, bf16[384,2304]{1,0:T(8,128)(2,1)}, u32[]{:S(2)}) copy-start(bf16[384,2304]{1,0:T(8,128)(2,1)} %param.14) | copy-start | bytes 5308420
  10.6 138.1 %collective-permute-start = (bf16[288,1728]{1,0:T(8,128)(2,1)}, bf16[288,1728]{1,0:T(8,128)(2,1)}, u32[]{:S(2)}, u32[]{:S(2)}) collective-permute-start(bf16[288,1728]{1,0:T(8,128)(2,1)} %get-tuple-element.39), channel_id=1, source_target_pairs={{0,8},{8,16},{16,24},{24,0},{1,9},{9,17},{17,25},{25,1},{2,10},{10... | collective-permute-start | bytes 2985992 | tf_op jit(solution)/shard_map/ppermute | solution.py:72
  13.7 135.0 %collective-permute-start.1 = (bf16[288,1728]{1,0:T(8,128)(2,1)}, bf16[288,1728]{1,0:T(8,128)(2,1)}, u32[]{:S(2)}, u32[]{:S(2)}) collective-permute-start(bf16[288,1728]{1,0:T(8,128)(2,1)} %get-tuple-element.40), channel_id=1, source_target_pairs={{0,24},{8,0},{16,8},{24,16},{1,25},{9,1},{17,9},{25,17},{2,26},{10... | collective-permute-start | bytes 2985992 | tf_op jit(solution)/shard_map/ppermute | solution.py:72
  15.7 213.7 %collective-permute-start.2 = (bf16[288,1728]{1,0:T(8,128)(2,1)}, bf16[288,1728]{1,0:T(8,128)(2,1)}, u32[]{:S(2)}, u32[]{:S(2)}) collective-permute-start(bf16[288,1728]{1,0:T(8,128)(2,1)} %get-tuple-element.45.refs_4_), channel_id=1, source_target_pairs={{0,4},{4,0},{1,5},{5,1},{2,6},{6,2},{3,7},{7,3},{8,12},{12,8},{9,1... | collective-permute-start | bytes 2985992 | tf_op jit(solution)/shard_map/ppermute | solution.py:72
  17.9 2.1 copy-start.23
  17.9 2.1 copy-start.24
  20.9 120.1 %copy-start.42 = (s32[1,8]{1,0:T(1,128)S(1)}, s32[1,8]{1,0:T(1,128)}, u32[]{:S(2)}) copy-start(s32[1,8]{1,0:T(1,128)} %param.16) | copy-start | bytes 100
  20.9 120.8 %copy-start.30 = (f32[2304]{0:T(1024)S(1)}, f32[2304]{0:T(1024)}, u32[]{:S(2)}) copy-start(f32[2304]{0:T(1024)} %param.17) | copy-start | bytes 27652
  148.7 4.6 copy-start.18
  148.7 4.6 copy-start.20
  156.7 69.1 %copy-start.9 = (f32[2,384,384]{1,2,0:T(8,128)}, f32[2,384,384]{1,2,0:T(8,128)S(1)}, u32[]{:S(2)}) copy-start(f32[2,384,384]{1,2,0:T(8,128)S(1)} %fusion.22) | copy-start | bytes 3538948
  163.1 21.5 %copy-start.28 = (f32[2304]{0:T(1024)S(1)}, f32[2304]{0:T(1024)}, u32[]{:S(2)}) copy-start(f32[2304]{0:T(1024)} %param.22) | copy-start | bytes 27652
  180.1 4.5 copy-start
  180.1 45.1 %collective-permute-start.5 = (bf16[288,1728]{1,0:T(8,128)(2,1)}, bf16[288,1728]{1,0:T(8,128)(2,1)}, u32[]{:S(2)}, u32[]{:S(2)}) collective-permute-start(bf16[288,1728]{1,0:T(8,128)(2,1)} %get-tuple-element.46), channel_id=1, source_target_pairs={{0,16},{8,24},{16,0},{24,8},{1,17},{9,25},{17,1},{25,9},{2,18},{10... | collective-permute-start | bytes 2985992 | tf_op jit(solution)/shard_map/ppermute | solution.py:72
  181.6 3.0 copy-start.38
  182.6 46.8 %collective-permute-start.3 = (bf16[288,1728]{1,0:T(8,128)(2,1)}, bf16[288,1728]{1,0:T(8,128)(2,1)}, u32[]{:S(2)}, u32[]{:S(2)}) collective-permute-start(bf16[288,1728]{1,0:T(8,128)(2,1)} %collective-permute-done.refs_5_), channel_id=1, source_target_pairs={{0,4},{4,0},{1,5},{5,1},{2,6},{6,2},{3,7},{7,3},{8,12},{12,8},{9,1... | collective-permute-start | bytes 2985992 | tf_op jit(solution)/shard_map/ppermute | solution.py:72
  183.1 47.6 %collective-permute-start.4 = (bf16[288,1728]{1,0:T(8,128)(2,1)}, bf16[288,1728]{1,0:T(8,128)(2,1)}, u32[]{:S(2)}, u32[]{:S(2)}) collective-permute-start(bf16[288,1728]{1,0:T(8,128)(2,1)} %collective-permute-done.1.refs_7_), channel_id=1, source_target_pairs={{0,4},{4,0},{1,5},{5,1},{2,6},{6,2},{3,7},{7,3},{8,12},{12,8},{9,1... | collective-permute-start | bytes 2985992 | tf_op jit(solution)/shard_map/ppermute | solution.py:72
  184.6 43.8 %copy-start.33 = (f32[96]{0:T(128)}, f32[96]{0:T(128)S(1)}, u32[]{:S(2)}) copy-start(f32[96]{0:T(128)S(1)} %fusion.80) | copy-start | bytes 1156
  186.1 43.2 %copy-start.37 = (f32[96]{0:T(128)}, f32[96]{0:T(128)S(1)}, u32[]{:S(2)}) copy-start(f32[96]{0:T(128)S(1)} %get-tuple-element.92) | copy-start | bytes 1156
  186.2 43.2 %copy-start.40 = (f32[96]{0:T(128)}, f32[96]{0:T(128)S(1)}, u32[]{:S(2)}) copy-start(f32[96]{0:T(128)S(1)} %get-tuple-element.78) | copy-start | bytes 1156
  186.2 42.3 %copy-start.27 = (f32[2304]{0:T(1024)S(1)}, f32[2304]{0:T(1024)}, u32[]{:S(2)}) copy-start(f32[2304]{0:T(1024)} %param.23) | copy-start | bytes 27652
  225.2 52.5 %collective-permute-start.6 = (bf16[288,1728]{1,0:T(8,128)(2,1)}, bf16[288,1728]{1,0:T(8,128)(2,1)}, u32[]{:S(2)}, u32[]{:S(2)}) collective-permute-start(bf16[288,1728]{1,0:T(8,128)(2,1)} %collective-permute-done.5.refs_6_), channel_id=1, source_target_pairs={{0,4},{4,0},{1,5},{5,1},{2,6},{6,2},{3,7},{7,3},{8,12},{12,8},{9,1... | collective-permute-start | bytes 2985992 | tf_op jit(solution)/shard_map/ppermute | solution.py:72
  293.1 2.9 copy-start.3
  298.8 55.3 %copy-start.32 = (f32[2304]{0:T(1024)S(1)}, f32[2304]{0:T(1024)}, u32[]{:S(2)}) copy-start(f32[2304]{0:T(1024)} %param.27) | copy-start | bytes 27652
  298.8 55.3 %copy-start.35 = (f32[96]{0:T(128)S(1)}, f32[96]{0:T(128)}, u32[]{:S(2)}) copy-start(f32[96]{0:T(128)} %dynamic-slice.3) | copy-start | bytes 1156
  352.7 4.0 copy-start.7
  496.2 6.4 copy-start.11
  496.2 6.6 copy-start.41
  496.2 6.6 copy-start.29
  496.2 6.6 copy-start.34
  500.6 26.0 %collective-permute-start.7 = (bf16[288,1728]{1,0:T(8,128)(2,1)}, bf16[288,1728]{1,0:T(8,128)(2,1)}, u32[]{:S(2)}, u32[]{:S(2)}) collective-permute-start(bf16[288,1728]{1,0:T(8,128)(2,1)} %get-tuple-element.87), channel_id=1, source_target_pairs={{0,4},{4,0},{1,5},{5,1},{2,6},{6,2},{3,7},{7,3},{8,12},{12,8},{9,1... | collective-permute-start | bytes 2985992 | tf_op jit(solution)/shard_map/ppermute | solution.py:72
  501.1 47.6 %collective-permute-start.8 = (bf16[288,1728]{1,0:T(8,128)(2,1)}, bf16[288,1728]{1,0:T(8,128)(2,1)}, u32[]{:S(2)}, u32[]{:S(2)}) collective-permute-start(bf16[288,1728]{1,0:T(8,128)(2,1)} %get-tuple-element.86), channel_id=1, source_target_pairs={{0,4},{4,0},{1,5},{5,1},{2,6},{6,2},{3,7},{7,3},{8,12},{12,8},{9,1... | collective-permute-start | bytes 2985992 | tf_op jit(solution)/shard_map/ppermute | solution.py:72
  502.8 5.8 copy-start.39
  504.5 48.1 %copy-start.4 = (f32[96,2304]{1,0:T(8,128)}, f32[96,2304]{1,0:T(8,128)S(1)}, u32[]{:S(2)}) copy-start(f32[96,2304]{1,0:T(8,128)S(1)} %get-tuple-element.77) | copy-start | bytes 2654212
  504.5 68.4 %collective-permute-start.10 = (bf16[288,1728]{1,0:T(8,128)(2,1)}, bf16[288,1728]{1,0:T(8,128)(2,1)}, u32[]{:S(2)}, u32[]{:S(2)}) collective-permute-start(bf16[288,1728]{1,0:T(8,128)(2,1)} %get-tuple-element.52), channel_id=1, source_target_pairs={{0,4},{4,0},{1,5},{5,1},{2,6},{6,2},{3,7},{7,3},{8,12},{12,8},{9,1... | collective-permute-start | bytes 2985992 | tf_op jit(solution)/shard_map/ppermute | solution.py:72
  505.2 84.8 %collective-permute-start.9 = (bf16[288,1728]{1,0:T(8,128)(2,1)}, bf16[288,1728]{1,0:T(8,128)(2,1)}, u32[]{:S(2)}, u32[]{:S(2)}) collective-permute-start(bf16[288,1728]{1,0:T(8,128)(2,1)} %get-tuple-element.51), channel_id=1, source_target_pairs={{0,4},{4,0},{1,5},{5,1},{2,6},{6,2},{3,7},{7,3},{8,12},{12,8},{9,1... | collective-permute-start | bytes 2985992 | tf_op jit(solution)/shard_map/ppermute | solution.py:72
  566.8 3.6 copy-start.10
  570.4 2.5 copy-start.17
  593.9 6.7 copy-start.8
  602.9 23.6 %copy-start.2 = (f32[384,2304]{1,0:T(8,128)S(1)}, f32[384,2304]{1,0:T(8,128)}, u32[]{:S(2)}) copy-start(f32[384,2304]{1,0:T(8,128)} %convert_element_type.164) | copy-start | bytes 10616836
  607.0 19.4 %copy-start.31 = (f32[2304]{0:T(1024)S(1)}, f32[2304]{0:T(1024)}, u32[]{:S(2)}) copy-start(f32[2304]{0:T(1024)} %param.17) | copy-start | bytes 27652
  607.0 19.4 %copy-start.36 = (f32[96]{0:T(128)S(1)}, f32[96]{0:T(128)}, u32[]{:S(2)}) copy-start(f32[96]{0:T(128)} %fusion.83) | copy-start | bytes 1156
  607.0 141.4 %collective-permute-start.13 = (bf16[288,1728]{1,0:T(8,128)(2,1)}, bf16[288,1728]{1,0:T(8,128)(2,1)}, u32[]{:S(2)}, u32[]{:S(2)}) collective-permute-start(bf16[288,1728]{1,0:T(8,128)(2,1)} %get-tuple-element.82), channel_id=1, source_target_pairs={{0,24},{8,0},{16,8},{24,16},{1,25},{9,1},{17,9},{25,17},{2,26},{10... | collective-permute-start | bytes 2985992 | tf_op jit(solution)/shard_map/ppermute | solution.py:72
  608.7 139.8 %collective-permute-start.11 = (bf16[288,1728]{1,0:T(8,128)(2,1)}, bf16[288,1728]{1,0:T(8,128)(2,1)}, u32[]{:S(2)}, u32[]{:S(2)}) collective-permute-start(bf16[288,1728]{1,0:T(8,128)(2,1)} %get-tuple-element.57), channel_id=1, source_target_pairs={{0,8},{8,16},{16,24},{24,0},{1,9},{9,17},{17,25},{25,1},{2,10},{10... | collective-permute-start | bytes 2985992 | tf_op jit(solution)/shard_map/ppermute | solution.py:72
  609.0 139.4 %collective-permute-start.12 = (bf16[288,1728]{1,0:T(8,128)(2,1)}, bf16[288,1728]{1,0:T(8,128)(2,1)}, u32[]{:S(2)}, u32[]{:S(2)}) collective-permute-start(bf16[288,1728]{1,0:T(8,128)(2,1)} %get-tuple-element.58), channel_id=1, source_target_pairs={{0,16},{8,24},{16,0},{24,8},{1,17},{9,25},{17,1},{25,9},{2,18},{10... | collective-permute-start | bytes 2985992 | tf_op jit(solution)/shard_map/ppermute | solution.py:72
  626.5 2.8 copy-start.5
  626.5 2.8 copy-start.6
  740.1 3.6 copy-start.22
  (11 other events, 15.3 us)

commit v5 on v4

--- a/solution.py
+++ b/solution.py
@@ -93,12 +93,14 @@
 
 
 def pack(count, part, gate, up, down_turned):
-    vmem = pl.BlockSpec(memory_space=pltpu.VMEM)
+    rows, width = gate.shape
+    tile = math.gcd(rows, 48)
     return pl.pallas_call(
         functools.partial(pack_kernel, part),
-        out_shape=[jax.ShapeDtypeStruct((gate.shape[0], 3 * part), gate.dtype)] * count,
-        in_specs=[vmem] * 3,
-        out_specs=[vmem] * count,
+        grid=(rows // tile,),
+        out_shape=[jax.ShapeDtypeStruct((rows, 3 * part), gate.dtype)] * count,
+        in_specs=[pl.BlockSpec((tile, width), lambda i: (i, 0))] * 3,
+        out_specs=[pl.BlockSpec((tile, 3 * part), lambda i: (i, 0))] * count,
         cost_estimate=pl.CostEstimate(
             flops=0, bytes_accessed=12 * gate.size, transcendentals=0
         ),
@@ -1151,8 +1153,7 @@
         place = (lax.rem(here + step, outer), lax.rem(row + turn, inner), 0, 0)
         return lax.dynamic_slice(grad_w_ffn, place, (1, 1, shard_rows, 3 * part))[0, 0]
 
-    half = max(outer // 2, 1)
-    groups_of_steps = (range(1, 1 + half), [*range(1 + half, outer), 0])
+    groups_of_steps = (range(1, outer), [0])
     outgoing = [
         {(step, turn): grad_block(step, turn) for step in steps for turn in range(1, inner)}
         for steps in groups_of_steps

time: 766 us -> 777 us (1.014)
  no operation moved by 1% of the time
where the time goes in v5:
time: 777 us; the launch traced here: 768 us
  Pallas kernels  517 us (67%)
  waiting for transfers between devices  101 us (13%)
  matrix products  51.7 us (7%)
  other arithmetic  47.7 us (6%)
  local copies, waits for them, and re-layouts  29.8 us (4%)
  starting transfers between devices  18.9 us (2%)
    pallas_call x4, Pallas kernels, gather_blocks(): pl.pallas_call(functools.partial(gather_kernel, lanes, chain, levels, pla...  228 us
    pallas_call x1, Pallas kernels, finish(): pl.pallas_call(functools.partial(finish_kernel, lanes), out_shape=[jax.Sh...  110 us
    pallas_call x2, Pallas kernels, product_scatter(): pl.pallas_call(functools.partial(product_scatter_kernel, lanes, chain, co...  108 us
    ppermute x14, waiting for transfers between devices, shifted(): lax.ppermute(block, axis, [(i, (i + step) % size) for i in range(size)])  101 us
    dot_general x4, matrix products, matmul(): return jnp.dot(left, right, preferred_element_type=jnp.float32)  34.1 us
    pallas_call x2, Pallas kernels, scatter_sum(): pl.pallas_call(functools.partial(scatter_kernel, lanes, chain, levels, or...  34 us
    pallas_call x1, Pallas kernels, weight_grads(): pl.pallas_call(weight_grads_kernel, grid=(width // tile,), out_shape=jax....  20.4 us
    ppermute x14, starting transfers between devices, shifted(): lax.ppermute(block, axis, [(i, (i + step) % size) for i in range(size)])  18.9 us
  transfers between devices with their start and end apart: 14, of which 5 were waited for; matrix products, arithmetic and copies ran while one was open for 8% of the time, Pallas kernels for 42%

profile of v5, /device:TPU:0, one launch (start us, length us, event | category | flops | bytes accessed | tf_op | source)
XLA Modules:
  0.0 768.2 jit_solution(4831409555891859517)
XLA Ops:
  0.7 8.9 %shard_map.238 = (bf16[288,1728]{1,0:T(8,128)(2,1)}, bf16[288,1728]{1,0:T(8,128)(2,1)}, bf16[288,1728]{1,0:T(8,128)(2,1)}, bf16[288,1728]{1,0:T(8,128)(2,1)}) custom-call(bf16[288,2304]{1,0:T(8,128)(2,1)} %g_ref.1, bf16[288,2304]{1,0:T(8,128)(2,1)} %u_ref.1, bf16[288,2304]{1,0:T(8,128)(2,1)} %bitcast.146), custom_call_target="tpu_custom_call" | custom-call | bytes 7962624 | tf_op jit(solution)/shard_map/pallas_call | solution.py:98
  9.6 3.0 collective-permute-start
  12.6 2.1 collective-permute-start.1
  14.7 1.7 collective-permute-start.2
  16.9 2.0 convert_element_type.164
  19.9 120.0 %shard_map.237 = bf16[8,288,1536]{2,1,0:T(8,128)(2,1)} custom-call(bf16[288,1536]{1,0:T(8,128)(2,1)} %pad_maximum_fusion.1.refs_0_), custom_call_target="tpu_custom_call" | custom-call | bytes 70778880 | tf_op jit(solution)/shard_map/pallas_call | solution.py:324
  141.2 2.2 copy.105.h_ref
  147.7 4.5 fusion.5
  155.6 2.4 convolution_convert_fusion.2
  158.0 4.0 convolution_convert_fusion.1
  162.0 17.0 %shard_map.239 = f32[96,2304]{1,0:T(8,128)} custom-call(bf16[4,96,2304]{2,1,0:T(8,128)(2,1)} %bitcast.144), custom_call_target="tpu_custom_call" | custom-call | bytes 17694720 | tf_op jit(solution)/shard_map/pallas_call | solution.py:497
  185.7 38.5 %collective-permute-done.5.refs_6_ = bf16[288,1728]{1,0:T(8,128)(2,1)} collective-permute-done((bf16[288,1728]{1,0:T(8,128)(2,1)}, bf16[288,1728]{1,0:T(8,128)(2,1)}, u32[]{:S(2)}, u32[]{:S(2)}) %collective-permute-start.5) | collective-permute-done | bytes 995360 | tf_op jit(solution)/shard_map/ppermute | solution.py:72
  224.6 2.7 fusion.26
  229.6 47.0 %shard_map.240 = (bf16[16,96,2304]{2,1,0:T(8,128)(2,1)}, bf16[8,288,1728]{2,1,0:T(8,128)(2,1)}) custom-call(bf16[96,2304]{1,0:T(8,128)(2,1)} %multiply_convert_fusion.3.refs_0_, bf16[288,1728]{1,0:T(8,128)(2,1)} %collective-permute-done.2.refs_1_, bf16[288,1728]{1,0:T(8,128)(2,1)} %collective-permute-done.3.refs_2_, ...), custom_call_target="tpu_custom_call" | custom-call | bytes 70778880 | tf_op jit(solution)/shard_map/pallas_call | solution.py:324
  276.6 2.2 bitcast_dynamic-update-slice_fusion
  278.9 13.1 %fusion.2 = f32[1536,1152]{1,0:T(8,128)S(1)} fusion(bf16[1536,2304]{1,0:T(8,128)(2,1)} %bitcast.157, bf16[2304,1728]{1,0:T(8,128)(2,1)} %bitcast.153), kind=kOutput, calls=%fused_computation.6 | convolution fusion | flops 8153726976 | bytes 19464192 | tf_op jit(solution)/shard_map/dot_general | solution.py:59
  292.0 2.9 copy-done.3
  294.9 2.8 multiply_convert_fusion.1.left_ref.hidden_ref
  297.7 53.9 %shard_map.241 = f32[96,2304]{1,0:T(8,128)} custom-call(bf16[1536,576]{1,0:T(8,128)(2,1)} %multiply_convert_fusion.1.left_ref.hidden_ref, bf16[2304,1728]{1,0:T(8,128)(2,1)} %bitcast.154), custom_call_target="tpu_custom_call" | custom-call | flops 4076863488 | bytes 141557760 | tf_op jit(solution)/shard_map/pallas_call | solution.py:685
  353.1 2.5 multiply_reduce_fusion.3
  355.6 2.1 fusion.39.refs_0_
  357.7 47.1 %shard_map.242 = bf16[16,96,2304]{2,1,0:T(8,128)(2,1)} custom-call(bf16[96,2304]{1,0:T(8,128)(2,1)} %fusion.39.refs_0_), custom_call_target="tpu_custom_call" | custom-call | bytes 70778880 | tf_op jit(solution)/shard_map/pallas_call | solution.py:324
  404.8 13.2 %fusion.10 = (bf16[1536,576]{1,0:T(8,128)(2,1)S(1)}, bf16[1536,576]{1,0:T(8,128)(2,1)S(1)}) fusion(f32[1536,1152]{1,0:T(8,128)} %copy-done.3, bf16[1536,2304]{1,0:T(8,128)(2,1)} %bitcast.127, bf16[2304,1728]{1,0:T(8,128)(2,1)} %bitcast.155), kind=kOutput, calls=%fused_computation.16 | convolution fusion | flops 4101636096 | bytes 21430272 | tf_op jit(solution)/shard_map/dot_general | solution.py:59
  418.0 2.9 pad_maximum_fusion.left_ref.both_ref
  420.9 20.4 %shard_map.244 = bf16[2304,1728]{1,0:T(8,128)(2,1)} custom-call(bf16[1536,2304]{1,0:T(8,128)(2,1)} %bitcast.158, bf16[1536,2304]{1,0:T(8,128)(2,1)} %bitcast.128, bf16[1536,1152]{1,0:T(8,128)(2,1)} %pad_maximum_fusion.left_ref.both_ref, bf16[1536,576]{1,0:T(8,128)(2,1)} %multiply_convert_fusion.1.left_ref.hidden_ref), custom_call_target="tpu_custom_call" | custom-call | flops 12230590464 | bytes 22118400 | tf_op jit(solution)/shard_map/pallas_call | solution.py:728
  441.3 53.9 %shard_map.243 = f32[96,2304]{1,0:T(8,128)} custom-call(bf16[1536,1152]{1,0:T(8,128)(2,1)} %pad_maximum_fusion.left_ref.both_ref, bf16[2304,1728]{1,0:T(8,128)(2,1)} %bitcast.156), custom_call_target="tpu_custom_call" | custom-call | flops 8153726976 | bytes 141557760 | tf_op jit(solution)/shard_map/pallas_call | solution.py:685
  495.2 4.3 dynamic-slice_bitcast_fusion
  502.4 1.7 multiply_reduce_fusion.5
  508.6 16.9 %collective-permute-done.7 = bf16[288,1728]{1,0:T(8,128)(2,1)} collective-permute-done((bf16[288,1728]{1,0:T(8,128)(2,1)}, bf16[288,1728]{1,0:T(8,128)(2,1)}, u32[]{:S(2)}, u32[]{:S(2)}) %collective-permute-start.7) | collective-permute-done | bytes 995360 | tf_op jit(solution)/shard_map/ppermute | solution.py:72
  525.5 22.1 %collective-permute-done.8 = bf16[288,1728]{1,0:T(8,128)(2,1)} collective-permute-done((bf16[288,1728]{1,0:T(8,128)(2,1)}, bf16[288,1728]{1,0:T(8,128)(2,1)}, u32[]{:S(2)}, u32[]{:S(2)}) %collective-permute-start.8) | collective-permute-done | bytes 995360 | tf_op jit(solution)/shard_map/ppermute | solution.py:72
  547.6 22.1 %collective-permute-done.9 = bf16[288,1728]{1,0:T(8,128)(2,1)} collective-permute-done((bf16[288,1728]{1,0:T(8,128)(2,1)}, bf16[288,1728]{1,0:T(8,128)(2,1)}, u32[]{:S(2)}, u32[]{:S(2)}) %collective-permute-start.9) | collective-permute-done | bytes 995360 | tf_op jit(solution)/shard_map/ppermute | solution.py:72
  569.8 4.8 fusion.19
  574.6 14.1 %shard_map.245 = bf16[4,96,2304]{2,1,0:T(8,128)(2,1)} custom-call(bf16[96,2304]{1,0:T(8,128)(2,1)} %fusion.41.refs_0_), custom_call_target="tpu_custom_call" | custom-call | bytes 17694720 | tf_op jit(solution)/shard_map/pallas_call | solution.py:324
  588.7 3.4 fusion.31
  592.3 2.5 fusion.34
  595.6 2.0 fusion.36
  598.8 5.7 convolution_convert_fusion
  605.5 2.2 copy.90
  607.7 3.0 fusion.18.refs_0_
  611.9 1.8 collective-permute-start.12
  613.7 2.3 collective-permute-start.13
  616.0 17.0 %shard_map.246 = f32[96,2304]{1,0:T(8,128)} custom-call(bf16[4,96,2304]{2,1,0:T(8,128)(2,1)} %bitcast.143), custom_call_target="tpu_custom_call" | custom-call | bytes 17694720 | tf_op jit(solution)/shard_map/pallas_call | solution.py:497
  633.0 2.1 multiply_reduce_fusion.2
  638.5 2.1 pad_maximum_fusion.2.tail_ref
  641.4 110.1 %shard_map.247 = (f32[304,1536]{1,0:T(8,128)}, bf16[4,192,2304]{2,1,0:T(8,128)(2,1)}) custom-call(bf16[2304,384]{1,0:T(8,128)(2,1)} %copy.105.h_ref, bf16[2304,384]{1,0:T(8,128)(2,1)} %bitcast.142, bf16[384,1024]{1,0:T(8,128)(2,1)} %pad_maximum_fusion.3.qkv_ref, bf16[384,512]{1,0:T(8,128)(2,1)} %copy.120.mixed_ref, bf16[8,16,1536]{2,1,0:T(8,128)(2,1)} %pad.4.strip_ref, ...), custom_call_target="tpu_custom_call" | custom-call | flops 2717908992 | bytes 70778880 | tf_op jit(solution)/shard_map/pallas_call | solution.py:980
  751.5 3.6 fusion.95
  757.7 2.1 bitcast_convert_fusion
  759.9 8.1 %shard_map.248 = (f32[288,2304]{1,0:T(8,128)}, f32[288,2304]{1,0:T(8,128)}, f32[288,2304]{1,0:T(8,128)}) custom-call(bf16[288,1728]{1,0:T(8,128)(2,1)} %fusion.18.refs_0_, bf16[288,1728]{1,0:T(8,128)(2,1)} %collective-permute-done.11.refs_1_, bf16[288,1728]{1,0:T(8,128)(2,1)} %collective-permute-done.12.refs_2_, ...), custom_call_target="tpu_custom_call" | custom-call | tf_op jit(solution)/shard_map/pallas_call | solution.py:767
  (166 shorter events, 39.6 us)
Async XLA Ops:
  0.6 15.8 %copy-start.1 = (bf16[384,2304]{1,0:T(8,128)(2,1)S(1)}, bf16[384,2304]{1,0:T(8,128)(2,1)}, u32[]{:S(2)}) copy-start(bf16[384,2304]{1,0:T(8,128)(2,1)} %param.14) | copy-start | bytes 5308420
  9.6 138.1 %collective-permute-start = (bf16[288,1728]{1,0:T(8,128)(2,1)}, bf16[288,1728]{1,0:T(8,128)(2,1)}, u32[]{:S(2)}, u32[]{:S(2)}) collective-permute-start(bf16[288,1728]{1,0:T(8,128)(2,1)} %get-tuple-element.38), channel_id=1, source_target_pairs={{0,8},{8,16},{16,24},{24,0},{1,9},{9,17},{17,25},{25,1},{2,10},{10... | collective-permute-start | bytes 2985992 | tf_op jit(solution)/shard_map/ppermute | solution.py:72
  12.6 135.0 %collective-permute-start.1 = (bf16[288,1728]{1,0:T(8,128)(2,1)}, bf16[288,1728]{1,0:T(8,128)(2,1)}, u32[]{:S(2)}, u32[]{:S(2)}) collective-permute-start(bf16[288,1728]{1,0:T(8,128)(2,1)} %get-tuple-element.39), channel_id=1, source_target_pairs={{0,24},{8,0},{16,8},{24,16},{1,25},{9,1},{17,9},{25,17},{2,26},{10... | collective-permute-start | bytes 2985992 | tf_op jit(solution)/shard_map/ppermute | solution.py:72
  14.7 213.6 %collective-permute-start.2 = (bf16[288,1728]{1,0:T(8,128)(2,1)}, bf16[288,1728]{1,0:T(8,128)(2,1)}, u32[]{:S(2)}, u32[]{:S(2)}) collective-permute-start(bf16[288,1728]{1,0:T(8,128)(2,1)} %get-tuple-element.44.refs_4_), channel_id=1, source_target_pairs={{0,4},{4,0},{1,5},{5,1},{2,6},{6,2},{3,7},{7,3},{8,12},{12,8},{9,1... | collective-permute-start | bytes 2985992 | tf_op jit(solution)/shard_map/ppermute | solution.py:72
  16.8 2.1 copy-start.23
  16.8 2.1 copy-start.24
  19.9 120.0 %copy-start.42 = (s32[1,8]{1,0:T(1,128)S(1)}, s32[1,8]{1,0:T(1,128)}, u32[]{:S(2)}) copy-start(s32[1,8]{1,0:T(1,128)} %param.16) | copy-start | bytes 100
  19.9 120.8 %copy-start.30 = (f32[2304]{0:T(1024)S(1)}, f32[2304]{0:T(1024)}, u32[]{:S(2)}) copy-start(f32[2304]{0:T(1024)} %param.17) | copy-start | bytes 27652
  147.6 4.6 copy-start.18
  147.6 4.6 copy-start.20
  155.6 69.0 %copy-start.9 = (f32[2,384,384]{1,2,0:T(8,128)}, f32[2,384,384]{1,2,0:T(8,128)S(1)}, u32[]{:S(2)}) copy-start(f32[2,384,384]{1,2,0:T(8,128)S(1)} %fusion.22) | copy-start | bytes 3538948
  162.0 21.5 %copy-start.28 = (f32[2304]{0:T(1024)S(1)}, f32[2304]{0:T(1024)}, u32[]{:S(2)}) copy-start(f32[2304]{0:T(1024)} %param.22) | copy-start | bytes 27652
  179.0 4.5 copy-start
  179.0 45.1 %collective-permute-start.5 = (bf16[288,1728]{1,0:T(8,128)(2,1)}, bf16[288,1728]{1,0:T(8,128)(2,1)}, u32[]{:S(2)}, u32[]{:S(2)}) collective-permute-start(bf16[288,1728]{1,0:T(8,128)(2,1)} %get-tuple-element.45), channel_id=1, source_target_pairs={{0,16},{8,24},{16,0},{24,8},{1,17},{9,25},{17,1},{25,9},{2,18},{10... | collective-permute-start | bytes 2985992 | tf_op jit(solution)/shard_map/ppermute | solution.py:72
  180.5 3.0 copy-start.38
  181.5 46.8 %collective-permute-start.3 = (bf16[288,1728]{1,0:T(8,128)(2,1)}, bf16[288,1728]{1,0:T(8,128)(2,1)}, u32[]{:S(2)}, u32[]{:S(2)}) collective-permute-start(bf16[288,1728]{1,0:T(8,128)(2,1)} %collective-permute-done.refs_5_), channel_id=1, source_target_pairs={{0,4},{4,0},{1,5},{5,1},{2,6},{6,2},{3,7},{7,3},{8,12},{12,8},{9,1... | collective-permute-start | bytes 2985992 | tf_op jit(solution)/shard_map/ppermute | solution.py:72
  182.0 47.6 %collective-permute-start.4 = (bf16[288,1728]{1,0:T(8,128)(2,1)}, bf16[288,1728]{1,0:T(8,128)(2,1)}, u32[]{:S(2)}, u32[]{:S(2)}) collective-permute-start(bf16[288,1728]{1,0:T(8,128)(2,1)} %collective-permute-done.1.refs_7_), channel_id=1, source_target_pairs={{0,4},{4,0},{1,5},{5,1},{2,6},{6,2},{3,7},{7,3},{8,12},{12,8},{9,1... | collective-permute-start | bytes 2985992 | tf_op jit(solution)/shard_map/ppermute | solution.py:72
  183.5 43.8 %copy-start.33 = (f32[96]{0:T(128)}, f32[96]{0:T(128)S(1)}, u32[]{:S(2)}) copy-start(f32[96]{0:T(128)S(1)} %fusion.80) | copy-start | bytes 1156
  185.0 43.2 %copy-start.37 = (f32[96]{0:T(128)}, f32[96]{0:T(128)S(1)}, u32[]{:S(2)}) copy-start(f32[96]{0:T(128)S(1)} %get-tuple-element.89) | copy-start | bytes 1156
  185.1 43.2 %copy-start.40 = (f32[96]{0:T(128)}, f32[96]{0:T(128)S(1)}, u32[]{:S(2)}) copy-start(f32[96]{0:T(128)S(1)} %get-tuple-element.76) | copy-start | bytes 1156
  185.1 42.3 %copy-start.27 = (f32[2304]{0:T(1024)S(1)}, f32[2304]{0:T(1024)}, u32[]{:S(2)}) copy-start(f32[2304]{0:T(1024)} %param.23) | copy-start | bytes 27652
  224.1 52.5 %collective-permute-start.6 = (bf16[288,1728]{1,0:T(8,128)(2,1)}, bf16[288,1728]{1,0:T(8,128)(2,1)}, u32[]{:S(2)}, u32[]{:S(2)}) collective-permute-start(bf16[288,1728]{1,0:T(8,128)(2,1)} %collective-permute-done.5.refs_6_), channel_id=1, source_target_pairs={{0,4},{4,0},{1,5},{5,1},{2,6},{6,2},{3,7},{7,3},{8,12},{12,8},{9,1... | collective-permute-start | bytes 2985992 | tf_op jit(solution)/shard_map/ppermute | solution.py:72
  292.0 2.9 copy-start.3
  297.7 55.3 %copy-start.32 = (f32[2304]{0:T(1024)S(1)}, f32[2304]{0:T(1024)}, u32[]{:S(2)}) copy-start(f32[2304]{0:T(1024)} %param.27) | copy-start | bytes 27652
  297.7 55.4 %copy-start.35 = (f32[96]{0:T(128)S(1)}, f32[96]{0:T(128)}, u32[]{:S(2)}) copy-start(f32[96]{0:T(128)} %dynamic-slice.3) | copy-start | bytes 1156
  351.6 4.0 copy-start.7
  495.2 6.9 copy-start.11
  495.2 7.1 copy-start.41
  495.2 7.1 copy-start.29
  495.2 7.1 copy-start.34
  499.5 26.0 %collective-permute-start.7 = (bf16[288,1728]{1,0:T(8,128)(2,1)}, bf16[288,1728]{1,0:T(8,128)(2,1)}, u32[]{:S(2)}, u32[]{:S(2)}) collective-permute-start(bf16[288,1728]{1,0:T(8,128)(2,1)} %get-tuple-element.85), channel_id=1, source_target_pairs={{0,4},{4,0},{1,5},{5,1},{2,6},{6,2},{3,7},{7,3},{8,12},{12,8},{9,1... | collective-permute-start | bytes 2985992 | tf_op jit(solution)/shard_map/ppermute | solution.py:72
  500.1 47.6 %collective-permute-start.8 = (bf16[288,1728]{1,0:T(8,128)(2,1)}, bf16[288,1728]{1,0:T(8,128)(2,1)}, u32[]{:S(2)}, u32[]{:S(2)}) collective-permute-start(bf16[288,1728]{1,0:T(8,128)(2,1)} %get-tuple-element.84), channel_id=1, source_target_pairs={{0,4},{4,0},{1,5},{5,1},{2,6},{6,2},{3,7},{7,3},{8,12},{12,8},{9,1... | collective-permute-start | bytes 2985992 | tf_op jit(solution)/shard_map/ppermute | solution.py:72
  501.5 68.2 %collective-permute-start.9 = (bf16[288,1728]{1,0:T(8,128)(2,1)}, bf16[288,1728]{1,0:T(8,128)(2,1)}, u32[]{:S(2)}, u32[]{:S(2)}) collective-permute-start(bf16[288,1728]{1,0:T(8,128)(2,1)} %get-tuple-element.83), channel_id=1, source_target_pairs={{0,4},{4,0},{1,5},{5,1},{2,6},{6,2},{3,7},{7,3},{8,12},{12,8},{9,1... | collective-permute-start | bytes 2985992 | tf_op jit(solution)/shard_map/ppermute | solution.py:72
  502.4 5.3 copy-start.39
  504.0 70.5 %copy-start.4 = (f32[96,2304]{1,0:T(8,128)}, f32[96,2304]{1,0:T(8,128)S(1)}, u32[]{:S(2)}) copy-start(f32[96,2304]{1,0:T(8,128)S(1)} %get-tuple-element.75) | copy-start | bytes 2654212
  504.0 90.7 %collective-permute-start.10 = (bf16[288,1728]{1,0:T(8,128)(2,1)}, bf16[288,1728]{1,0:T(8,128)(2,1)}, u32[]{:S(2)}, u32[]{:S(2)}) collective-permute-start(bf16[288,1728]{1,0:T(8,128)(2,1)} %get-tuple-element.50), channel_id=1, source_target_pairs={{0,4},{4,0},{1,5},{5,1},{2,6},{6,2},{3,7},{7,3},{8,12},{12,8},{9,1... | collective-permute-start | bytes 2985992 | tf_op jit(solution)/shard_map/ppermute | solution.py:72
  588.7 3.6 copy-start.10
  592.3 2.5 copy-start.17
  598.7 6.7 copy-start.8
  607.7 25.3 %copy-start.2 = (f32[384,2304]{1,0:T(8,128)S(1)}, f32[384,2304]{1,0:T(8,128)}, u32[]{:S(2)}) copy-start(f32[384,2304]{1,0:T(8,128)} %convert_element_type.164) | copy-start | bytes 10616836
  610.6 22.4 %copy-start.31 = (f32[2304]{0:T(1024)S(1)}, f32[2304]{0:T(1024)}, u32[]{:S(2)}) copy-start(f32[2304]{0:T(1024)} %param.17) | copy-start | bytes 27652
  610.6 22.4 %copy-start.36 = (f32[96]{0:T(128)S(1)}, f32[96]{0:T(128)}, u32[]{:S(2)}) copy-start(f32[96]{0:T(128)} %fusion.83) | copy-start | bytes 1156
  610.6 149.2 %collective-permute-start.11 = (bf16[288,1728]{1,0:T(8,128)(2,1)}, bf16[288,1728]{1,0:T(8,128)(2,1)}, u32[]{:S(2)}, u32[]{:S(2)}) collective-permute-start(bf16[288,1728]{1,0:T(8,128)(2,1)} %get-tuple-element.55), channel_id=1, source_target_pairs={{0,8},{8,16},{16,24},{24,0},{1,9},{9,17},{17,25},{25,1},{2,10},{10... | collective-permute-start | bytes 2985992 | tf_op jit(solution)/shard_map/ppermute | solution.py:72
  611.9 147.9 %collective-permute-start.12 = (bf16[288,1728]{1,0:T(8,128)(2,1)}, bf16[288,1728]{1,0:T(8,128)(2,1)}, u32[]{:S(2)}, u32[]{:S(2)}) collective-permute-start(bf16[288,1728]{1,0:T(8,128)(2,1)} %get-tuple-element.56), channel_id=1, source_target_pairs={{0,16},{8,24},{16,0},{24,8},{1,17},{9,25},{17,1},{25,9},{2,18},{10... | collective-permute-start | bytes 2985992 | tf_op jit(solution)/shard_map/ppermute | solution.py:72
  613.7 146.1 %collective-permute-start.13 = (bf16[288,1728]{1,0:T(8,128)(2,1)}, bf16[288,1728]{1,0:T(8,128)(2,1)}, u32[]{:S(2)}, u32[]{:S(2)}) collective-permute-start(bf16[288,1728]{1,0:T(8,128)(2,1)} %get-tuple-element.57), channel_id=1, source_target_pairs={{0,24},{8,0},{16,8},{24,16},{1,25},{9,1},{17,9},{25,17},{2,26},{10... | collective-permute-start | bytes 2985992 | tf_op jit(solution)/shard_map/ppermute | solution.py:72
  633.0 2.8 copy-start.5
  633.0 2.7 copy-start.6
  751.5 3.6 copy-start.22
  (11 other events, 15.3 us)
